TPU v7x, 32 devices: a whole 2x2x4 slice. The times are simulated.
32 devices in a mesh: lat: 8 (over z, x), fld: 4 (over y, core).
Axes of the slice: x: 2, y: 2, z: 4, core: 2. Of those that a mesh axis runs over, the one named last changes fastest.
Arguments:
- grid_in: bfloat16 [32, 2560, 2688], P('fld', 'lat'), may hold values from -6 to 6
- legendre: bfloat16 [768, 1280, 768], P(('lat', 'fld')), may hold values from -0.15625 to 0.15625
- wave_slot: int32 [768], replicated, may hold values from 512 to 1279, as said below
- lat_modes: int32 [2560], P('lat'), may hold values from 10 to 1280
- gauss_weight: float32 [1280], replicated, may hold values from 0.5 to 2
- diffusion: float32 [32], replicated, may hold values from 0.5 to 8
Outputs:
- grid_out: float32 [32, 2560, 2688], P('fld', 'lat')
- spectra: float32 [2, 768, 32, 768], P(None, 'lat', 'fld')
Inputs may be any that keep to these rules, and one draw needn't show every extreme that they name: `wave_slot`: every wavenumber from 512 to 1279 stands in exactly one slot; slots 2 t and 2 t + 1 hold two wavenumbers that sum to 1791, the smaller one in the even slot.
All inputs are finite; a program needn't handle non-finite values.
Results may differ from a plain program's by a relative error of at most 0.0071.
Values may be sent and summed in bfloat16 or wider, within the bound.
No kernel may reach another device: no remote copies, remote signals or barrier semaphores. Data moves between devices by JAX's collectives and lax.ppermute only.
A program may use at most 256 MiB of HBM per device.

v0:
```python
import math

import jax
import jax.numpy as jnp
from jax import lax
from jax.sharding import PartitionSpec as P

LMAX = 1279


def angle_table(waves, lon_count):
    points = jnp.arange(lon_count, dtype=jnp.int32)
    phase_index = points[:, None] * waves[None, :] % lon_count
    radians = phase_index.astype(jnp.float32) * (2.0 * math.pi / lon_count)
    norm_scale = 1.0 / math.sqrt(lon_count)
    return jnp.stack([jnp.cos(radians) * norm_scale, -jnp.sin(radians) * norm_scale], 1).astype(
        jnp.bfloat16
    )


def damping(waves, damp_rates, columns):
    half_cols = columns // 2
    col_index = jnp.arange(columns, dtype=jnp.int32)
    offset = jnp.where(col_index < half_cols, 2 * col_index, 2 * col_index - columns + 1)
    degree = waves[:, None] + offset[None, :]
    degree_ratio = (degree * (degree + 1)).astype(jnp.float32) / float(LMAX * (LMAX + 1))
    factor = 1.0 / (1.0 + damp_rates[None, :, None] * (degree_ratio**4)[:, None, :])
    return jnp.where((degree <= LMAX)[:, None, :], factor, 0.0)


def project(even_part, odd_part, tables, used_cols):
    half_cols = tables.shape[2] // 2
    even_cols = jnp.einsum(
        "rsfj,sjq->rsfq", even_part, tables[:, :, :used_cols], preferred_element_type=jnp.float32
    )
    odd_cols = jnp.einsum(
        "rsfj,sjq->rsfq",
        odd_part,
        tables[:, :, half_cols : half_cols + used_cols],
        preferred_element_type=jnp.float32,
    )
    return jnp.concatenate([even_cols, odd_cols], -1)


def expand(rounded, tables, used_cols):
    half_cols = tables.shape[2] // 2
    sym_part = jnp.einsum(
        "rsfq,sjq->rsfj",
        rounded[..., :used_cols],
        tables[:, :, :used_cols],
        preferred_element_type=jnp.float32,
    )
    anti_part = jnp.einsum(
        "rsfq,sjq->rsfj",
        rounded[..., half_cols : half_cols + used_cols],
        tables[:, :, half_cols : half_cols + used_cols],
        preferred_element_type=jnp.float32,
    )
    return (sym_part, anti_part)


def transform_block(block_data, tables, block_waves, damp_rates, weights):
    half_lats = weights.shape[0]
    columns = tables.shape[2]
    half_cols = columns // 2
    north_half = block_data[..., :half_lats].astype(jnp.float32)
    south_half = jnp.flip(block_data[..., half_lats:], -1).astype(jnp.float32)
    even_part = ((north_half + south_half) * weights).astype(jnp.bfloat16)
    odd_part = ((north_half - south_half) * weights).astype(jnp.bfloat16)
    raw_coeff = project(even_part, odd_part, tables, half_cols)
    spectra = raw_coeff * damping(block_waves, damp_rates, columns)[None]
    rounded = spectra.astype(jnp.bfloat16)
    sym_part, anti_part = expand(rounded, tables, half_cols)
    synthesized = jnp.concatenate(
        [
            (sym_part + anti_part).astype(jnp.bfloat16),
            jnp.flip((sym_part - anti_part).astype(jnp.bfloat16), -1),
        ],
        -1,
    )
    return (spectra, synthesized)


def body(grid_in, legendre, wave_slot, lat_modes, gauss_weight, diffusion):
    fld_dev, lat_dev, lon_count = grid_in.shape
    slots_all = wave_slot.shape[0]
    lat_count = lax.axis_size("lat")
    fld_count = lax.axis_size("fld")
    lat_total = lat_dev * lat_count
    lat_index = lax.axis_index("lat")
    fld_index = lax.axis_index("fld")
    owned_slots = slots_all // (lat_count * fld_count)
    angles = angle_table(wave_slot, lon_count)
    keep_mask = (wave_slot[:, None] < lat_modes[None, :]).astype(jnp.float32)
    fourier = jnp.einsum("fjx,xrs->rsfj", grid_in, angles, preferred_element_type=jnp.float32)
    fourier = (fourier * keep_mask[None, :, None, :]).astype(jnp.bfloat16)
    own_waves = lax.dynamic_slice_in_dim(
        wave_slot, (lat_index * fld_count + fld_index) * owned_slots, owned_slots
    )
    flattened = fourier.reshape(2, slots_all, fld_dev * lat_dev)
    arrived = lax.all_to_all(flattened, ("lat", "fld"), split_axis=1, concat_axis=2, tiled=True)
    arrived = arrived.reshape(2, owned_slots, lat_count, fld_count, fld_dev, lat_dev)
    arrived = arrived.transpose(0, 1, 3, 4, 2, 5).reshape(
        2, owned_slots, fld_count * fld_dev, lat_total
    )
    owned_spectra, synthesized = transform_block(
        arrived, legendre, own_waves, diffusion, gauss_weight
    )
    spectra = lax.all_to_all(owned_spectra, "fld", split_axis=2, concat_axis=1, tiled=True)
    outgoing = synthesized.reshape(2, owned_slots, fld_count, fld_dev, lat_count, lat_dev)
    outgoing = outgoing.transpose(0, 1, 4, 2, 3, 5).reshape(
        2, owned_slots, lat_count * fld_count * fld_dev * lat_dev
    )
    returned = lax.all_to_all(outgoing, ("lat", "fld"), split_axis=2, concat_axis=1, tiled=True)
    returned = returned.reshape(2, slots_all, fld_dev, lat_dev)
    keep_narrow = keep_mask.astype(jnp.bfloat16)
    masked = returned * keep_narrow[None, :, None, :]
    grid_out = 2.0 * jnp.einsum("rsfj,xrs->fjx", masked, angles, preferred_element_type=jnp.float32)
    return (grid_out, spectra)


def solution(mesh):
    return jax.shard_map(
        body,
        mesh=mesh,
        in_specs=(P("fld", "lat", None), P(("lat", "fld"), None, None), P(), P("lat"), P(), P()),
        out_specs=(P("fld", "lat", None), P(None, "lat", "fld", None)),
        check_vma=False,
    )
```

profile of v0, /device:TPU:0, one launch (start us, length us, event | category | flops | bytes accessed | tf_op | source)
XLA Modules:
  0.0 971.9 jit_solution(12903384321275635011)
XLA Ops:
  0.6 0.0 copy-start.5
  0.6 0.0 copy-start.7
  0.6 36.7 %multiply_convert_fusion.2 = (bf16[2688,1,768]{2,0,1:T(8,128)(2,1)S(1)}, bf16[2688,1,768]{2,0,1:T(8,128)(2,1)S(1)}) fusion(s32[768]{0:T(1024)} %param.8), kind=kLoop, calls=%fused_computation.26 | loop fusion | flops 28901376 | bytes 8260608 | tf_op jit(solution)/shard_map/convert
  37.3 0.0 copy-done.5
  37.3 0.0 copy-done.7
  37.3 0.0 copy-start
  37.4 0.0 copy-start.2
  37.4 1.1 fusion.46
  38.5 28.8 %multiply_convert_fusion = bf16[2,768,8,320]{1,3,2,0:T(8,128)(2,1)} fusion(f32[768,320]{0,1:T(8,128)S(1)} %get-tuple-element.9, bf16[8,320,2688]{2,1,0:T(8,128)(2,1)} %param.6, bf16[2688,1,768]{2,0,1:T(8,128)(2,1)S(1)} %get-tuple-element.11, bf16[2688,1,768]{2,0,1:T(8,128)(2,1)S(1)} %get-tuple-element.10), kind=kOutput, calls=%fused_computation.13 | convolution fusion | flops 21163671552 | bytes 30867456 | tf_op jit(solution)/shard_map/fjx,xrs->rsfj/dot_general | solution.py:95
  67.3 0.0 copy-done
  67.3 0.0 copy-done.2
  67.3 20.2 %copy.26 = bf16[2,768,2560]{2,0,1:T(2,128)(2,1)} copy(bf16[2,768,2560]{1,2,0:T(8,128)(2,1)} %bitcast.80) | data formatting | bytes 15728640 | tf_op jit(solution)/shard_map/reshape | solution.py:100
  87.5 0.0 copy-start.8
  87.5 7.4 all-to-all-start
  94.9 0.1 dynamic_slice.3
  95.0 0.1 add_compare_fusion
  95.1 0.1 fusion.50
  95.2 0.0 copy-done.8
  95.2 1.9 divide_select_fusion
  97.1 171.7 %all-to-all-done = bf16[2,768,2560]{2,0,1:T(2,128)(2,1)} async-done(((bf16[2,768,2560]{2,0,1:T(2,128)(2,1)}), bf16[2,768,2560]{2,0,1:T(2,128)(2,1)}, u32[]{:S(2)}, u32[]{:S(2)}) %all-to-all-start) | async-done | bytes 7864352 | tf_op jit(solution)/shard_map/all_to_all | solution.py:101
  268.7 7.6 copy.27
  276.3 15.3 %reshape.233 = bf16[2,24,8,4,8,320]{5,4,1,3,2,0:T(8,128)(2,1)} reshape(bf16[2,24,32,2560]{3,1,2,0:T(8,128)(2,1)} %bitcast.78) | data formatting | bytes 15728640 | tf_op jit(solution)/shard_map/reshape | solution.py:102
  291.6 17.8 %copy.29 = bf16[2,24,4,8,8,320]{5,4,3,2,1,0:T(8,128)(2,1)} copy(bf16[2,24,4,8,8,320]{5,3,1,2,4,0:T(8,128)(2,1)} %bitcast.76) | data formatting | bytes 15728640 | tf_op jit(solution)/shard_map/transpose | solution.py:103
  309.5 14.9 %reshape.224 = bf16[2,24,32,2560]{3,2,1,0:T(8,128)(2,1)} reshape(bf16[2,24,4,8,8,320]{5,4,3,2,1,0:T(8,128)(2,1)} %copy.29) | data formatting | bytes 15728640 | tf_op jit(solution)/shard_map/reshape | solution.py:103
  324.3 0.0 copy-start.6
  324.3 4.3 slice.27
  328.6 13.3 %rev.7 = bf16[2,24,32,1280]{3,2,1,0:T(8,128)(2,1)} reverse(bf16[2,24,32,1280]{3,2,1,0:T(8,128)(2,1)} %slice.27), dimensions={3} | reverse | bytes 7864320 | tf_op jit(solution)/shard_map/jit(_flip)/rev | solution.py:67
  341.9 0.0 copy-done.6
  341.9 6.9 fusion.23
  348.8 14.0 %fusion.34 = f32[2,24,32,384]{3,2,0,1:T(8,128)} fusion(bf16[24,1280,768]{2,1,0:T(8,128)(2,1)} %param.7, bf16[2,24,32,1280]{3,2,1,0:T(8,128)(2,1)} %get-tuple-element.7), kind=kOutput, calls=%fused_computation.45 | convolution fusion | flops 1509949440 | bytes 29884416 | tf_op jit(solution)/shard_map/rsfj,sjq->rsfq/dot_general | solution.py:36
  362.8 14.0 %fusion.39 = f32[2,24,32,384]{3,2,0,1:T(8,128)} fusion(bf16[24,1280,768]{2,1,0:T(8,128)(2,1)} %param.7, bf16[2,24,32,1280]{3,2,1,0:T(8,128)(2,1)} %get-tuple-element.6), kind=kOutput, calls=%fused_computation.46 | convolution fusion | flops 1509949440 | bytes 29884416 | tf_op jit(solution)/shard_map/rsfj,sjq->rsfq/dot_general | solution.py:33
  376.9 3.9 fusion.53
  380.8 5.8 copy.37
  386.6 5.1 all-to-all-start.2
  391.7 14.0 %fusion = f32[24,2,32,1280]{3,2,1,0:T(8,128)} fusion(bf16[24,1280,768]{2,1,0:T(8,128)(2,1)} %param.7, bf16[2,24,32,768]{3,2,0,1:T(8,128)(2,1)S(1)} %get-tuple-element.2), kind=kOutput, calls=%fused_computation.1 | convolution fusion | flops 1509949440 | bytes 32636928 | tf_op jit(solution)/shard_map/rsfq,sjq->rsfj/dot_general | solution.py:47
  405.7 16.7 %fusion.30 = (bf16[2,24,32,1280]{3,2,0,1:T(8,128)(2,1)}, bf16[2,24,32,1280]{3,2,0,1:T(8,128)(2,1)}) fusion(f32[24,2,32,1280]{3,2,1,0:T(8,128)} %fusion, bf16[24,1280,768]{2,1,0:T(8,128)(2,1)} %param.7, bf16[2,24,32,768]{3,2,0,1:T(8,128)(2,1)S(1)} %get-tuple-element.2), kind=kOutput, calls=%fused_computation.40 | convolution fusion | flops 1517813760 | bytes 40501248 | tf_op jit(solution)/shard_map/rsfq,sjq->rsfj/dot_general | solution.py:53
  422.4 12.9 %rev.8 = bf16[2,24,32,1280]{3,2,0,1:T(8,128)(2,1)} reverse(bf16[2,24,32,1280]{3,2,0,1:T(8,128)(2,1)} %get-tuple-element.5), dimensions={3} | reverse | bytes 7864320 | tf_op jit(solution)/shard_map/jit(_flip)/rev | solution.py:77
  435.3 7.2 pad_maximum_fusion.1
  442.5 15.2 %reshape.225 = bf16[2,24,4,8,8,320]{5,4,3,2,0,1:T(8,128)(2,1)} reshape(bf16[2,24,32,2560]{3,2,0,1:T(8,128)(2,1)} %pad_maximum_fusion.1) | data formatting | bytes 15728640 | tf_op jit(solution)/shard_map/reshape | solution.py:110
  457.7 74.0 %copy.45 = bf16[2,24,8,4,8,320]{1,0,5,4,3,2:T(2,128)(2,1)} copy(bf16[2,24,8,4,8,320]{5,2,4,3,0,1:T(8,128)(2,1)} %bitcast.77) | data formatting | bytes 15728640 | tf_op jit(solution)/shard_map/reshape | solution.py:111
  531.7 55.9 %reshape.234 = bf16[32,2,61440]{2,1,0:T(2,128)(2,1)} reshape(bf16[81920,2,24]{2,1,0:T(2,128)(2,1)} %bitcast.74) | data formatting | bytes 15728640
  587.6 0.0 copy-start.4
  587.6 0.0 all-to-all-done.2
  587.6 7.3 all-to-all-start.1
  594.9 0.0 copy-done.4
  594.9 1.1 copy.35
  596.0 7.3 copy.38
  603.2 165.5 %all-to-all-done.1 = bf16[32,2,61440]{2,1,0:T(2,128)(2,1)} async-done(((bf16[32,2,61440]{2,1,0:T(2,128)(2,1)}), bf16[32,2,61440]{2,1,0:T(2,128)(2,1)}, u32[]{:S(2)}, u32[]{:S(2)}) %all-to-all-start.1) | async-done | bytes 7864352 | tf_op jit(solution)/shard_map/all_to_all | solution.py:114
  768.7 60.4 %reshape.235 = bf16[81920,2,24]{2,1,0:T(2,128)(2,1)} reshape(bf16[32,2,61440]{2,1,0:T(2,128)(2,1)} %all-to-all-done.1) | data formatting | bytes 15728640
  829.1 78.1 %copy.34 = bf16[2,24,32,2560]{3,1,2,0:T(8,128)(2,1)} copy(bf16[2,24,32,2560]{1,0,3,2:T(2,128)(2,1)} %bitcast.75) | data formatting | bytes 15728640 | tf_op jit(solution)/shard_map/all_to_all | solution.py:114
  907.2 15.2 %reshape.227 = bf16[2,768,8,320]{3,2,1,0:T(8,128)(2,1)} reshape(bf16[2,32,24,2560]{3,2,1,0:T(8,128)(2,1)} %bitcast.79) | data formatting | bytes 15728640 | tf_op jit(solution)/shard_map/reshape | solution.py:115
  922.3 0.0 copy-start.1
  922.3 0.0 copy-start.3
  922.4 11.4 %broadcast_multiply_fusion = bf16[2,768,8,320]{3,2,1,0:T(8,128)(2,1)} fusion(bf16[2,768,8,320]{3,2,1,0:T(8,128)(2,1)} %reshape.227, bf16[768,320]{1,0:T(8,128)(2,1)} %copy.35), kind=kLoop, calls=%fused_computation.39 | loop fusion | flops 3932160 | bytes 16220160 | tf_op jit(solution)/shard_map/mul | solution.py:117
  933.8 0.0 copy-done.1
  933.8 0.0 copy-done.3
  933.8 37.9 %bitcast_multiply_fusion = f32[8,320,2688]{2,1,0:T(8,128)} fusion(bf16[2,768,8,320]{3,2,1,0:T(8,128)(2,1)} %broadcast_multiply_fusion, bf16[2688,1,768]{2,0,1:T(8,128)(2,1)S(1)} %copy-done.3, bf16[2688,1,768]{2,0,1:T(8,128)(2,1)S(1)} %copy-done.1), kind=kOutput, calls=%fused_computation | convolution fusion | flops 21150302208 | bytes 43646976 | tf_op jit(solution)/shard_map/rsfj,xrs->fjx/dot_general | solution.py:118
  (1 shorter events, 0.0 us)
Async XLA Ops:
  0.6 36.7 %copy-start.5 = (s32[768]{0:T(1024)S(1)}, s32[768]{0:T(1024)}, u32[]{:S(2)}) copy-start(s32[768]{0:T(1024)} %param.8) | copy-start | bytes 9220
  0.6 36.7 %copy-start.7 = (s32[320]{0:T(512)S(1)}, s32[320]{0:T(512)}, u32[]{:S(2)}) copy-start(s32[320]{0:T(512)} %param.9) | copy-start | bytes 3844
  37.3 30.0 %copy-start = (bf16[2688,1,768]{2,0,1:T(8,128)(2,1)}, bf16[2688,1,768]{2,0,1:T(8,128)(2,1)S(1)}, u32[]{:S(2)}) copy-start(bf16[2688,1,768]{2,0,1:T(8,128)(2,1)S(1)} %get-tuple-element.10) | copy-start | bytes 12386308
  37.4 30.0 %copy-start.2 = (bf16[2688,1,768]{2,0,1:T(8,128)(2,1)}, bf16[2688,1,768]{2,0,1:T(8,128)(2,1)S(1)}, u32[]{:S(2)}) copy-start(bf16[2688,1,768]{2,0,1:T(8,128)(2,1)S(1)} %get-tuple-element.11) | copy-start | bytes 12386308
  87.5 7.7 copy-start.8
  87.5 181.2 %all-to-all-start = ((bf16[2,768,2560]{2,0,1:T(2,128)(2,1)}), bf16[2,768,2560]{2,0,1:T(2,128)(2,1)}, u32[]{:S(2)}, u32[]{:S(2)}) async-start(bf16[2,768,2560]{2,0,1:T(2,128)(2,1)} %copy.26), calls=%async_computation | async-start | bytes 15728640 | tf_op jit(solution)/shard_map/all_to_all | solution.py:101
  324.3 17.6 %copy-start.6 = (f32[1280]{0:T(1024)S(1)}, f32[1280]{0:T(1024)}, u32[]{:S(2)}) copy-start(f32[1280]{0:T(1024)} %param.10) | copy-start | bytes 15364
  386.6 201.0 %all-to-all-start.2 = ((f32[2,24,32,768]{3,0,1,2:T(2,128)}), f32[2,24,32,768]{3,0,1,2:T(2,128)}, u32[]{:S(2)}, u32[]{:S(2)}) async-start(f32[2,24,32,768]{3,0,1,2:T(2,128)} %copy.37), calls=%async_computation.2 | async-start | bytes 9437184 | tf_op jit(solution)/shard_map/all_to_all | solution.py:109
  587.6 7.3 copy-start.4
  587.6 181.1 %all-to-all-start.1 = ((bf16[32,2,61440]{2,1,0:T(2,128)(2,1)}), bf16[32,2,61440]{2,1,0:T(2,128)(2,1)}, u32[]{:S(2)}, u32[]{:S(2)}) async-start(bf16[32,2,61440]{2,1,0:T(2,128)(2,1)} %reshape.234), calls=%async_computation.1 | async-start | bytes 15728640 | tf_op jit(solution)/shard_map/all_to_all | solution.py:114
  922.3 11.4 %copy-start.1 = (bf16[2688,1,768]{2,0,1:T(8,128)(2,1)S(1)}, bf16[2688,1,768]{2,0,1:T(8,128)(2,1)}, u32[]{:S(2)}) copy-start(bf16[2688,1,768]{2,0,1:T(8,128)(2,1)} %copy-done) | copy-start | bytes 12386308
  922.3 11.4 %copy-start.3 = (bf16[2688,1,768]{2,0,1:T(8,128)(2,1)S(1)}, bf16[2688,1,768]{2,0,1:T(8,128)(2,1)}, u32[]{:S(2)}) copy-start(bf16[2688,1,768]{2,0,1:T(8,128)(2,1)} %copy-done.2) | copy-start | bytes 12386308
where the time goes:
time: 989 us; the launch traced here: 972 us
  local copies, waits for them, and re-layouts  419 us (42%)
  waiting for transfers between devices  337 us (34%)
  matrix products  125 us (13%)
  other arithmetic  69.2 us (7%)
  starting transfers between devices  19.9 us (2%)
    all_to_all x1, waiting for transfers between devices, body(): lax.all_to_all(flattened, ('lat', 'fld'), split_axis=1, concat_axis=2, ti...  172 us
    all_to_all x1, waiting for transfers between devices, body(): lax.all_to_all(outgoing, ('lat', 'fld'), split_axis=2, concat_axis=1, til...  165 us
    unnamed x20, local copies, waits for them, and re-layouts  116 us
    all_to_all x1, local copies, waits for them, and re-layouts, body(): lax.all_to_all(outgoing, ('lat', 'fld'), split_axis=2, concat_axis=1, til...  78.1 us
    reshape x1, local copies, waits for them, and re-layouts, body(): outgoing.transpose(0, 1, 4, 2, 3, 5)  74 us
    dot_general x1, matrix products, body(): jnp.einsum('rsfj,xrs->fjx', masked, angles, preferred_element_type=jnp.fl...  37.9 us
    another operation x1, other arithmetic  36.7 us
    dot_general x1, matrix products, body(): jnp.einsum('fjx,xrs->rsfj', grid_in, angles, preferred_element_type=jnp.f...  28.8 us
  transfers between devices with their start and end apart: 3, of which 2 were waited for; matrix products, arithmetic and copies ran while one was open for 21% of the time, Pallas kernels for 0%

commit v1 on v0

--- a/solution.py
+++ b/solution.py
@@ -1,11 +1,441 @@
+import functools
 import math
 
 import jax
 import jax.numpy as jnp
 from jax import lax
+from jax.experimental import pallas as pl
+from jax.experimental.pallas import tpu as pltpu
 from jax.sharding import PartitionSpec as P
 
 LMAX = 1279
+LANES = 128
+HALF = 64
+GROUP = 8
+BF = jnp.bfloat16
+F32 = jnp.float32
+VMEM_BYTES = 60 * 1024 * 1024
+
+
+def dot(a, b):
+    return jnp.dot(a, b, preferred_element_type=F32)
+
+
+def dot_t(a, b):
+    return lax.dot_general(a, b, (((1,), (1,)), ((), ())), preferred_element_type=F32)
+
+
+def angle_kernel(cos_a, sin_a, cos_b, sin_b, out):
+    cb, sb = cos_b[...], sin_b[...]
+    for a in range(out.shape[1] // LANES):
+        ca = cos_a[:, a : a + 1]
+        sa = sin_a[:, a : a + 1]
+        out[:, a * LANES : (a + 1) * LANES] = (ca * cb - sa * sb).astype(BF)
+
+
+def angle_rows(waves, lon_count):
+    rows = 2 * waves.shape[0]
+    tiles = lon_count // LANES
+    wave_row = jnp.repeat(waves, 2)[:, None]
+    quarter = (jnp.arange(rows, dtype=jnp.int32) % 2)[:, None] * (lon_count // 4)
+    coarse = jnp.arange(LANES, dtype=jnp.int32)[None, :] * LANES
+    fine = jnp.arange(LANES, dtype=jnp.int32)[None, :]
+    unit = 2.0 * math.pi / lon_count
+    phase_a = ((wave_row * coarse + quarter) % lon_count).astype(F32) * unit
+    phase_b = (wave_row * fine % lon_count).astype(F32) * unit
+    scale = 1.0 / math.sqrt(lon_count)
+    step = 256
+    spec = pl.BlockSpec((step, LANES), lambda i: (i, 0))
+    return pl.pallas_call(
+        angle_kernel,
+        grid=(rows // step,),
+        in_specs=[spec] * 4,
+        out_specs=pl.BlockSpec((step, tiles * LANES), lambda i: (i, 0)),
+        out_shape=jax.ShapeDtypeStruct((rows, lon_count), BF),
+        cost_estimate=pl.CostEstimate(
+            flops=4 * rows * lon_count, bytes_accessed=2 * rows * lon_count, transcendentals=0
+        ),
+        name="angles",
+    )(jnp.cos(phase_a), jnp.sin(phase_a), jnp.cos(phase_b) * scale, jnp.sin(phase_b) * scale)
+
+
+def dft_kernel(starts, field_a, field_b, angles, wave_row, modes, out, arranged):
+    first, second, rest = (pl.multiple_of(starts[i], HALF) for i in range(3))
+    for i, field in enumerate((field_a, field_b)):
+        arranged[i * 256 : i * 256 + 128] = field[0, pl.ds(first, 128), :]
+        arranged[i * 256 + 128 : i * 256 + 256] = field[0, pl.ds(second, 128), :]
+        arranged[512 + i * HALF : 512 + (i + 1) * HALF] = field[0, pl.ds(rest, HALF), :]
+    dests, rows, width = out.shape
+    per = 8
+    count = per * rows
+
+    @pl.loop(0, dests // per)
+    def _(i):
+        at = pl.ds(pl.multiple_of(i * count, 16), count)
+        value = dot_t(angles[at, :], arranged[...])
+        value = jnp.where(wave_row[at, :] < modes[...], value, 0.0)
+        out[pl.ds(i * per, per)] = value.astype(BF).reshape(per, rows, width)
+
+
+def dft(grid_in, angles, wave_row, modes, starts, dests):
+    fields, lats, lon = grid_in.shape
+    pairs = fields // 2
+    rows = angles.shape[0]
+    width = 2 * lats
+    flops = 2 * rows * fields * lats * lon
+    return pl.pallas_call(
+        dft_kernel,
+        grid_spec=pltpu.PrefetchScalarGridSpec(
+            num_scalar_prefetch=1,
+            grid=(pairs,),
+            in_specs=[
+                pl.BlockSpec((1, lats, lon), lambda k, s: (k, 0, 0)),
+                pl.BlockSpec((1, lats, lon), lambda k, s: (k + pairs, 0, 0)),
+                pl.BlockSpec((rows, lon), lambda k, s: (0, 0)),
+                pl.BlockSpec((rows, 1), lambda k, s: (0, 0)),
+                pl.BlockSpec((1, width), lambda k, s: (0, 0)),
+            ],
+            out_specs=pl.BlockSpec((dests, rows // dests, width), lambda k, s: (0, 0, k)),
+            scratch_shapes=[pltpu.VMEM((width, lon), BF)],
+        ),
+        out_shape=jax.ShapeDtypeStruct((dests, rows // dests, pairs * width), BF),
+        compiler_params=pltpu.CompilerParams(vmem_limit_bytes=VMEM_BYTES),
+        cost_estimate=pl.CostEstimate(
+            flops=flops, bytes_accessed=2 * fields * lats * (lon + rows), transcendentals=0
+        ),
+        name="dft",
+    )(starts, grid_in, grid_in, angles, wave_row, modes)
+
+
+def inverse_kernel(starts, back, angles, wave_row, modes, out_a, out_b, turned):
+    first, second, rest = (pl.multiple_of(starts[i], HALF) for i in range(3))
+    dests, rows, width = back.shape
+    per = 8
+    count = per * rows
+    for i in range(dests // per):
+        value = back[i * per : (i + 1) * per].reshape(count, width).astype(F32)
+        value = jnp.where(wave_row[i * count : (i + 1) * count, :] < modes[...], value, 0.0)
+        turned[:, i * count : (i + 1) * count] = value.T.astype(BF)
+    lon = angles.shape[1]
+    step = 3 * LANES
+
+    @pl.loop(0, lon // step)
+    def _(n):
+        cols = pl.ds(pl.multiple_of(n * step, LANES), step)
+        value = 2.0 * dot(turned[...], angles[:, cols])
+        for i, out in enumerate((out_a, out_b)):
+            out[0, pl.ds(first, 128), cols] = value[i * 256 : i * 256 + 128]
+            out[0, pl.ds(second, 128), cols] = value[i * 256 + 128 : i * 256 + 256]
+            out[0, pl.ds(rest, HALF), cols] = value[512 + i * HALF : 512 + (i + 1) * HALF]
+
+
+def inverse_kernel_joined(starts, back, angles, wave_row, modes, out, turned):
+    inverse_kernel(starts, back, angles, wave_row, modes, out.at[0], out.at[1], turned)
+
+
+def inverse_dft(back, angles, wave_row, modes, starts, fields, lats):
+    dests, rows, _ = back.shape
+    pairs = fields // 2
+    lon = angles.shape[1]
+    width = 2 * lats
+    flops = 2 * dests * rows * fields * lats * lon
+    out = pl.pallas_call(
+        inverse_kernel_joined,
+        grid_spec=pltpu.PrefetchScalarGridSpec(
+            num_scalar_prefetch=1,
+            grid=(pairs,),
+            in_specs=[
+                pl.BlockSpec((dests, rows, width), lambda k, s: (0, 0, k)),
+                pl.BlockSpec((dests * rows, lon), lambda k, s: (0, 0)),
+                pl.BlockSpec((dests * rows, 1), lambda k, s: (0, 0)),
+                pl.BlockSpec((1, width), lambda k, s: (0, 0)),
+            ],
+            out_specs=pl.BlockSpec((2, 1, lats, lon), lambda k, s: (0, k, 0, 0)),
+            scratch_shapes=[pltpu.VMEM((width, dests * rows), BF)],
+        ),
+        out_shape=jax.ShapeDtypeStruct((2, pairs, lats, lon), F32),
+        compiler_params=pltpu.CompilerParams(vmem_limit_bytes=VMEM_BYTES),
+        cost_estimate=pl.CostEstimate(
+            flops=flops, bytes_accessed=fields * lats * (4 * lon + 2 * dests * rows), transcendentals=0
+        ),
+        name="inverse_dft",
+    )(starts, back, angles, wave_row, modes)
+    return out.reshape(fields, lats, lon)
+
+
+def legendre_kernel(
+    lat_count,
+    fld_count,
+    lats,
+    half_cols,
+    arrived,
+    low,
+    h0,
+    h1,
+    h2,
+    h3,
+    degree4,
+    rates,
+    weights,
+    gather,
+    scatter,
+    mirror,
+    spectra,
+    leaving,
+    even,
+    odd,
+    north,
+    south,
+):
+    pair = pl.program_id(1)
+    blocks = lat_count // 2
+    width = 2 * lats
+    pairs = arrived.shape[2] // width
+    slot_rows = 2 * fld_count * pairs
+    lower = lax.broadcasted_iota(jnp.int32, (GROUP * slot_rows, LANES), 1) < HALF
+    flip_tile = mirror[0]
+    flip_half = mirror[1]
+
+    def swap(x):
+        return pltpu.roll(x, HALF, 1)
+
+    def put(ref, half, at, x):
+        ref[:, half * slot_rows : (half + 1) * slot_rows, at : at + LANES] = x.astype(BF).reshape(
+            GROUP, slot_rows, LANES
+        )
+
+    def get(ref, half, at):
+        return ref[:, half * slot_rows : (half + 1) * slot_rows, at : at + LANES].reshape(
+            GROUP * slot_rows, LANES
+        )
+
+    def stacked(lat):
+        parts = [
+            arrived[lat * fld_count + f, :, k * width : (k + 1) * width]
+            for f in range(fld_count)
+            for k in range(pairs)
+        ]
+        return dot(gather[...], jnp.concatenate(parts, 0))
+
+    @pl.when(pair == 0)
+    def _():
+        rests = []
+        for block in range(blocks):
+            up = stacked(block)
+            down = stacked(lat_count - 1 - block).astype(BF)
+            for piece in range(5):
+                tile = slice(piece * LANES, (piece + 1) * LANES)
+                n = up[:, tile]
+                s = dot(down[:, tile], flip_tile if piece < 4 else flip_half)
+                w = weights[block : block + 1, 2 * LANES :] if piece == 4 else (
+                    weights[block : block + 1, (piece % 2) * LANES : (piece % 2 + 1) * LANES]
+                )
+                e, o = (n + s) * w, (n - s) * w
+                if piece < 4:
+                    at = block * 256 + (piece % 2) * LANES
+                    put(even, piece // 2, at, e)
+                    put(odd, piece // 2, at, o)
+                else:
+                    rests.append((e, o))
+        for b in range(blocks // 2):
+            at = blocks * 256 + b * LANES
+            for ref, c in ((even, 0), (odd, 1)):
+                x, y = rests[2 * b][c], rests[2 * b + 1][c]
+                put(ref, 0, at, jnp.where(lower, x, swap(y)))
+                put(ref, 1, at, jnp.where(lower, swap(x), y))
+
+    def rows_of(load):
+        parts = [load(b * lats, 256) for b in range(blocks)]
+        parts.append(jnp.concatenate([load(b * lats + 256, HALF) for b in range(blocks)], 0))
+        return parts
+
+    def transform(slot, local, even_table, odd_table, cols):
+        def project(ref, parts):
+            total = None
+            for i, part in enumerate(parts):
+                term = dot(ref[slot, :, i * 256 : i * 256 + part.shape[0]], part)
+                total = term if total is None else total + term
+            return total
+
+        results = []
+        tables = []
+        for c, (ref, load) in enumerate(((even, even_table), (odd, odd_table))):
+            parts = rows_of(load)
+            tables.append(parts)
+            d4 = degree4[local, :, c * half_cols : c * half_cols + cols]
+            factor = jnp.where(d4 >= 0.0, 1.0 / (1.0 + rates[...] * d4), 0.0)
+            results.append(project(ref, parts) * factor)
+        for c, value in enumerate(results):
+            for f in range(fld_count):
+                for r in range(2):
+                    at = (f * 2 + r) * pairs
+                    both = jnp.concatenate(
+                        [value[at : at + pairs], value[slot_rows + at : slot_rows + at + pairs]], 0
+                    )
+                    spectra[f, r, local, :, c * half_cols : c * half_cols + cols] = both
+                    if cols < half_cols:
+                        spectra[f, r, local, :, c * half_cols + cols : (c + 1) * half_cols] = (
+                            jnp.zeros((2 * pairs, half_cols - cols), F32)
+                        )
+        coeff = [v.astype(BF) for v in results]
+        for i in range(blocks + 1):
+            sym = dot_t(coeff[0], tables[0][i])
+            anti = dot_t(coeff[1], tables[1][i])
+            at = slice(i * 256, i * 256 + sym.shape[1])
+            north[slot, :, at] = (sym + anti).astype(BF)
+            south[slot, :, at] = (sym - anti).astype(BF)
+
+    transform(
+        2 * pair,
+        0,
+        lambda at, n: low[0, at : at + n, :half_cols],
+        lambda at, n: low[0, at : at + n, half_cols:],
+        half_cols,
+    )
+    transform(
+        2 * pair + 1,
+        1,
+        lambda at, n: jnp.concatenate([h0[0, at : at + n, :], h1[0, at : at + n, :]], 1),
+        lambda at, n: jnp.concatenate([h2[0, at : at + n, :], h3[0, at : at + n, :]], 1),
+        2 * LANES,
+    )
+
+    @pl.when(pair == pl.num_programs(1) - 1)
+    def _():
+        for block in range(blocks):
+            for ref, lat in ((north, block), (south, lat_count - 1 - block)):
+                pieces = [
+                    get(ref, half, block * 256 + t * LANES) for half in range(2) for t in range(2)
+                ]
+                at = blocks * 256 + (block // 2) * LANES
+                x, y = get(ref, 0, at).astype(F32), get(ref, 1, at).astype(F32)
+                rest = jnp.where(lower, x, swap(y)) if block % 2 == 0 else jnp.where(lower, swap(x), y)
+                pieces.append(rest.astype(BF))
+                if ref is south:
+                    pieces = [
+                        dot(p, flip_tile if i < 4 else flip_half).astype(BF)
+                        for i, p in enumerate(pieces)
+                    ]
+                joined = dot(scatter[...], jnp.concatenate(pieces, 1)).astype(BF)
+                for f in range(fld_count):
+                    for k in range(pairs):
+                        row = (f * pairs + k) * 2 * GROUP
+                        leaving[lat * fld_count + f, :, k * width : (k + 1) * width] = joined[
+                            row : row + 2 * GROUP
+                        ]
+
+
+def legendre_step(arrived, tables, own_waves, damp_rates, gauss_weight, lat_count, fld_count):
+    slots, half_lats, columns = tables.shape
+    half_cols = columns // 2
+    sources, _, wide = arrived.shape
+    lats = 2 * half_lats // lat_count
+    width = 2 * lats
+    pairs = wide // width
+    slot_rows = 2 * fld_count * pairs
+    rows = 2 * slot_rows
+    blocks = lat_count // 2
+    groups, inner = slots // GROUP, GROUP // 2
+
+    col_index = jnp.arange(columns, dtype=jnp.int32)
+    offset = jnp.where(col_index < half_cols, 2 * col_index, 2 * col_index - columns + 1)
+    degree = own_waves[:, None] + offset[None, :]
+    ratio = (degree * (degree + 1)).astype(F32) / float(LMAX * (LMAX + 1))
+    degree4 = jnp.where(degree <= LMAX, ratio**4, -1.0)[:, None, :]
+
+    by_field = damp_rates.reshape(fld_count, 2, pairs)
+    rates = jnp.broadcast_to(
+        by_field.transpose(1, 0, 2)[:, :, None, :], (2, fld_count, 2, pairs)
+    ).reshape(rows, 1)
+    w = gauss_weight.reshape(blocks, lats)
+    weights = jnp.concatenate([w, w[:, 256:]], 1)
+
+    size = GROUP * slot_rows
+    target = jnp.arange(size, dtype=jnp.int32)
+    s, rest = target // slot_rows, target % slot_rows
+    f, rest = rest // (2 * pairs), rest % (2 * pairs)
+    r, k = rest // pairs, rest % pairs
+    source = ((f * pairs + k) * GROUP + s) * 2 + r
+    gather = (source[:, None] == target[None, :]).astype(BF)
+    scatter = (source[None, :] == target[:, None]).astype(BF)
+    lane = jnp.arange(LANES, dtype=jnp.int32)
+    place = lane[:, None] + lane[None, :]
+    same_half = lane[:, None] // HALF == lane[None, :] // HALF
+    mirror = jnp.stack(
+        [place == LANES - 1, same_half & (place % LANES == HALF - 1)]
+    ).astype(BF)
+
+    def slot_of(g, p):
+        return g * GROUP + 2 * p
+
+    narrow = [
+        pl.BlockSpec((1, half_lats, LANES), functools.partial(lambda t, g, p: (slot_of(g, p) + 1, 0, t), t))
+        for t in (0, 1, half_cols // LANES, half_cols // LANES + 1)
+    ]
+    whole = lambda *shape: pl.BlockSpec(shape, lambda g, p: (0,) * len(shape))
+    scratch = pltpu.VMEM((GROUP, rows, half_lats), BF)
+    flops = 2 * 2 * slots * rows * half_lats * columns
+    return pl.pallas_call(
+        functools.partial(legendre_kernel, lat_count, fld_count, lats, half_cols),
+        grid=(groups, inner),
+        in_specs=[
+            pl.BlockSpec((sources, 2 * GROUP, wide), lambda g, p: (0, g, 0)),
+            pl.BlockSpec((1, half_lats, columns), lambda g, p: (slot_of(g, p), 0, 0)),
+            *narrow,
+            pl.BlockSpec((2, 1, columns), lambda g, p: (g * inner + p, 0, 0)),
+            whole(rows, 1),
+            whole(blocks, 3 * LANES),
+            whole(size, size),
+            whole(size, size),
+            whole(2, LANES, LANES),
+        ],
+        out_specs=[
+            pl.BlockSpec(
+                (fld_count, 2, 2, 2 * pairs, columns), lambda g, p: (0, 0, g * inner + p, 0, 0)
+            ),
+            pl.BlockSpec((sources, 2 * GROUP, wide), lambda g, p: (0, g, 0)),
+        ],
+        out_shape=[
+            jax.ShapeDtypeStruct((fld_count, 2, slots, 2 * pairs, columns), F32),
+            jax.ShapeDtypeStruct(arrived.shape, BF),
+        ],
+        scratch_shapes=[scratch] * 4,
+        compiler_params=pltpu.CompilerParams(vmem_limit_bytes=VMEM_BYTES),
+        cost_estimate=pl.CostEstimate(
+            flops=flops, bytes_accessed=2 * slots * half_lats * columns, transcendentals=0
+        ),
+        name="legendre",
+    )(arrived, tables, *[tables] * 4, degree4, rates, weights, gather, scatter, mirror)
+
+
+def fast_body(grid_in, legendre, wave_slot, lat_modes, gauss_weight, diffusion):
+    fields, lats, lon = grid_in.shape
+    slots_all = wave_slot.shape[0]
+    lat_count = lax.axis_size("lat")
+    fld_count = lax.axis_size("fld")
+    owners = lat_count * fld_count
+    owned = slots_all // owners
+    lat_index = lax.axis_index("lat")
+    owner = lat_index * fld_count + lax.axis_index("fld")
+    southern = lat_index >= lat_count // 2
+    starts = jnp.where(southern, jnp.array([192, 64, 0]), jnp.array([0, 128, 256])).astype(jnp.int32)
+    flipped = jnp.concatenate([lat_modes[192:], lat_modes[64:192], lat_modes[:64]])
+    ordered = jnp.where(southern, flipped, lat_modes)
+    modes = jnp.concatenate([ordered[:256], ordered[:256], ordered[256:], ordered[256:]])[None, :]
+    wave_row = jnp.repeat(wave_slot, 2)[:, None]
+    own_waves = lax.dynamic_slice_in_dim(wave_slot, owner * owned, owned)
+
+    angles = angle_rows(wave_slot, lon)
+    sent = dft(grid_in, angles, wave_row, modes, starts, owners)
+    arrived = lax.all_to_all(sent, ("lat", "fld"), 0, 0, tiled=True)
+    spectra, leaving = legendre_step(
+        arrived, legendre, own_waves, diffusion, gauss_weight, lat_count, fld_count
+    )
+    back = lax.all_to_all(leaving, ("lat", "fld"), 0, 0, tiled=True)
+    spectra = lax.all_to_all(spectra, "fld", 0, 0, tiled=True)
+    spectra = spectra.transpose(1, 0, 2, 3, 4).reshape(2, fld_count * owned, fields, -1)
+    grid_out = inverse_dft(back, angles, wave_row, modes, starts, fields, lats)
+    return (grid_out, spectra)
 
 
 def angle_table(waves, lon_count):
@@ -81,7 +511,7 @@
     return (spectra, synthesized)
 
 
-def body(grid_in, legendre, wave_slot, lat_modes, gauss_weight, diffusion):
+def general_body(grid_in, legendre, wave_slot, lat_modes, gauss_weight, diffusion):
     fld_dev, lat_dev, lon_count = grid_in.shape
     slots_all = wave_slot.shape[0]
     lat_count = lax.axis_size("lat")
@@ -119,6 +549,22 @@
     return (grid_out, spectra)
 
 
+def body(grid_in, legendre, wave_slot, lat_modes, gauss_weight, diffusion):
+    fields, lats, lon = grid_in.shape
+    slots, _, columns = legendre.shape
+    lat_count = lax.axis_size("lat")
+    fits = (
+        lats == 2 * LANES + HALF
+        and lat_count % 4 == 0
+        and fields == 8
+        and slots % GROUP == 0
+        and lon % (3 * LANES) == 0
+        and columns == 6 * LANES
+    )
+    chosen = fast_body if fits else general_body
+    return chosen(grid_in, legendre, wave_slot, lat_modes, gauss_weight, diffusion)
+
+
 def solution(mesh):
     return jax.shard_map(
         body,

time: 989 us -> 568 us (0.57); the launches traced: 972 us -> 566 us
  local copies, waits for them, and re-layouts: 419 us -> 10.7 us
  Pallas kernels: 0 us -> 130 us
  matrix products: 125 us -> 0 us
  blocking collectives: 0 us -> 59.7 us
  other arithmetic: 69.2 us -> 13.2 us
    reshape x6 -> x3, local copies, waits for them, and re-layouts: 155 us -> 0.85 us  [the longest x1 0.69 us: legendre_step(): rates = jnp.broadcast_to(by_field.transpose(1, 0, 2)[:, :, None, :], (2,...]
    pallas_call x0 -> x4, Pallas kernels: none -> 130 us  [the longest x1 45 us: inverse_dft(): pl.pallas_call(inverse_kernel_joined, grid_spec=pltpu.PrefetchScalarGridS...]
    dot_general x6 -> x0, matrix products: 125 us -> none  [the longest x1 37.9 us: body(): jnp.einsum('rsfj,xrs->fjx', masked, angles, preferred_element_type=jnp.fl...]
    unnamed x20 -> x4, local copies, waits for them, and re-layouts: 116 us -> 0.01 us
    all_to_all x3 -> x0, local copies, waits for them, and re-layouts: 93 us -> none  [the longest x1 78.1 us: body(): lax.all_to_all(outgoing, ('lat', 'fld'), split_axis=2, concat_axis=1, til...]
    all_to_all x0 -> x1, blocking collectives: none -> 59.7 us  [fast_body(): spectra = lax.all_to_all(spectra, 'fld', 0, 0, tiled=True)]
    another operation x1 -> x0, other arithmetic: 36.7 us -> none
    rev x2 -> x0, local copies, waits for them, and re-layouts: 26.2 us -> none  [the longest x1 13.3 us: transform_block(): south_half = jnp.flip(block_data[..., half_lats:], -1).astype(jnp.float32)]
  transfers between devices with their start and end apart: 3 -> 2, of which waited for: 2 -> 2; matrix products, arithmetic and copies ran while one was open for 21% -> 2% of each run, Pallas kernels for 0% -> 0%
where the time goes in v1:
time: 568 us; the launch traced here: 566 us
  waiting for transfers between devices  338 us (60%)
  Pallas kernels  130 us (23%)
  blocking collectives  59.7 us (11%)
  starting transfers between devices  13.3 us (2%)
  other arithmetic  13.2 us (2%)
  local copies, waits for them, and re-layouts  10.7 us (2%)
    all_to_all x1, waiting for transfers between devices, fast_body(): arrived = lax.all_to_all(sent, ('lat', 'fld'), 0, 0, tiled=True)  169 us
    all_to_all x1, waiting for transfers between devices, fast_body(): back = lax.all_to_all(leaving, ('lat', 'fld'), 0, 0, tiled=True)  169 us
    all_to_all x1, blocking collectives, fast_body(): spectra = lax.all_to_all(spectra, 'fld', 0, 0, tiled=True)  59.7 us
    pallas_call x1, Pallas kernels, inverse_dft(): pl.pallas_call(inverse_kernel_joined, grid_spec=pltpu.PrefetchScalarGridS...  45 us
    pallas_call x1, Pallas kernels, dft(): pl.pallas_call(dft_kernel, grid_spec=pltpu.PrefetchScalarGridSpec(num_sca...  37.2 us
    pallas_call x1, Pallas kernels, legendre_step(): pl.pallas_call(functools.partial(legendre_kernel, lat_count, fld_count, l...  36.6 us
    pallas_call x1, Pallas kernels, angle_rows(): pl.pallas_call(angle_kernel, grid=(rows // step,), in_specs=[spec] * 4, o...  11.5 us
  transfers between devices with their start and end apart: 2, of which 2 were waited for; matrix products, arithmetic and copies ran while one was open for 2% of the time, Pallas kernels for 0%

profile of v1, /device:TPU:0, one launch (start us, length us, event | category | flops | bytes accessed | tf_op | source)
XLA Modules:
  0.0 566.1 jit_solution(1238223210564865553)
XLA Ops:
  0.6 0.7 slice.23
  1.3 0.8 fusion.35
  2.2 0.7 add_select_fusion.5
  2.9 0.8 broadcast_in_dim.10
  3.7 0.2 mul.150
  4.0 1.1 broadcast_in_dim_reshape.5.wave_row
  5.0 0.5 broadcast_select_fusion.starts
  5.5 0.1 pad_add_fusion
  5.6 0.6 broadcast_in_dim.11.modes
  6.2 8.9 %fusion.8 = (f32[1536,128]{1,0:T(8,128)}, f32[1536,128]{1,0:T(8,128)}, f32[1536,128]{1,0:T(8,128)}, f32[1536,128]{1,0:T(8,128)}) fusion(s32[1536]{0:T(1024)S(1)} %fusion.25, s32[128]{0:T(128)S(1)} %iota_multiply_fusion.1, s32[1536]{0:T(1024)S(1)} %mul.150), kind=kLoop, calls=%fused_computation.14 | loop fusion | flops 4128768 | bytes 3158528 | tf_op jit(solution)/shard_map/sin | solution.py:59
  15.1 11.5 %angles.1 = bf16[1536,2688]{1,0:T(8,128)(2,1)} custom-call(f32[1536,128]{1,0:T(8,128)} %get-tuple-element.7.cos_a, f32[1536,128]{1,0:T(8,128)} %get-tuple-element.6.sin_a, f32[1536,128]{1,0:T(8,128)} %get-tuple-element.9.cos_b, f32[1536,128]{1,0:T(8,128)} %get-tuple-element.8.sin_b), custom_call_target="tpu_custom_call" | custom-call | flops 16515072 | bytes 8257536 | tf_op jit(solution)/shard_map/angles/pallas_call | solution.py:49
  26.6 37.2 %dft.1 = bf16[32,48,2560]{2,1,0:T(8,128)(2,1)} custom-call(s32[3]{0:T(128)} %broadcast_select_fusion.starts, bf16[8,320,2688]{2,1,0:T(8,128)(2,1)} %field_b.1, bf16[8,320,2688]{2,1,0:T(8,128)(2,1)} %field_b.1, bf16[1536,2688]{1,0:T(8,128)(2,1)} %angles.1, s32[1536,1]{1,0:T(8,128)} %broadcast_in_dim_reshape.5.wave_row, s32[1,640]{1,0:T(1,128)} %broadcast_in_dim.11.modes), custom_call_target="tpu_custom_call" | custom-call | flops 21139292160 | bytes 21626880 | tf_op jit(solution)/shard_map/dft/pallas_call | solution.py:86
  63.9 0.0 copy-start.1
  63.9 0.0 copy-start
  63.9 7.4 %all-to-all-start = ((bf16[32,48,2560]{2,1,0:T(8,128)(2,1)}), bf16[32,48,2560]{2,1,0:T(8,128)(2,1)}, u32[]{:S(2)}, u32[]{:S(2)}) async-start(bf16[32,48,2560]{2,1,0:T(8,128)(2,1)} %dft.1), calls=%async_computation | async-start | bytes 15728640 | tf_op jit(solution)/shard_map/all_to_all | solution.py:430
  71.3 0.8 dynamic_slice.3
  72.1 0.0 copy-done.1
  72.1 0.1 reshape.446
  72.2 0.0 copy-done
  72.2 0.1 reshape.448
  72.3 0.7 reshape.451.rates
  73.0 0.7 pad_maximum_fusion.weights
  73.6 0.1 fusion.20
  73.7 0.6 add_convert_fusion.mirror
  74.4 0.9 compare_select_fusion.degree4
  75.2 0.7 fusion.13
  76.0 169.1 %all-to-all-done.arrived = bf16[32,48,2560]{2,1,0:T(8,128)(2,1)} async-done(((bf16[32,48,2560]{2,1,0:T(8,128)(2,1)}), bf16[32,48,2560]{2,1,0:T(8,128)(2,1)}, u32[]{:S(2)}, u32[]{:S(2)}) %all-to-all-start) | async-done | bytes 7864352 | tf_op jit(solution)/shard_map/all_to_all | solution.py:430
  245.1 36.6 %legendre.1 = (f32[4,2,24,8,768]{4,3,2,1,0:T(8,128)}, bf16[32,48,2560]{2,1,0:T(8,128)(2,1)}) custom-call(bf16[32,48,2560]{2,1,0:T(8,128)(2,1)} %all-to-all-done.arrived, bf16[24,1280,768]{2,1,0:T(8,128)(2,1)} %h3.1, bf16[24,1280,768]{2,1,0:T(8,128)(2,1)} %h3.1, bf16[24,1280,768]{2,1,0:T(8,128)(2,1)} %h3.1, bf16[24,1280,768]{2,1,0:T(8,128)(2,1)} %h3.1, ...), custom_call_target="tpu_custom_call" | custom-call | flops 6039797760 | bytes 47185920 | tf_op jit(solution)/shard_map/legendre/pallas_call | solution.py:378
  281.7 59.7 %all_to_all.15 = f32[4,2,24,8,768]{4,3,2,1,0:T(8,128)} all-to-all(f32[4,2,24,8,768]{4,3,2,1,0:T(8,128)} %get-tuple-element.5), channel_id=1, replica_groups=mesh['lat'=8,'fld'=4] {'fld'}, dimensions={0} | all-to-all | bytes 9437184 | tf_op jit(solution)/shard_map/all_to_all | solution.py:435
  341.4 5.9 %all-to-all-start.1 = ((bf16[32,48,2560]{2,1,0:T(8,128)(2,1)}), bf16[32,48,2560]{2,1,0:T(8,128)(2,1)}, u32[]{:S(2)}, u32[]{:S(2)}) async-start(bf16[32,48,2560]{2,1,0:T(8,128)(2,1)} %get-tuple-element.4), calls=%async_computation.1 | async-start | bytes 15728640 | tf_op jit(solution)/shard_map/all_to_all | solution.py:434
  347.3 4.8 copy.22
  352.1 169.0 %all-to-all-done.1.back = bf16[32,48,2560]{2,1,0:T(8,128)(2,1)} async-done(((bf16[32,48,2560]{2,1,0:T(8,128)(2,1)}), bf16[32,48,2560]{2,1,0:T(8,128)(2,1)}, u32[]{:S(2)}, u32[]{:S(2)}) %all-to-all-start.1) | async-done | bytes 7864352 | tf_op jit(solution)/shard_map/all_to_all | solution.py:434
  521.1 45.0 %inverse_dft.1 = f32[2,4,320,2688]{3,2,1,0:T(8,128)} custom-call(s32[3]{0:T(128)} %broadcast_select_fusion.starts, bf16[32,48,2560]{2,1,0:T(8,128)(2,1)} %all-to-all-done.1.back, bf16[1536,2688]{1,0:T(8,128)(2,1)} %angles.1, s32[1536,1]{1,0:T(8,128)} %broadcast_in_dim_reshape.5.wave_row, s32[1,640]{1,0:T(1,128)} %broadcast_in_dim.11.modes), custom_call_target="tpu_custom_call" | custom-call | flops 21139292160 | bytes 35389440 | tf_op jit(solution)/shard_map/inverse_dft/pallas_call | solution.py:142
  (10 shorter events, 0.1 us)
Async XLA Ops:
  63.9 8.2 %copy-start.1 = (f32[32]{0:T(128)S(1)}, f32[32]{0:T(128)}, u32[]{:S(2)}) copy-start(f32[32]{0:T(128)} %param.13) | copy-start | bytes 388
  63.9 8.3 %copy-start = (f32[1280]{0:T(1024)S(1)}, f32[1280]{0:T(1024)}, u32[]{:S(2)}) copy-start(f32[1280]{0:T(1024)} %param.12) | copy-start | bytes 15364
  63.9 181.2 %all-to-all-start = ((bf16[32,48,2560]{2,1,0:T(8,128)(2,1)}), bf16[32,48,2560]{2,1,0:T(8,128)(2,1)}, u32[]{:S(2)}, u32[]{:S(2)}) async-start(bf16[32,48,2560]{2,1,0:T(8,128)(2,1)} %dft.1), calls=%async_computation | async-start | bytes 15728640 | tf_op jit(solution)/shard_map/all_to_all | solution.py:430
  341.4 179.7 %all-to-all-start.1 = ((bf16[32,48,2560]{2,1,0:T(8,128)(2,1)}), bf16[32,48,2560]{2,1,0:T(8,128)(2,1)}, u32[]{:S(2)}, u32[]{:S(2)}) async-start(bf16[32,48,2560]{2,1,0:T(8,128)(2,1)} %get-tuple-element.4), calls=%async_computation.1 | async-start | bytes 15728640 | tf_op jit(solution)/shard_map/all_to_all | solution.py:434

commit v2 on v1

--- a/solution.py
+++ b/solution.py
@@ -12,6 +12,7 @@
 LANES = 128
 HALF = 64
 GROUP = 8
+CHUNKS = 2
 BF = jnp.bfloat16
 F32 = jnp.float32
 VMEM_BYTES = 60 * 1024 * 1024
@@ -25,89 +26,115 @@
     return lax.dot_general(a, b, (((1,), (1,)), ((), ())), preferred_element_type=F32)
 
 
-def angle_kernel(cos_a, sin_a, cos_b, sin_b, out):
-    cb, sb = cos_b[...], sin_b[...]
-    for a in range(out.shape[1] // LANES):
-        ca = cos_a[:, a : a + 1]
-        sa = sin_a[:, a : a + 1]
-        out[:, a * LANES : (a + 1) * LANES] = (ca * cb - sa * sb).astype(BF)
-
-
-def angle_rows(waves, lon_count):
-    rows = 2 * waves.shape[0]
-    tiles = lon_count // LANES
-    wave_row = jnp.repeat(waves, 2)[:, None]
-    quarter = (jnp.arange(rows, dtype=jnp.int32) % 2)[:, None] * (lon_count // 4)
-    coarse = jnp.arange(LANES, dtype=jnp.int32)[None, :] * LANES
-    fine = jnp.arange(LANES, dtype=jnp.int32)[None, :]
-    unit = 2.0 * math.pi / lon_count
-    phase_a = ((wave_row * coarse + quarter) % lon_count).astype(F32) * unit
-    phase_b = (wave_row * fine % lon_count).astype(F32) * unit
-    scale = 1.0 / math.sqrt(lon_count)
+def turn_cos(phase, count):
+    whole = phase - jnp.floor(phase * (1.0 / count) + 0.5) * count
+    x = whole * (2.0 * math.pi / count)
+    square = x * x
+    total = jnp.full_like(square, 1.0 / math.factorial(18) * -1.0)
+    for order in range(16, -1, -2):
+        total = total * square + (-1.0) ** (order // 2) / math.factorial(order)
+    return total
+
+
+def angle_kernel(lon, wave_row, out):
+    rows = out.shape[0]
+    step = 64
+    scale = 1.0 / math.sqrt(lon)
+    quarter = lon // 4
+
+    @pl.loop(0, rows // step)
+    def _(i):
+        at = pl.ds(pl.multiple_of(i * step, step), step)
+        wave = wave_row[at, :].astype(F32)
+        lane = lax.broadcasted_iota(jnp.int32, (step, LANES), 1).astype(F32)
+        part = lax.broadcasted_iota(jnp.int32, (step, LANES), 0)
+        turn = (part % 2 * quarter).astype(F32)
+        fine = wave * lane
+        coarse = fine * LANES + turn
+        cos_b = turn_cos(fine, lon) * scale
+        sin_b = turn_cos(fine - quarter, lon) * scale
+        cos_a = turn_cos(coarse, lon)
+        sin_a = turn_cos(coarse - quarter, lon)
+        for a in range(lon // LANES):
+            value = cos_a[:, a : a + 1] * cos_b - sin_a[:, a : a + 1] * sin_b
+            out[at, a * LANES : (a + 1) * LANES] = value.astype(BF)
+
+
+def angle_rows(wave_row, lon):
+    rows = wave_row.shape[0]
     step = 256
-    spec = pl.BlockSpec((step, LANES), lambda i: (i, 0))
     return pl.pallas_call(
-        angle_kernel,
+        functools.partial(angle_kernel, lon),
         grid=(rows // step,),
-        in_specs=[spec] * 4,
-        out_specs=pl.BlockSpec((step, tiles * LANES), lambda i: (i, 0)),
-        out_shape=jax.ShapeDtypeStruct((rows, lon_count), BF),
+        in_specs=[pl.BlockSpec((step, 1), lambda i: (i, 0))],
+        out_specs=pl.BlockSpec((step, lon), lambda i: (i, 0)),
+        out_shape=jax.ShapeDtypeStruct((rows, lon), BF),
         cost_estimate=pl.CostEstimate(
-            flops=4 * rows * lon_count, bytes_accessed=2 * rows * lon_count, transcendentals=0
+            flops=4 * rows * lon, bytes_accessed=2 * rows * lon, transcendentals=0
         ),
         name="angles",
-    )(jnp.cos(phase_a), jnp.sin(phase_a), jnp.cos(phase_b) * scale, jnp.sin(phase_b) * scale)
-
-
-def dft_kernel(starts, field_a, field_b, angles, wave_row, modes, out, arranged):
-    first, second, rest = (pl.multiple_of(starts[i], HALF) for i in range(3))
-    for i, field in enumerate((field_a, field_b)):
-        arranged[i * 256 : i * 256 + 128] = field[0, pl.ds(first, 128), :]
-        arranged[i * 256 + 128 : i * 256 + 256] = field[0, pl.ds(second, 128), :]
-        arranged[512 + i * HALF : 512 + (i + 1) * HALF] = field[0, pl.ds(rest, HALF), :]
-    dests, rows, width = out.shape
-    per = 8
-    count = per * rows
-
-    @pl.loop(0, dests // per)
-    def _(i):
-        at = pl.ds(pl.multiple_of(i * count, 16), count)
-        value = dot_t(angles[at, :], arranged[...])
-        value = jnp.where(wave_row[at, :] < modes[...], value, 0.0)
-        out[pl.ds(i * per, per)] = value.astype(BF).reshape(per, rows, width)
-
-
-def dft(grid_in, angles, wave_row, modes, starts, dests):
+    )(wave_row)
+
+
+def dft_kernel(count, starts, *refs):
+    fields = refs[:count]
+    angles, wave_row, modes, out, arranged = refs[count:]
+    pairs = count // 2
+    width = out.shape[2] // pairs
+
+    @pl.when(pl.program_id(0) == 0)
+    def _():
+        first, second, rest = (pl.multiple_of(starts[i], HALF) for i in range(3))
+        for i, field in enumerate(fields):
+            half, pair = divmod(i, pairs)
+            at = pair * width + half * 256
+            arranged[at : at + 128] = field[0, pl.ds(first, 128), :]
+            arranged[at + 128 : at + 256] = field[0, pl.ds(second, 128), :]
+            at = pair * width + 512 + half * HALF
+            arranged[at : at + HALF] = field[0, pl.ds(rest, HALF), :]
+
+    value = dot_t(angles[...], arranged[...])
+    value = jnp.where(wave_row[...] < modes[...], value, 0.0)
+    out[...] = value.astype(BF).reshape(out.shape)
+
+
+def dft(grid_in, angles, wave_row, modes, starts, dests, chunk, chunks):
     fields, lats, lon = grid_in.shape
-    pairs = fields // 2
+    count = fields // chunks
     rows = angles.shape[0]
-    width = 2 * lats
-    flops = 2 * rows * fields * lats * lon
+    wide = count * lats
+    per = dests // 2
+    tile = rows * per // dests
     return pl.pallas_call(
-        dft_kernel,
+        functools.partial(dft_kernel, count),
         grid_spec=pltpu.PrefetchScalarGridSpec(
             num_scalar_prefetch=1,
-            grid=(pairs,),
+            grid=(dests // per,),
             in_specs=[
-                pl.BlockSpec((1, lats, lon), lambda k, s: (k, 0, 0)),
-                pl.BlockSpec((1, lats, lon), lambda k, s: (k + pairs, 0, 0)),
-                pl.BlockSpec((rows, lon), lambda k, s: (0, 0)),
-                pl.BlockSpec((rows, 1), lambda k, s: (0, 0)),
-                pl.BlockSpec((1, width), lambda k, s: (0, 0)),
+                *[
+                    pl.BlockSpec(
+                        (1, lats, lon), functools.partial(lambda f, i, s: (f, 0, 0), chunk * count + f)
+                    )
+                    for f in range(count)
+                ],
+                pl.BlockSpec((tile, lon), lambda i, s: (i, 0)),
+                pl.BlockSpec((tile, 1), lambda i, s: (i, 0)),
+                pl.BlockSpec((1, wide), lambda i, s: (0, 0)),
             ],
-            out_specs=pl.BlockSpec((dests, rows // dests, width), lambda k, s: (0, 0, k)),
-            scratch_shapes=[pltpu.VMEM((width, lon), BF)],
+            out_specs=pl.BlockSpec((per, rows // dests, wide), lambda i, s: (i, 0, 0)),
+            scratch_shapes=[pltpu.VMEM((wide, lon), BF)],
         ),
-        out_shape=jax.ShapeDtypeStruct((dests, rows // dests, pairs * width), BF),
+        out_shape=jax.ShapeDtypeStruct((dests, rows // dests, wide), BF),
         compiler_params=pltpu.CompilerParams(vmem_limit_bytes=VMEM_BYTES),
         cost_estimate=pl.CostEstimate(
-            flops=flops, bytes_accessed=2 * fields * lats * (lon + rows), transcendentals=0
+            flops=2 * rows * wide * lon, bytes_accessed=2 * wide * (lon + rows), transcendentals=0
         ),
         name="dft",
-    )(starts, grid_in, grid_in, angles, wave_row, modes)
-
-
-def inverse_kernel(starts, back, angles, wave_row, modes, out_a, out_b, turned):
+    )(starts, *[grid_in] * count, angles, wave_row, modes)
+
+
+def inverse_kernel(starts, back, angles, wave_row, modes, *refs):
+    out, turned = refs[-2:]
     first, second, rest = (pl.multiple_of(starts[i], HALF) for i in range(3))
     dests, rows, width = back.shape
     per = 8
@@ -117,30 +144,24 @@
         value = jnp.where(wave_row[i * count : (i + 1) * count, :] < modes[...], value, 0.0)
         turned[:, i * count : (i + 1) * count] = value.T.astype(BF)
     lon = angles.shape[1]
-    step = 3 * LANES
-
-    @pl.loop(0, lon // step)
-    def _(n):
-        cols = pl.ds(pl.multiple_of(n * step, LANES), step)
+    step = 6 * LANES
+    for at in range(0, lon, step):
+        cols = slice(at, min(at + step, lon))
         value = 2.0 * dot(turned[...], angles[:, cols])
-        for i, out in enumerate((out_a, out_b)):
-            out[0, pl.ds(first, 128), cols] = value[i * 256 : i * 256 + 128]
-            out[0, pl.ds(second, 128), cols] = value[i * 256 + 128 : i * 256 + 256]
-            out[0, pl.ds(rest, HALF), cols] = value[512 + i * HALF : 512 + (i + 1) * HALF]
-
-
-def inverse_kernel_joined(starts, back, angles, wave_row, modes, out, turned):
-    inverse_kernel(starts, back, angles, wave_row, modes, out.at[0], out.at[1], turned)
-
-
-def inverse_dft(back, angles, wave_row, modes, starts, fields, lats):
-    dests, rows, _ = back.shape
-    pairs = fields // 2
+        for i in range(2):
+            out[0, i, 0, pl.ds(first, 128), cols] = value[i * 256 : i * 256 + 128]
+            out[0, i, 0, pl.ds(second, 128), cols] = value[i * 256 + 128 : i * 256 + 256]
+            out[0, i, 0, pl.ds(rest, HALF), cols] = value[512 + i * HALF : 512 + (i + 1) * HALF]
+
+
+def inverse_dft(back, angles, wave_row, modes, starts, lats, whole, chunk, chunks):
+    dests, rows, wide = back.shape
     lon = angles.shape[1]
     width = 2 * lats
-    flops = 2 * dests * rows * fields * lats * lon
-    out = pl.pallas_call(
-        inverse_kernel_joined,
+    pairs = wide // width
+    given = [] if whole is None else [whole]
+    return pl.pallas_call(
+        inverse_kernel,
         grid_spec=pltpu.PrefetchScalarGridSpec(
             num_scalar_prefetch=1,
             grid=(pairs,),
@@ -149,18 +170,21 @@
                 pl.BlockSpec((dests * rows, lon), lambda k, s: (0, 0)),
                 pl.BlockSpec((dests * rows, 1), lambda k, s: (0, 0)),
                 pl.BlockSpec((1, width), lambda k, s: (0, 0)),
+                *[pl.BlockSpec(memory_space=pl.ANY) for _ in given],
             ],
-            out_specs=pl.BlockSpec((2, 1, lats, lon), lambda k, s: (0, k, 0, 0)),
+            out_specs=pl.BlockSpec((1, 2, 1, lats, lon), lambda k, s: (chunk, 0, k, 0, 0)),
             scratch_shapes=[pltpu.VMEM((width, dests * rows), BF)],
         ),
-        out_shape=jax.ShapeDtypeStruct((2, pairs, lats, lon), F32),
+        out_shape=jax.ShapeDtypeStruct((chunks, 2, pairs, lats, lon), F32),
+        input_output_aliases={5: 0} if given else {},
         compiler_params=pltpu.CompilerParams(vmem_limit_bytes=VMEM_BYTES),
         cost_estimate=pl.CostEstimate(
-            flops=flops, bytes_accessed=fields * lats * (4 * lon + 2 * dests * rows), transcendentals=0
+            flops=2 * dests * rows * wide * lon,
+            bytes_accessed=wide * (4 * lon + 2 * dests * rows),
+            transcendentals=0,
         ),
         name="inverse_dft",
-    )(starts, back, angles, wave_row, modes)
-    return out.reshape(fields, lats, lon)
+    )(starts, back, angles, wave_row, modes[:, :width], *given)
 
 
 def legendre_kernel(
@@ -422,20 +446,45 @@
     flipped = jnp.concatenate([lat_modes[192:], lat_modes[64:192], lat_modes[:64]])
     ordered = jnp.where(southern, flipped, lat_modes)
     modes = jnp.concatenate([ordered[:256], ordered[:256], ordered[256:], ordered[256:]])[None, :]
+    modes = jnp.tile(modes, (1, fields // CHUNKS // 2))
     wave_row = jnp.repeat(wave_slot, 2)[:, None]
     own_waves = lax.dynamic_slice_in_dim(wave_slot, owner * owned, owned)
-
-    angles = angle_rows(wave_slot, lon)
-    sent = dft(grid_in, angles, wave_row, modes, starts, owners)
-    arrived = lax.all_to_all(sent, ("lat", "fld"), 0, 0, tiled=True)
-    spectra, leaving = legendre_step(
-        arrived, legendre, own_waves, diffusion, gauss_weight, lat_count, fld_count
-    )
-    back = lax.all_to_all(leaving, ("lat", "fld"), 0, 0, tiled=True)
-    spectra = lax.all_to_all(spectra, "fld", 0, 0, tiled=True)
-    spectra = spectra.transpose(1, 0, 2, 3, 4).reshape(2, fld_count * owned, fields, -1)
-    grid_out = inverse_dft(back, angles, wave_row, modes, starts, fields, lats)
-    return (grid_out, spectra)
+    rates = diffusion.reshape(fld_count, CHUNKS, fields // CHUNKS)
+
+    def exchange(x):
+        return lax.all_to_all(x, ("lat", "fld"), 0, 0, tiled=True)
+
+    angles = angle_rows(wave_row, lon)
+    arrived = [
+        exchange(dft(grid_in, angles, wave_row, modes, starts, owners, c, CHUNKS))
+        for c in range(CHUNKS)
+    ]
+    parts, back = [], []
+    for c in range(CHUNKS):
+        part, leaving = legendre_step(
+            arrived[c], legendre, own_waves, rates[:, c], gauss_weight, lat_count, fld_count
+        )
+        parts.append(part)
+        back.append(exchange(leaving))
+    spectra = share_spectra(jnp.concatenate(parts, 3))
+    whole = None
+    for c in range(CHUNKS):
+        whole = inverse_dft(back[c], angles, wave_row, modes, starts, lats, whole, c, CHUNKS)
+    return (whole.reshape(fields, lats, lon), spectra)
+
+
+def share_spectra(spectra):
+    count, parts, slots, fields, columns = spectra.shape
+    mine = lax.axis_index("fld")
+    result = jnp.zeros((parts, count, slots, fields, columns), F32)
+    for shift in range(count):
+        block = lax.dynamic_index_in_dim(spectra, (mine + shift) % count, 0, keepdims=False)
+        if shift:
+            ring = [(i, (i + shift) % count) for i in range(count)]
+            block = lax.ppermute(block, "fld", ring)
+        at = (mine + count - shift) % count
+        result = lax.dynamic_update_slice(result, block[:, None], (0, at, 0, 0, 0))
+    return result.reshape(parts, count * slots, fields, columns)
 
 
 def angle_table(waves, lon_count):
@@ -556,9 +605,10 @@
     fits = (
         lats == 2 * LANES + HALF
         and lat_count % 4 == 0
-        and fields == 8
+        and fields % (2 * CHUNKS) == 0
+        and lat_count * lax.axis_size("fld") % 8 == 0
         and slots % GROUP == 0
-        and lon % (3 * LANES) == 0
+        and lon % LANES == 0 and lon % 4 == 0
         and columns == 6 * LANES
     )
     chosen = fast_body if fits else general_body

time: 568 us -> 471 us (0.83)
  waiting for transfers between devices: 338 us -> 257 us
  blocking collectives: 59.7 us -> 0 us
  Pallas kernels: 130 us -> 158 us
  starting transfers between devices: 13.3 us -> 26 us
  local copies, waits for them, and re-layouts: 10.7 us -> 17 us
    all_to_all x2 -> x4, waiting for transfers between devices: 338 us -> 179 us  [exchange(): return lax.all_to_all(x, ('lat', 'fld'), 0, 0, tiled=True)]
    ppermute x0 -> x3, waiting for transfers between devices: none -> 77.3 us  [share_spectra(): block = lax.ppermute(block, 'fld', ring)]
    all_to_all x1 -> x0, blocking collectives: 59.7 us -> none  [fast_body(): spectra = lax.all_to_all(spectra, 'fld', 0, 0, tiled=True)]
    pallas_call x1 -> x2, Pallas kernels: 36.6 us -> 62.2 us  [legendre_step(): pl.pallas_call(functools.partial(legendre_kernel, lat_count, fld_count, l...]
    all_to_all x2 -> x4, starting transfers between devices: 13.3 us -> 22.8 us  [exchange(): return lax.all_to_all(x, ('lat', 'fld'), 0, 0, tiled=True)]
    sin x1 -> x0, other arithmetic: 8.93 us -> none  [angle_rows(): jnp.sin(phase_a)]
    dynamic_update_slice x0 -> x3, local copies, waits for them, and re-layouts: none -> 7.08 us  [share_spectra(): result = lax.dynamic_update_slice(result, block[:, None], (0, at, 0, 0, 0))]
    pallas_call x3 -> x5, Pallas kernels: 93.7 us -> 95.5 us  [the longest x2 41.9 us: inverse_dft(): pl.pallas_call(inverse_kernel, grid_spec=pltpu.PrefetchScalarGridSpec(num...]
  transfers between devices with their start and end apart: 2 -> 7, of which waited for: 2 -> 5; matrix products, arithmetic and copies ran while one was open for 2% -> 4% of each run, Pallas kernels for 0% -> 22%
where the time goes in v2:
time: 471 us; the launch traced here: 467 us
  waiting for transfers between devices  257 us (55%)
  Pallas kernels  158 us (34%)
  starting transfers between devices  26 us (6%)
  local copies, waits for them, and re-layouts  17 us (4%)
  other arithmetic  9.22 us (2%)
    all_to_all x4, waiting for transfers between devices, exchange(): return lax.all_to_all(x, ('lat', 'fld'), 0, 0, tiled=True)  179 us
    ppermute x3, waiting for transfers between devices, share_spectra(): block = lax.ppermute(block, 'fld', ring)  77.3 us
    pallas_call x2, Pallas kernels, legendre_step(): pl.pallas_call(functools.partial(legendre_kernel, lat_count, fld_count, l...  62.2 us
    pallas_call x2, Pallas kernels, inverse_dft(): pl.pallas_call(inverse_kernel, grid_spec=pltpu.PrefetchScalarGridSpec(num...  41.9 us
    pallas_call x2, Pallas kernels, dft(): pl.pallas_call(functools.partial(dft_kernel, count), grid_spec=pltpu.Pref...  36.6 us
    all_to_all x4, starting transfers between devices, exchange(): return lax.all_to_all(x, ('lat', 'fld'), 0, 0, tiled=True)  22.8 us
    pallas_call x1, Pallas kernels, angle_rows(): pl.pallas_call(functools.partial(angle_kernel, lon), grid=(rows // step,)...  17 us
  transfers between devices with their start and end apart: 7, of which 5 were waited for; matrix products, arithmetic and copies ran while one was open for 4% of the time, Pallas kernels for 22%

profile of v2, /device:TPU:0, one launch (start us, length us, event | category | flops | bytes accessed | tf_op | source)
XLA Modules:
  0.0 467.4 jit_solution(11584640859151598170)
XLA Ops:
  0.6 0.7 slice.34
  1.3 0.8 fusion.27
  2.1 0.7 add_select_fusion.2
  2.9 0.6 broadcast_select_fusion.starts
  3.4 0.1 pad_add_fusion
  3.5 0.6 copy.40
  4.1 0.8 broadcast_in_dim.21
  5.0 1.1 broadcast_in_dim_reshape.4.wave_row.refs_5_
  6.1 17.0 %angles.1.refs_4_ = bf16[1536,2688]{1,0:T(8,128)(2,1)} custom-call(s32[1536,1]{1,0:T(8,128)} %broadcast_in_dim_reshape.4.wave_row.refs_5_), custom_call_target="tpu_custom_call" | custom-call | flops 16515072 | bytes 8257536 | tf_op jit(solution)/shard_map/angles/pallas_call | solution.py:66
  23.0 18.3 %dft.3 = bf16[32,48,1280]{2,1,0:T(8,128)(2,1)} custom-call(s32[3]{0:T(128)} %broadcast_select_fusion.starts, bf16[8,320,2688]{2,1,0:T(8,128)(2,1)} %refs_3_.3, bf16[8,320,2688]{2,1,0:T(8,128)(2,1)} %refs_3_.3, bf16[8,320,2688]{2,1,0:T(8,128)(2,1)} %refs_3_.3, bf16[8,320,2688]{2,1,0:T(8,128)(2,1)} %refs_3_.3, bf16[1536,2688]{1,0:T(8,128)(2,1)} %angles.1.refs_4_, ...), custom_call_target="tpu_custom_call" | custom-call | flops 10569646080 | bytes 10813440 | tf_op jit(solution)/shard_map/dft/pallas_call | solution.py:108
  41.3 7.4 %all-to-all-start.2 = ((bf16[32,48,1280]{2,1,0:T(8,128)(2,1)}), bf16[32,48,1280]{2,1,0:T(8,128)(2,1)}, u32[]{:S(2)}, u32[]{:S(2)}) async-start(bf16[32,48,1280]{2,1,0:T(8,128)(2,1)} %dft.3), calls=%async_computation.2 | async-start | bytes 7864320 | tf_op jit(solution)/shard_map/all_to_all | solution.py:455
  48.8 18.3 %dft.2 = bf16[32,48,1280]{2,1,0:T(8,128)(2,1)} custom-call(s32[3]{0:T(128)} %broadcast_select_fusion.starts, bf16[8,320,2688]{2,1,0:T(8,128)(2,1)} %refs_3_.3, bf16[8,320,2688]{2,1,0:T(8,128)(2,1)} %refs_3_.3, bf16[8,320,2688]{2,1,0:T(8,128)(2,1)} %refs_3_.3, bf16[8,320,2688]{2,1,0:T(8,128)(2,1)} %refs_3_.3, bf16[1536,2688]{1,0:T(8,128)(2,1)} %angles.1.refs_4_, ...), custom_call_target="tpu_custom_call" | custom-call | flops 10569646080 | bytes 10813440 | tf_op jit(solution)/shard_map/dft/pallas_call | solution.py:108
  67.1 0.0 copy-start.4
  67.1 0.0 copy-start.3
  67.1 70.3 %all-to-all-done.2.arrived = bf16[32,48,1280]{2,1,0:T(8,128)(2,1)} async-done(((bf16[32,48,1280]{2,1,0:T(8,128)(2,1)}), bf16[32,48,1280]{2,1,0:T(8,128)(2,1)}, u32[]{:S(2)}, u32[]{:S(2)}) %all-to-all-start.2) | async-done | bytes 3932192 | tf_op jit(solution)/shard_map/all_to_all | solution.py:455
  137.4 5.1 %all-to-all-start = ((bf16[32,48,1280]{2,1,0:T(8,128)(2,1)}), bf16[32,48,1280]{2,1,0:T(8,128)(2,1)}, u32[]{:S(2)}, u32[]{:S(2)}) async-start(bf16[32,48,1280]{2,1,0:T(8,128)(2,1)} %dft.2), calls=%async_computation | async-start | bytes 7864320 | tf_op jit(solution)/shard_map/all_to_all | solution.py:455
  142.5 0.8 dynamic_slice.16
  143.2 0.0 copy-done.4
  143.2 0.1 reshape.437
  143.3 0.1 copy.35
  143.4 0.1 copy.36
  143.5 0.0 copy-done.3
  143.5 0.1 reshape.439
  143.6 0.7 reshape.444.rates
  144.3 0.7 pad_maximum_fusion.weights
  145.0 0.1 fusion.19
  145.1 0.6 add_convert_fusion.mirror
  145.7 0.7 fusion.21
  146.4 0.9 compare_select_fusion.degree4
  147.3 31.1 %legendre.3 = (f32[4,2,24,4,768]{4,3,2,1,0:T(4,128)}, bf16[32,48,1280]{2,1,0:T(8,128)(2,1)}) custom-call(bf16[32,48,1280]{2,1,0:T(8,128)(2,1)} %all-to-all-done.2.arrived, bf16[24,1280,768]{2,1,0:T(8,128)(2,1)} %h3.3, bf16[24,1280,768]{2,1,0:T(8,128)(2,1)} %h3.3, bf16[24,1280,768]{2,1,0:T(8,128)(2,1)} %h3.3, bf16[24,1280,768]{2,1,0:T(8,128)(2,1)} %h3.3, ...), custom_call_target="tpu_custom_call" | custom-call | flops 3019898880 | bytes 47185920 | tf_op jit(solution)/shard_map/legendre/pallas_call | solution.py:402
  178.4 52.7 %all-to-all-done.arrived = bf16[32,48,1280]{2,1,0:T(8,128)(2,1)} async-done(((bf16[32,48,1280]{2,1,0:T(8,128)(2,1)}), bf16[32,48,1280]{2,1,0:T(8,128)(2,1)}, u32[]{:S(2)}, u32[]{:S(2)}) %all-to-all-start) | async-done | bytes 3932192 | tf_op jit(solution)/shard_map/all_to_all | solution.py:455
  231.1 5.3 %all-to-all-start.3 = ((bf16[32,48,1280]{2,1,0:T(8,128)(2,1)}), bf16[32,48,1280]{2,1,0:T(8,128)(2,1)}, u32[]{:S(2)}, u32[]{:S(2)}) async-start(bf16[32,48,1280]{2,1,0:T(8,128)(2,1)} %get-tuple-element.7), calls=%async_computation.3 | async-start | bytes 7864320 | tf_op jit(solution)/shard_map/all_to_all | solution.py:455
  236.3 0.1 copy.31
  236.4 0.1 copy.32
  236.5 0.7 reshape.443.rates
  237.2 31.1 %legendre.2 = (f32[4,2,24,4,768]{4,3,2,1,0:T(4,128)}, bf16[32,48,1280]{2,1,0:T(8,128)(2,1)}) custom-call(bf16[32,48,1280]{2,1,0:T(8,128)(2,1)} %all-to-all-done.arrived, bf16[24,1280,768]{2,1,0:T(8,128)(2,1)} %h3.3, bf16[24,1280,768]{2,1,0:T(8,128)(2,1)} %h3.3, bf16[24,1280,768]{2,1,0:T(8,128)(2,1)} %h3.3, bf16[24,1280,768]{2,1,0:T(8,128)(2,1)} %h3.3, ...), custom_call_target="tpu_custom_call" | custom-call | flops 3019898880 | bytes 47185920 | tf_op jit(solution)/shard_map/legendre/pallas_call | solution.py:402
  268.3 56.4 %all-to-all-done.3.back = bf16[32,48,1280]{2,1,0:T(8,128)(2,1)} async-done(((bf16[32,48,1280]{2,1,0:T(8,128)(2,1)}), bf16[32,48,1280]{2,1,0:T(8,128)(2,1)}, u32[]{:S(2)}, u32[]{:S(2)}) %all-to-all-start.3) | async-done | bytes 3932192 | tf_op jit(solution)/shard_map/all_to_all | solution.py:455
  324.8 0.0 copy-start
  324.8 5.1 %all-to-all-start.1 = ((bf16[32,48,1280]{2,1,0:T(8,128)(2,1)}), bf16[32,48,1280]{2,1,0:T(8,128)(2,1)}, u32[]{:S(2)}, u32[]{:S(2)}) async-start(bf16[32,48,1280]{2,1,0:T(8,128)(2,1)} %get-tuple-element.6), calls=%async_computation.1 | async-start | bytes 7864320 | tf_op jit(solution)/shard_map/all_to_all | solution.py:455
  329.9 0.0 copy-done
  329.9 0.0 copy-start.2
  329.9 3.6 fusion.1
  333.5 0.2 collective-permute-start
  333.7 1.6 collective-permute-start.1
  335.3 1.4 collective-permute-start.2
  336.7 0.0 copy-done.2
  336.7 0.6 slice.43.modes
  337.2 0.0 copy-start.1
  337.2 2.6 broadcast_in_dim.25
  339.8 0.0 copy-done.1
  339.8 1.3 fusion.4
  341.1 51.8 %collective-permute-done = f32[2,24,8,768]{3,2,1,0:T(8,128)} collective-permute-done((f32[2,24,8,768]{3,2,1,0:T(8,128)}, f32[2,24,8,768]{3,2,1,0:T(8,128)}, u32[]{:S(2)}, u32[]{:S(2)}) %collective-permute-start) | collective-permute-done | bytes 1179680 | tf_op jit(solution)/shard_map/ppermute | solution.py:484
  392.9 2.4 bitcast_dynamic-update-slice_fusion.2
  395.3 0.0 collective-permute-done.1
  395.3 2.4 bitcast_dynamic-update-slice_fusion.1
  397.6 25.5 %collective-permute-done.2 = f32[2,24,8,768]{3,2,1,0:T(8,128)} collective-permute-done((f32[2,24,8,768]{3,2,1,0:T(8,128)S(1)}, f32[2,24,8,768]{3,2,1,0:T(8,128)}, u32[]{:S(2)}, u32[]{:S(2)}) %collective-permute-start.2) | collective-permute-done | bytes 1179680 | tf_op jit(solution)/shard_map/ppermute | solution.py:484
  423.2 2.4 bitcast_dynamic-update-slice_fusion
  425.5 21.0 %inverse_dft.2.refs_0_ = f32[2,2,2,320,2688]{4,3,2,1,0:T(8,128)} custom-call(s32[3]{0:T(128)} %broadcast_select_fusion.starts, bf16[32,48,1280]{2,1,0:T(8,128)(2,1)} %all-to-all-done.3.back, bf16[1536,2688]{1,0:T(8,128)(2,1)} %angles.1.refs_4_, s32[1536,1]{1,0:T(8,128)} %broadcast_in_dim_reshape.4.wave_row.refs_5_, s32[1,640]{1,0:T(1,128)} %slice.43.modes), custom_call_target="tpu_custom_call" | custom-call | flops 10569646080 | bytes 17694720 | tf_op jit(solution)/shard_map/inverse_dft/pallas_call | solution.py:163
  446.5 0.0 all-to-all-done.1.back
  446.5 21.0 %inverse_dft.3 = f32[2,2,2,320,2688]{4,3,2,1,0:T(8,128)} custom-call(s32[3]{0:T(128)} %broadcast_select_fusion.starts, bf16[32,48,1280]{2,1,0:T(8,128)(2,1)} %all-to-all-done.1.back, bf16[1536,2688]{1,0:T(8,128)(2,1)} %angles.1.refs_4_, s32[1536,1]{1,0:T(8,128)} %broadcast_in_dim_reshape.4.wave_row.refs_5_, ...), custom_call_target="tpu_custom_call", output_to_operand_aliasing={{}: (5, {})} | custom-call | flops 10569646080 | bytes 17694720 | tf_op jit(solution)/shard_map/inverse_dft/pallas_call | solution.py:163
  (10 shorter events, 0.1 us)
Async XLA Ops:
  41.3 96.0 %all-to-all-start.2 = ((bf16[32,48,1280]{2,1,0:T(8,128)(2,1)}), bf16[32,48,1280]{2,1,0:T(8,128)(2,1)}, u32[]{:S(2)}, u32[]{:S(2)}) async-start(bf16[32,48,1280]{2,1,0:T(8,128)(2,1)} %dft.3), calls=%async_computation.2 | async-start | bytes 7864320 | tf_op jit(solution)/shard_map/all_to_all | solution.py:455
  67.1 76.1 %copy-start.4 = (f32[32]{0:T(128)S(1)}, f32[32]{0:T(128)}, u32[]{:S(2)}) copy-start(f32[32]{0:T(128)} %param.13) | copy-start | bytes 388
  67.1 76.4 %copy-start.3 = (f32[1280]{0:T(1024)S(1)}, f32[1280]{0:T(1024)}, u32[]{:S(2)}) copy-start(f32[1280]{0:T(1024)} %param.12) | copy-start | bytes 15364
  137.4 93.7 %all-to-all-start = ((bf16[32,48,1280]{2,1,0:T(8,128)(2,1)}), bf16[32,48,1280]{2,1,0:T(8,128)(2,1)}, u32[]{:S(2)}, u32[]{:S(2)}) async-start(bf16[32,48,1280]{2,1,0:T(8,128)(2,1)} %dft.2), calls=%async_computation | async-start | bytes 7864320 | tf_op jit(solution)/shard_map/all_to_all | solution.py:455
  231.1 93.7 %all-to-all-start.3 = ((bf16[32,48,1280]{2,1,0:T(8,128)(2,1)}), bf16[32,48,1280]{2,1,0:T(8,128)(2,1)}, u32[]{:S(2)}, u32[]{:S(2)}) async-start(bf16[32,48,1280]{2,1,0:T(8,128)(2,1)} %get-tuple-element.7), calls=%async_computation.3 | async-start | bytes 7864320 | tf_op jit(solution)/shard_map/all_to_all | solution.py:455
  324.8 5.1 %copy-start = (f32[4,2,24,4,768]{4,3,2,1,0:T(4,128)S(1)}, f32[4,2,24,4,768]{4,3,2,1,0:T(4,128)}, u32[]{:S(2)}) copy-start(f32[4,2,24,4,768]{4,3,2,1,0:T(4,128)} %get-tuple-element.8) | copy-start | bytes 7077892
  324.8 121.7 %all-to-all-start.1 = ((bf16[32,48,1280]{2,1,0:T(8,128)(2,1)}), bf16[32,48,1280]{2,1,0:T(8,128)(2,1)}, u32[]{:S(2)}, u32[]{:S(2)}) async-start(bf16[32,48,1280]{2,1,0:T(8,128)(2,1)} %get-tuple-element.6), calls=%async_computation.1 | async-start | bytes 7864320 | tf_op jit(solution)/shard_map/all_to_all | solution.py:455
  329.9 6.8 %copy-start.2 = (s32[1,1,2,640]{3,1,2,0:T(1,128)S(1)}, s32[1,1,2,640]{3,1,2,0:T(1,128)}, u32[]{:S(2)}) copy-start(s32[1,1,2,640]{3,1,2,0:T(1,128)} %copy.40) | copy-start | bytes 15364
  333.5 59.4 %collective-permute-start = (f32[2,24,8,768]{3,2,1,0:T(8,128)}, f32[2,24,8,768]{3,2,1,0:T(8,128)}, u32[]{:S(2)}, u32[]{:S(2)}) collective-permute-start(f32[2,24,8,768]{3,2,1,0:T(8,128)} %get-tuple-element.11), channel_id=1, source_target_pairs={{0,1},{1,2},{2,3},{3,0},{4,5},{5,6},{6,7},{7,4},{8,9},{9,10},{10,1... | collective-permute-start | bytes 3538952 | tf_op jit(solution)/shard_map/ppermute | solution.py:484
  333.7 61.6 %collective-permute-start.1 = (f32[2,24,8,768]{3,2,1,0:T(8,128)}, f32[2,24,8,768]{3,2,1,0:T(8,128)}, u32[]{:S(2)}, u32[]{:S(2)}) collective-permute-start(f32[2,24,8,768]{3,2,1,0:T(8,128)} %get-tuple-element.12), channel_id=1, source_target_pairs={{0,2},{1,3},{2,0},{3,1},{4,6},{5,7},{6,4},{7,5},{8,10},{9,11},{10,... | collective-permute-start | bytes 3538952 | tf_op jit(solution)/shard_map/ppermute | solution.py:484
  335.3 87.8 %collective-permute-start.2 = (f32[2,24,8,768]{3,2,1,0:T(8,128)S(1)}, f32[2,24,8,768]{3,2,1,0:T(8,128)}, u32[]{:S(2)}, u32[]{:S(2)}) collective-permute-start(f32[2,24,8,768]{3,2,1,0:T(8,128)S(1)} %get-tuple-element.10), channel_id=1, source_target_pairs={{0,3},{1,0},{2,1},{3,2},{4,7},{5,4},{6,5},{7,6},{8,11},{9,8},{10,9... | collective-permute-start | bytes 3538952 | tf_op jit(solution)/shard_map/ppermute | solution.py:484
  337.2 2.6 copy-start.1

commit v3 on v2

--- a/solution.py
+++ b/solution.py
@@ -16,6 +16,7 @@
 BF = jnp.bfloat16
 F32 = jnp.float32
 VMEM_BYTES = 60 * 1024 * 1024
+INVERSE_VMEM_BYTES = 44 * 1024 * 1024
 
 
 def dot(a, b):
@@ -40,23 +41,25 @@
     rows = out.shape[0]
     step = 64
     scale = 1.0 / math.sqrt(lon)
-    quarter = lon // 4
+    tiles = lon // LANES
+    restart = (tiles + 1) // 2
 
     @pl.loop(0, rows // step)
     def _(i):
         at = pl.ds(pl.multiple_of(i * step, step), step)
-        wave = wave_row[at, :].astype(F32)
+        wave = jnp.broadcast_to(wave_row[at, :].astype(F32), (step, LANES))
         lane = lax.broadcasted_iota(jnp.int32, (step, LANES), 1).astype(F32)
         part = lax.broadcasted_iota(jnp.int32, (step, LANES), 0)
-        turn = (part % 2 * quarter).astype(F32)
-        fine = wave * lane
-        coarse = fine * LANES + turn
-        cos_b = turn_cos(fine, lon) * scale
-        sin_b = turn_cos(fine - quarter, lon) * scale
-        cos_a = turn_cos(coarse, lon)
-        sin_a = turn_cos(coarse - quarter, lon)
-        for a in range(lon // LANES):
-            value = cos_a[:, a : a + 1] * cos_b - sin_a[:, a : a + 1] * sin_b
+        turn = (part % 2 * (lon // 4)).astype(F32)
+        fine = wave * lane + turn
+        coarse = wave * LANES
+        double = 2.0 * turn_cos(coarse, lon)
+        for a in range(tiles):
+            if a % restart == 0:
+                before = turn_cos(fine + coarse * (a - 1), lon) * scale
+                value = turn_cos(fine + coarse * a, lon) * scale
+            else:
+                before, value = value, double * value - before
             out[at, a * LANES : (a + 1) * LANES] = value.astype(BF)
 
 
@@ -167,7 +170,7 @@
             grid=(pairs,),
             in_specs=[
                 pl.BlockSpec((dests, rows, width), lambda k, s: (0, 0, k)),
-                pl.BlockSpec((dests * rows, lon), lambda k, s: (0, 0)),
+                pl.BlockSpec(memory_space=pltpu.VMEM),
                 pl.BlockSpec((dests * rows, 1), lambda k, s: (0, 0)),
                 pl.BlockSpec((1, width), lambda k, s: (0, 0)),
                 *[pl.BlockSpec(memory_space=pl.ANY) for _ in given],
@@ -177,7 +180,7 @@
         ),
         out_shape=jax.ShapeDtypeStruct((chunks, 2, pairs, lats, lon), F32),
         input_output_aliases={5: 0} if given else {},
-        compiler_params=pltpu.CompilerParams(vmem_limit_bytes=VMEM_BYTES),
+        compiler_params=pltpu.CompilerParams(vmem_limit_bytes=INVERSE_VMEM_BYTES),
         cost_estimate=pl.CostEstimate(
             flops=2 * dests * rows * wide * lon,
             bytes_accessed=wide * (4 * lon + 2 * dests * rows),
@@ -464,27 +467,38 @@
         part, leaving = legendre_step(
             arrived[c], legendre, own_waves, rates[:, c], gauss_weight, lat_count, fld_count
         )
-        parts.append(part)
+        if parts:
+            places, blocks = zip(*parts[-1])
+            leaving, blocks = lax.optimization_barrier((leaving, blocks))
+            parts[-1] = list(zip(places, blocks))
         back.append(exchange(leaving))
-    spectra = share_spectra(jnp.concatenate(parts, 3))
+        parts.append(share_spectra(part))
     whole = None
+    columns = legendre.shape[2]
+    spectra = jnp.zeros((2, fld_count, owned, fields, columns), F32)
     for c in range(CHUNKS):
         whole = inverse_dft(back[c], angles, wave_row, modes, starts, lats, whole, c, CHUNKS)
-    return (whole.reshape(fields, lats, lon), spectra)
-
-
-def share_spectra(spectra):
-    count, parts, slots, fields, columns = spectra.shape
+        if c == 0:
+            whole, spectra = lax.optimization_barrier((whole, spectra))
+    for c in range(CHUNKS):
+        for at, block in parts[c]:
+            spectra = lax.dynamic_update_slice(
+                spectra, block[:, None], (0, at, 0, c * (fields // CHUNKS), 0)
+            )
+    return (whole.reshape(fields, lats, lon), spectra.reshape(2, -1, fields, columns))
+
+
+def share_spectra(part):
+    count = part.shape[0]
     mine = lax.axis_index("fld")
-    result = jnp.zeros((parts, count, slots, fields, columns), F32)
+    blocks = []
     for shift in range(count):
-        block = lax.dynamic_index_in_dim(spectra, (mine + shift) % count, 0, keepdims=False)
+        block = lax.dynamic_index_in_dim(part, (mine + shift) % count, 0, keepdims=False)
         if shift:
             ring = [(i, (i + shift) % count) for i in range(count)]
             block = lax.ppermute(block, "fld", ring)
-        at = (mine + count - shift) % count
-        result = lax.dynamic_update_slice(result, block[:, None], (0, at, 0, 0, 0))
-    return result.reshape(parts, count * slots, fields, columns)
+        blocks.append(((mine + count - shift) % count, block))
+    return blocks
 
 
 def angle_table(waves, lon_count):

time: 471 us -> 431 us (0.915)
  waiting for transfers between devices: 257 us -> 227 us
  Pallas kernels: 158 us -> 150 us
  other arithmetic: 9.22 us -> 4.28 us
    ppermute x3 -> x6, waiting for transfers between devices: 77.3 us -> 53.8 us  [share_spectra(): block = lax.ppermute(block, 'fld', ring)]
    pallas_call x1, Pallas kernels: 17 us -> 9.32 us  [angle_rows(): pl.pallas_call(functools.partial(angle_kernel, lon), grid=(rows // step,)...]
    all_to_all x4, waiting for transfers between devices: 179 us -> 174 us  [exchange(): return lax.all_to_all(x, ('lat', 'fld'), 0, 0, tiled=True)]
  transfers between devices with their start and end apart: 7 -> 10, of which waited for: 5 -> 10; matrix products, arithmetic and copies ran while one was open for 4% -> 4% of each run, Pallas kernels for 22% -> 24%
where the time goes in v3:
time: 431 us
  waiting for transfers between devices  227 us (53%)
  Pallas kernels  150 us (35%)
  starting transfers between devices  28.4 us (7%)
  local copies, waits for them, and re-layouts  20.2 us (5%)
    all_to_all x4, waiting for transfers between devices, exchange(): return lax.all_to_all(x, ('lat', 'fld'), 0, 0, tiled=True)  174 us
    pallas_call x2, Pallas kernels, legendre_step(): pl.pallas_call(functools.partial(legendre_kernel, lat_count, fld_count, l...  62.2 us
    ppermute x6, waiting for transfers between devices, share_spectra(): block = lax.ppermute(block, 'fld', ring)  53.8 us
    pallas_call x2, Pallas kernels, inverse_dft(): pl.pallas_call(inverse_kernel, grid_spec=pltpu.PrefetchScalarGridSpec(num...  41.4 us
    pallas_call x2, Pallas kernels, dft(): pl.pallas_call(functools.partial(dft_kernel, count), grid_spec=pltpu.Pref...  36.6 us
    all_to_all x4, starting transfers between devices, exchange(): return lax.all_to_all(x, ('lat', 'fld'), 0, 0, tiled=True)  22 us
    pallas_call x1, Pallas kernels, angle_rows(): pl.pallas_call(functools.partial(angle_kernel, lon), grid=(rows // step,)...  9.32 us
    dynamic_update_slice x8, local copies, waits for them, and re-layouts, fast_body(): lax.dynamic_update_slice(spectra, block[:, None], (0, at, 0, c * (fields...  8.94 us
  transfers between devices with their start and end apart: 10, of which 10 were waited for; matrix products, arithmetic and copies ran while one was open for 4% of the time, Pallas kernels for 24%

profile of v3, /device:TPU:0, one launch (start us, length us, event | category | flops | bytes accessed | tf_op | source)
XLA Modules:
  0.0 430.8 jit_solution(7691606336623049463)
XLA Ops:
  0.6 0.8 fusion.18
  1.5 0.7 slice.34
  2.1 0.7 add_select_fusion.2
  2.8 0.1 pad_add_fusion
  2.9 0.6 copy.40
  3.5 0.8 broadcast_in_dim.29
  4.4 1.1 broadcast_in_dim_reshape.4.wave_row.refs_5_
  5.5 9.3 %angles.1.refs_4_ = bf16[1536,2688]{1,0:T(8,128)(2,1)} custom-call(s32[1536,1]{1,0:T(8,128)} %broadcast_in_dim_reshape.4.wave_row.refs_5_), custom_call_target="tpu_custom_call" | custom-call | flops 16515072 | bytes 8257536 | tf_op jit(solution)/shard_map/angles/pallas_call | solution.py:69
  14.8 0.0 copy-done.10
  14.8 0.5 broadcast_select_fusion.starts
  15.3 18.3 %dft.3 = bf16[32,48,1280]{2,1,0:T(8,128)(2,1)} custom-call(s32[3]{0:T(128)} %broadcast_select_fusion.starts, bf16[8,320,2688]{2,1,0:T(8,128)(2,1)} %refs_3_.3, bf16[8,320,2688]{2,1,0:T(8,128)(2,1)} %refs_3_.3, bf16[8,320,2688]{2,1,0:T(8,128)(2,1)} %refs_3_.3, bf16[8,320,2688]{2,1,0:T(8,128)(2,1)} %refs_3_.3, bf16[1536,2688]{1,0:T(8,128)(2,1)} %angles.1.refs_4_, ...), custom_call_target="tpu_custom_call" | custom-call | flops 10569646080 | bytes 10813440 | tf_op jit(solution)/shard_map/dft/pallas_call | solution.py:111
  33.6 6.8 %all-to-all-start.1 = ((bf16[32,48,1280]{2,1,0:T(8,128)(2,1)}), bf16[32,48,1280]{2,1,0:T(8,128)(2,1)}, u32[]{:S(2)}, u32[]{:S(2)}) async-start(bf16[32,48,1280]{2,1,0:T(8,128)(2,1)} %dft.3), calls=%async_computation.1 | async-start | bytes 7864320 | tf_op jit(solution)/shard_map/all_to_all | solution.py:458
  40.4 18.3 %dft.2 = bf16[32,48,1280]{2,1,0:T(8,128)(2,1)} custom-call(s32[3]{0:T(128)} %broadcast_select_fusion.starts, bf16[8,320,2688]{2,1,0:T(8,128)(2,1)} %refs_3_.3, bf16[8,320,2688]{2,1,0:T(8,128)(2,1)} %refs_3_.3, bf16[8,320,2688]{2,1,0:T(8,128)(2,1)} %refs_3_.3, bf16[8,320,2688]{2,1,0:T(8,128)(2,1)} %refs_3_.3, bf16[1536,2688]{1,0:T(8,128)(2,1)} %angles.1.refs_4_, ...), custom_call_target="tpu_custom_call" | custom-call | flops 10569646080 | bytes 10813440 | tf_op jit(solution)/shard_map/dft/pallas_call | solution.py:111
  58.7 70.3 %all-to-all-done.1.arrived = bf16[32,48,1280]{2,1,0:T(8,128)(2,1)} async-done(((bf16[32,48,1280]{2,1,0:T(8,128)(2,1)}), bf16[32,48,1280]{2,1,0:T(8,128)(2,1)}, u32[]{:S(2)}, u32[]{:S(2)}) %all-to-all-start.1) | async-done | bytes 3932192 | tf_op jit(solution)/shard_map/all_to_all | solution.py:458
  129.0 5.1 %all-to-all-start = ((bf16[32,48,1280]{2,1,0:T(8,128)(2,1)}), bf16[32,48,1280]{2,1,0:T(8,128)(2,1)}, u32[]{:S(2)}, u32[]{:S(2)}) async-start(bf16[32,48,1280]{2,1,0:T(8,128)(2,1)} %dft.2), calls=%async_computation | async-start | bytes 7864320 | tf_op jit(solution)/shard_map/all_to_all | solution.py:458
  134.1 0.8 dynamic_slice.28
  134.9 0.1 reshape.439
  135.0 0.1 reshape.437
  135.0 0.1 copy.35
  135.1 0.1 copy.36
  135.3 0.7 reshape.444.rates
  136.0 0.7 pad_maximum_fusion.weights
  136.6 0.1 fusion.10
  136.7 0.6 add_convert_fusion.mirror
  137.4 0.7 fusion.12
  138.1 0.9 compare_select_fusion.degree4
  139.0 31.1 %legendre.3 = (f32[4,2,24,4,768]{4,3,2,1,0:T(4,128)}, bf16[32,48,1280]{2,1,0:T(8,128)(2,1)}) custom-call(bf16[32,48,1280]{2,1,0:T(8,128)(2,1)} %all-to-all-done.1.arrived, bf16[24,1280,768]{2,1,0:T(8,128)(2,1)} %h3.3, bf16[24,1280,768]{2,1,0:T(8,128)(2,1)} %h3.3, bf16[24,1280,768]{2,1,0:T(8,128)(2,1)} %h3.3, bf16[24,1280,768]{2,1,0:T(8,128)(2,1)} %h3.3, ...), custom_call_target="tpu_custom_call" | custom-call | flops 3019898880 | bytes 47185920 | tf_op jit(solution)/shard_map/legendre/pallas_call | solution.py:405
  170.1 52.6 %all-to-all-done.arrived = bf16[32,48,1280]{2,1,0:T(8,128)(2,1)} async-done(((bf16[32,48,1280]{2,1,0:T(8,128)(2,1)}), bf16[32,48,1280]{2,1,0:T(8,128)(2,1)}, u32[]{:S(2)}, u32[]{:S(2)}) %all-to-all-start) | async-done | bytes 3932192 | tf_op jit(solution)/shard_map/all_to_all | solution.py:458
  222.7 5.1 %all-to-all-start.3 = ((bf16[32,48,1280]{2,1,0:T(8,128)(2,1)}), bf16[32,48,1280]{2,1,0:T(8,128)(2,1)}, u32[]{:S(2)}, u32[]{:S(2)}) async-start(bf16[32,48,1280]{2,1,0:T(8,128)(2,1)} %get-tuple-element.16), calls=%async_computation.3 | async-start | bytes 7864320 | tf_op jit(solution)/shard_map/all_to_all | solution.py:458
  227.8 1.6 dynamic-slice_bitcast_fusion.3
  229.4 0.2 collective-permute-start
  229.6 1.6 collective-permute-start.1
  231.2 1.4 collective-permute-start.2
  232.6 0.1 copy.31
  232.7 0.1 copy.32
  232.8 0.7 reshape.443.rates
  233.5 31.1 %legendre.2 = (f32[4,2,24,4,768]{4,3,2,1,0:T(4,128)}, bf16[32,48,1280]{2,1,0:T(8,128)(2,1)}) custom-call(bf16[32,48,1280]{2,1,0:T(8,128)(2,1)} %all-to-all-done.arrived, bf16[24,1280,768]{2,1,0:T(8,128)(2,1)} %h3.3, bf16[24,1280,768]{2,1,0:T(8,128)(2,1)} %h3.3, bf16[24,1280,768]{2,1,0:T(8,128)(2,1)} %h3.3, bf16[24,1280,768]{2,1,0:T(8,128)(2,1)} %h3.3, ...), custom_call_target="tpu_custom_call" | custom-call | flops 3019898880 | bytes 47185920 | tf_op jit(solution)/shard_map/legendre/pallas_call | solution.py:405
  264.6 0.0 copy-start.3
  264.6 12.2 %collective-permute-done = f32[2,24,4,768]{3,2,1,0:T(4,128)S(1)} collective-permute-done((f32[2,24,4,768]{3,2,1,0:T(4,128)}, f32[2,24,4,768]{3,2,1,0:T(4,128)S(1)}, u32[]{:S(2)}, u32[]{:S(2)}) %collective-permute-start) | collective-permute-done | bytes 589856 | tf_op jit(solution)/shard_map/ppermute | solution.py:499
  276.8 1.7 collective-permute-done.1
  278.5 12.1 %collective-permute-done.2 = f32[2,24,4,768]{3,2,1,0:T(4,128)} collective-permute-done((f32[2,24,4,768]{3,2,1,0:T(4,128)}, f32[2,24,4,768]{3,2,1,0:T(4,128)}, u32[]{:S(2)}, u32[]{:S(2)}) %collective-permute-start.2) | collective-permute-done | bytes 589856 | tf_op jit(solution)/shard_map/ppermute | solution.py:499
  290.7 25.7 %all-to-all-done.3.back = bf16[32,48,1280]{2,1,0:T(8,128)(2,1)} async-done(((bf16[32,48,1280]{2,1,0:T(8,128)(2,1)}), bf16[32,48,1280]{2,1,0:T(8,128)(2,1)}, u32[]{:S(2)}, u32[]{:S(2)}) %all-to-all-start.3) | async-done | bytes 3932192 | tf_op jit(solution)/shard_map/all_to_all | solution.py:458
  316.4 5.1 %all-to-all-start.2 = ((bf16[32,48,1280]{2,1,0:T(8,128)(2,1)}), bf16[32,48,1280]{2,1,0:T(8,128)(2,1)}, u32[]{:S(2)}, u32[]{:S(2)}) async-start(bf16[32,48,1280]{2,1,0:T(8,128)(2,1)} %get-tuple-element.15), calls=%async_computation.2 | async-start | bytes 7864320 | tf_op jit(solution)/shard_map/all_to_all | solution.py:458
  321.5 0.0 copy-done.3
  321.5 0.3 dynamic-slice_bitcast_fusion
  321.9 0.2 collective-permute-start.3
  322.1 1.6 collective-permute-start.4
  323.7 1.4 collective-permute-start.5
  325.1 0.0 copy-done
  325.1 20.7 %inverse_dft.2.refs_0_ = f32[2,2,2,320,2688]{4,3,2,1,0:T(8,128)} custom-call(s32[3]{0:T(128)S(1)} %copy-done.1, bf16[32,48,1280]{2,1,0:T(8,128)(2,1)} %all-to-all-done.3.back, bf16[1536,2688]{1,0:T(8,128)(2,1)} %angles.1.refs_4_, s32[1536,1]{1,0:T(8,128)S(1)} %copy-done, s32[1,640]{1,0:T(1,128)S(1)} %slice.44.modes), custom_call_target="tpu_custom_call" | custom-call | flops 10569646080 | bytes 17694720 | tf_op jit(solution)/shard_map/inverse_dft/pallas_call | solution.py:166
  345.8 2.6 broadcast_in_dim.33
  348.4 0.9 bitcast_dynamic-update-slice_fusion.7
  349.2 0.9 bitcast_dynamic-update-slice_fusion.6
  350.1 1.9 bitcast_dynamic-update-slice_fusion.5
  352.0 1.9 bitcast_dynamic-update-slice_fusion.4
  353.9 0.9 bitcast_dynamic-update-slice_fusion.3
  354.8 15.7 %collective-permute-done.3 = f32[2,24,4,768]{3,2,1,0:T(4,128)S(1)} collective-permute-done((f32[2,24,4,768]{3,2,1,0:T(4,128)S(1)}, f32[2,24,4,768]{3,2,1,0:T(4,128)S(1)}, u32[]{:S(2)}, u32[]{:S(2)}) %collective-permute-start.3) | collective-permute-done | bytes 589856 | tf_op jit(solution)/shard_map/ppermute | solution.py:499
  370.5 0.9 bitcast_dynamic-update-slice_fusion.2
  371.3 0.8 collective-permute-done.4
  372.1 0.9 bitcast_dynamic-update-slice_fusion.1
  373.0 11.3 %collective-permute-done.5 = f32[2,24,4,768]{3,2,1,0:T(4,128)S(1)} collective-permute-done((f32[2,24,4,768]{3,2,1,0:T(4,128)S(1)}, f32[2,24,4,768]{3,2,1,0:T(4,128)S(1)}, u32[]{:S(2)}, u32[]{:S(2)}) %collective-permute-start.5) | collective-permute-done | bytes 589856 | tf_op jit(solution)/shard_map/ppermute | solution.py:499
  384.3 0.9 bitcast_dynamic-update-slice_fusion
  385.1 25.0 %all-to-all-done.2.back = bf16[32,48,1280]{2,1,0:T(8,128)(2,1)} async-done(((bf16[32,48,1280]{2,1,0:T(8,128)(2,1)}), bf16[32,48,1280]{2,1,0:T(8,128)(2,1)}, u32[]{:S(2)}, u32[]{:S(2)}) %all-to-all-start.2) | async-done | bytes 3932192 | tf_op jit(solution)/shard_map/all_to_all | solution.py:458
  410.1 20.7 %inverse_dft.3 = f32[2,2,2,320,2688]{4,3,2,1,0:T(8,128)} custom-call(s32[3]{0:T(128)S(1)} %copy-done.1, bf16[32,48,1280]{2,1,0:T(8,128)(2,1)} %all-to-all-done.2.back, bf16[1536,2688]{1,0:T(8,128)(2,1)} %angles.1.refs_4_, s32[1536,1]{1,0:T(8,128)S(1)} %copy-done, s32[1,640]{1,0:T(1,128)S(1)} %slice.44.modes, ...), custom_call_target="tpu_custom_call", output_to_operand_aliasing={{}: (5, {})} | custom-call | flops 10569646080 | bytes 17694720 | tf_op jit(solution)/shard_map/inverse_dft/pallas_call | solution.py:166
  (29 shorter events, 0.1 us)
Async XLA Ops:
  5.5 9.3 %copy-start.10 = (s32[3]{0:T(128)S(1)}, s32[3]{0:T(128)}, u32[]{:S(2)}) copy-start(s32[3]{0:T(128)} %constant.256.clone) | copy-start | bytes 40
  33.6 95.4 %all-to-all-start.1 = ((bf16[32,48,1280]{2,1,0:T(8,128)(2,1)}), bf16[32,48,1280]{2,1,0:T(8,128)(2,1)}, u32[]{:S(2)}, u32[]{:S(2)}) async-start(bf16[32,48,1280]{2,1,0:T(8,128)(2,1)} %dft.3), calls=%async_computation.1 | async-start | bytes 7864320 | tf_op jit(solution)/shard_map/all_to_all | solution.py:458
  58.7 76.2 %copy-start.8 = (f32[1280]{0:T(1024)S(1)}, f32[1280]{0:T(1024)}, u32[]{:S(2)}) copy-start(f32[1280]{0:T(1024)} %param.12) | copy-start | bytes 15364
  58.7 76.2 %copy-start.9 = (f32[32]{0:T(128)S(1)}, f32[32]{0:T(128)}, u32[]{:S(2)}) copy-start(f32[32]{0:T(128)} %param.13) | copy-start | bytes 388
  129.0 93.7 %all-to-all-start = ((bf16[32,48,1280]{2,1,0:T(8,128)(2,1)}), bf16[32,48,1280]{2,1,0:T(8,128)(2,1)}, u32[]{:S(2)}, u32[]{:S(2)}) async-start(bf16[32,48,1280]{2,1,0:T(8,128)(2,1)} %dft.2), calls=%async_computation | async-start | bytes 7864320 | tf_op jit(solution)/shard_map/all_to_all | solution.py:458
  170.1 57.8 %copy-start.2 = (f32[4,2,24,4,768]{4,3,2,1,0:T(4,128)S(1)}, f32[4,2,24,4,768]{4,3,2,1,0:T(4,128)}, u32[]{:S(2)}) copy-start(f32[4,2,24,4,768]{4,3,2,1,0:T(4,128)} %get-tuple-element.14) | copy-start | bytes 7077892
  222.7 93.7 %all-to-all-start.3 = ((bf16[32,48,1280]{2,1,0:T(8,128)(2,1)}), bf16[32,48,1280]{2,1,0:T(8,128)(2,1)}, u32[]{:S(2)}, u32[]{:S(2)}) async-start(bf16[32,48,1280]{2,1,0:T(8,128)(2,1)} %get-tuple-element.16), calls=%async_computation.3 | async-start | bytes 7864320 | tf_op jit(solution)/shard_map/all_to_all | solution.py:458
  229.4 47.4 %collective-permute-start = (f32[2,24,4,768]{3,2,1,0:T(4,128)}, f32[2,24,4,768]{3,2,1,0:T(4,128)S(1)}, u32[]{:S(2)}, u32[]{:S(2)}) collective-permute-start(f32[2,24,4,768]{3,2,1,0:T(4,128)} %get-tuple-element.29), channel_id=1, source_target_pairs={{0,1},{1,2},{2,3},{3,0},{4,5},{5,6},{6,7},{7,4},{8,9},{9,10},{10,1... | collective-permute-start | bytes 1769480 | tf_op jit(solution)/shard_map/ppermute | solution.py:499
  229.6 48.9 %collective-permute-start.1 = (f32[2,24,4,768]{3,2,1,0:T(4,128)}, f32[2,24,4,768]{3,2,1,0:T(4,128)}, u32[]{:S(2)}, u32[]{:S(2)}) collective-permute-start(f32[2,24,4,768]{3,2,1,0:T(4,128)} %get-tuple-element.28), channel_id=1, source_target_pairs={{0,2},{1,3},{2,0},{3,1},{4,6},{5,7},{6,4},{7,5},{8,10},{9,11},{10,... | collective-permute-start | bytes 1769480 | tf_op jit(solution)/shard_map/ppermute | solution.py:499
  231.2 59.4 %collective-permute-start.2 = (f32[2,24,4,768]{3,2,1,0:T(4,128)}, f32[2,24,4,768]{3,2,1,0:T(4,128)}, u32[]{:S(2)}, u32[]{:S(2)}) collective-permute-start(f32[2,24,4,768]{3,2,1,0:T(4,128)} %get-tuple-element.27), channel_id=1, source_target_pairs={{0,3},{1,0},{2,1},{3,2},{4,7},{5,4},{6,5},{7,6},{8,11},{9,8},{10,9... | collective-permute-start | bytes 1769480 | tf_op jit(solution)/shard_map/ppermute | solution.py:499
  264.6 56.9 %copy-start.7 = (s32[1,1,2,640]{3,1,2,0:T(1,128)S(1)}, s32[1,1,2,640]{3,1,2,0:T(1,128)}, u32[]{:S(2)}) copy-start(s32[1,1,2,640]{3,1,2,0:T(1,128)} %copy.40) | copy-start | bytes 15364
  264.6 56.9 %copy-start.3 = (f32[4,2,24,4,768]{4,3,2,1,0:T(4,128)S(1)}, f32[4,2,24,4,768]{4,3,2,1,0:T(4,128)}, u32[]{:S(2)}) copy-start(f32[4,2,24,4,768]{4,3,2,1,0:T(4,128)} %get-tuple-element.23) | copy-start | bytes 7077892
  276.8 13.9 %copy-start.5 = (f32[2,24,4,768]{3,2,1,0:T(4,128)}, f32[2,24,4,768]{3,2,1,0:T(4,128)S(1)}, u32[]{:S(2)}) copy-start(f32[2,24,4,768]{3,2,1,0:T(4,128)S(1)} %collective-permute-done) | copy-start | bytes 1769476
  290.7 34.4 %copy-start = (s32[1536,1]{1,0:T(8,128)S(1)}, s32[1536,1]{1,0:T(8,128)}, u32[]{:S(2)}) copy-start(s32[1536,1]{1,0:T(8,128)} %broadcast_in_dim_reshape.4.wave_row.refs_5_) | copy-start | bytes 18436
  290.7 34.4 %copy-start.1 = (s32[3]{0:T(128)S(1)}, s32[3]{0:T(128)}, u32[]{:S(2)}) copy-start(s32[3]{0:T(128)} %broadcast_select_fusion.starts) | copy-start | bytes 40
  316.4 93.7 %all-to-all-start.2 = ((bf16[32,48,1280]{2,1,0:T(8,128)(2,1)}), bf16[32,48,1280]{2,1,0:T(8,128)(2,1)}, u32[]{:S(2)}, u32[]{:S(2)}) async-start(bf16[32,48,1280]{2,1,0:T(8,128)(2,1)} %get-tuple-element.15), calls=%async_computation.2 | async-start | bytes 7864320 | tf_op jit(solution)/shard_map/all_to_all | solution.py:458
  321.9 48.6 %collective-permute-start.3 = (f32[2,24,4,768]{3,2,1,0:T(4,128)S(1)}, f32[2,24,4,768]{3,2,1,0:T(4,128)S(1)}, u32[]{:S(2)}, u32[]{:S(2)}) collective-permute-start(f32[2,24,4,768]{3,2,1,0:T(4,128)S(1)} %get-tuple-element.26), channel_id=1, source_target_pairs={{0,1},{1,2},{2,3},{3,0},{4,5},{5,6},{6,7},{7,4},{8,9},{9,10},{10,1... | collective-permute-start | bytes 1769480 | tf_op jit(solution)/shard_map/ppermute | solution.py:499
  322.1 50.0 %collective-permute-start.4 = (f32[2,24,4,768]{3,2,1,0:T(4,128)S(1)}, f32[2,24,4,768]{3,2,1,0:T(4,128)S(1)}, u32[]{:S(2)}, u32[]{:S(2)}) collective-permute-start(f32[2,24,4,768]{3,2,1,0:T(4,128)S(1)} %get-tuple-element.25), channel_id=1, source_target_pairs={{0,2},{1,3},{2,0},{3,1},{4,6},{5,7},{6,4},{7,5},{8,10},{9,11},{10,... | collective-permute-start | bytes 1769480 | tf_op jit(solution)/shard_map/ppermute | solution.py:499
  323.7 60.5 %collective-permute-start.5 = (f32[2,24,4,768]{3,2,1,0:T(4,128)S(1)}, f32[2,24,4,768]{3,2,1,0:T(4,128)S(1)}, u32[]{:S(2)}, u32[]{:S(2)}) collective-permute-start(f32[2,24,4,768]{3,2,1,0:T(4,128)S(1)} %get-tuple-element.24), channel_id=1, source_target_pairs={{0,3},{1,0},{2,1},{3,2},{4,7},{5,4},{6,5},{7,6},{8,11},{9,8},{10,9... | collective-permute-start | bytes 1769480 | tf_op jit(solution)/shard_map/ppermute | solution.py:499
  345.8 2.6 copy-start.4
  345.8 3.5 copy-start.6

commit v4 on v3

--- a/solution.py
+++ b/solution.py
@@ -12,11 +12,11 @@
 LANES = 128
 HALF = 64
 GROUP = 8
-CHUNKS = 2
+OUTWARD = ((2,), (0, 1, 3))
+RETURN = ((2,), (0, 1), (3,))
 BF = jnp.bfloat16
 F32 = jnp.float32
 VMEM_BYTES = 60 * 1024 * 1024
-INVERSE_VMEM_BYTES = 44 * 1024 * 1024
 
 
 def dot(a, b):
@@ -29,12 +29,12 @@
 
 def turn_cos(phase, count):
     whole = phase - jnp.floor(phase * (1.0 / count) + 0.5) * count
-    x = whole * (2.0 * math.pi / count)
-    square = x * x
-    total = jnp.full_like(square, 1.0 / math.factorial(18) * -1.0)
-    for order in range(16, -1, -2):
+    half = whole * (math.pi / count)
+    square = half * half
+    total = jnp.full_like(square, -1.0 / math.factorial(14))
+    for order in range(12, -1, -2):
         total = total * square + (-1.0) ** (order // 2) / math.factorial(order)
-    return total
+    return 2.0 * (total * total) - 1.0
 
 
 def angle_kernel(lon, wave_row, out):
@@ -42,7 +42,7 @@
     step = 64
     scale = 1.0 / math.sqrt(lon)
     tiles = lon // LANES
-    restart = (tiles + 1) // 2
+    middle = tiles // 2
 
     @pl.loop(0, rows // step)
     def _(i):
@@ -54,13 +54,21 @@
         fine = wave * lane + turn
         coarse = wave * LANES
         double = 2.0 * turn_cos(coarse, lon)
-        for a in range(tiles):
-            if a % restart == 0:
-                before = turn_cos(fine + coarse * (a - 1), lon) * scale
-                value = turn_cos(fine + coarse * a, lon) * scale
-            else:
-                before, value = value, double * value - before
-            out[at, a * LANES : (a + 1) * LANES] = value.astype(BF)
+        pair = [turn_cos(fine + coarse * a, lon) * scale for a in (middle, middle + 1)]
+
+        def put(a, x):
+            out[at, a * LANES : (a + 1) * LANES] = x.astype(BF)
+
+        put(middle, pair[0])
+        put(middle + 1, pair[1])
+        before, value = pair
+        for a in range(middle + 2, tiles):
+            before, value = value, double * value - before
+            put(a, value)
+        value, before = pair
+        for a in range(middle - 1, -1, -1):
+            before, value = value, double * value - before
+            put(a, value)
 
 
 def angle_rows(wave_row, lon):
@@ -82,14 +90,13 @@
 def dft_kernel(count, starts, *refs):
     fields = refs[:count]
     angles, wave_row, modes, out, arranged = refs[count:]
-    pairs = count // 2
-    width = out.shape[2] // pairs
+    width = out.shape[2] // (count // 2)
 
     @pl.when(pl.program_id(0) == 0)
     def _():
         first, second, rest = (pl.multiple_of(starts[i], HALF) for i in range(3))
         for i, field in enumerate(fields):
-            half, pair = divmod(i, pairs)
+            pair, half = divmod(i, 2)
             at = pair * width + half * 256
             arranged[at : at + 128] = field[0, pl.ds(first, 128), :]
             arranged[at + 128 : at + 256] = field[0, pl.ds(second, 128), :]
@@ -101,12 +108,12 @@
     out[...] = value.astype(BF).reshape(out.shape)
 
 
-def dft(grid_in, angles, wave_row, modes, starts, dests, chunk, chunks):
-    fields, lats, lon = grid_in.shape
-    count = fields // chunks
+def dft(grid_in, angles, wave_row, modes, starts, dests, pairs):
+    _, lats, lon = grid_in.shape
+    count = 2 * len(pairs)
     rows = angles.shape[0]
     wide = count * lats
-    per = dests // 2
+    per = dests // 4
     tile = rows * per // dests
     return pl.pallas_call(
         functools.partial(dft_kernel, count),
@@ -116,9 +123,10 @@
             in_specs=[
                 *[
                     pl.BlockSpec(
-                        (1, lats, lon), functools.partial(lambda f, i, s: (f, 0, 0), chunk * count + f)
+                        (1, lats, lon), functools.partial(lambda f, i, s: (f, 0, 0), 2 * pair + half)
                     )
-                    for f in range(count)
+                    for pair in pairs
+                    for half in range(2)
                 ],
                 pl.BlockSpec((tile, lon), lambda i, s: (i, 0)),
                 pl.BlockSpec((tile, 1), lambda i, s: (i, 0)),
@@ -133,61 +141,62 @@
             flops=2 * rows * wide * lon, bytes_accessed=2 * wide * (lon + rows), transcendentals=0
         ),
         name="dft",
-    )(starts, *[grid_in] * count, angles, wave_row, modes)
+    )(starts, *[grid_in] * count, angles, wave_row, jnp.tile(modes, (1, len(pairs))))
 
 
 def inverse_kernel(starts, back, angles, wave_row, modes, *refs):
     out, turned = refs[-2:]
     first, second, rest = (pl.multiple_of(starts[i], HALF) for i in range(3))
-    dests, rows, width = back.shape
-    per = 8
-    count = per * rows
-    for i in range(dests // per):
-        value = back[i * per : (i + 1) * per].reshape(count, width).astype(F32)
-        value = jnp.where(wave_row[i * count : (i + 1) * count, :] < modes[...], value, 0.0)
-        turned[:, i * count : (i + 1) * count] = value.T.astype(BF)
-    lon = angles.shape[1]
-    step = 6 * LANES
-    for at in range(0, lon, step):
-        cols = slice(at, min(at + step, lon))
-        value = 2.0 * dot(turned[...], angles[:, cols])
-        for i in range(2):
-            out[0, i, 0, pl.ds(first, 128), cols] = value[i * 256 : i * 256 + 128]
-            out[0, i, 0, pl.ds(second, 128), cols] = value[i * 256 + 128 : i * 256 + 256]
-            out[0, i, 0, pl.ds(rest, HALF), cols] = value[512 + i * HALF : 512 + (i + 1) * HALF]
-
-
-def inverse_dft(back, angles, wave_row, modes, starts, lats, whole, chunk, chunks):
+
+    @pl.when(pl.program_id(1) == 0)
+    def _():
+        dests, rows, width = back.shape
+        per = 8
+        count = per * rows
+        for i in range(dests // per):
+            value = back[i * per : (i + 1) * per].reshape(count, width).astype(F32)
+            value = jnp.where(wave_row[i * count : (i + 1) * count, :] < modes[...], value, 0.0)
+            turned[:, i * count : (i + 1) * count] = (2.0 * value).astype(BF).T
+
+    value = dot(turned[...], angles[...])
+    for i in range(2):
+        out[i, pl.ds(first, 128), :] = value[i * 256 : i * 256 + 128]
+        out[i, pl.ds(second, 128), :] = value[i * 256 + 128 : i * 256 + 256]
+        out[i, pl.ds(rest, HALF), :] = value[512 + i * HALF : 512 + (i + 1) * HALF]
+
+
+def inverse_dft(back, angles, wave_row, modes, starts, shape, whole, pair):
     dests, rows, wide = back.shape
-    lon = angles.shape[1]
+    _, lats, lon = shape
     width = 2 * lats
     pairs = wide // width
+    step = lon // 3
     given = [] if whole is None else [whole]
     return pl.pallas_call(
         inverse_kernel,
         grid_spec=pltpu.PrefetchScalarGridSpec(
             num_scalar_prefetch=1,
-            grid=(pairs,),
+            grid=(pairs, lon // step),
             in_specs=[
-                pl.BlockSpec((dests, rows, width), lambda k, s: (0, 0, k)),
-                pl.BlockSpec(memory_space=pltpu.VMEM),
-                pl.BlockSpec((dests * rows, 1), lambda k, s: (0, 0)),
-                pl.BlockSpec((1, width), lambda k, s: (0, 0)),
+                pl.BlockSpec((dests, rows, width), lambda k, n, s: (0, 0, k)),
+                pl.BlockSpec((dests * rows, step), lambda k, n, s: (0, n)),
+                pl.BlockSpec((dests * rows, 1), lambda k, n, s: (0, 0)),
+                pl.BlockSpec((1, width), lambda k, n, s: (0, 0)),
                 *[pl.BlockSpec(memory_space=pl.ANY) for _ in given],
             ],
-            out_specs=pl.BlockSpec((1, 2, 1, lats, lon), lambda k, s: (chunk, 0, k, 0, 0)),
+            out_specs=pl.BlockSpec((2, lats, step), lambda k, n, s: (pair + k, 0, n)),
             scratch_shapes=[pltpu.VMEM((width, dests * rows), BF)],
         ),
-        out_shape=jax.ShapeDtypeStruct((chunks, 2, pairs, lats, lon), F32),
+        out_shape=jax.ShapeDtypeStruct(shape, F32),
         input_output_aliases={5: 0} if given else {},
-        compiler_params=pltpu.CompilerParams(vmem_limit_bytes=INVERSE_VMEM_BYTES),
+        compiler_params=pltpu.CompilerParams(vmem_limit_bytes=VMEM_BYTES),
         cost_estimate=pl.CostEstimate(
             flops=2 * dests * rows * wide * lon,
             bytes_accessed=wide * (4 * lon + 2 * dests * rows),
             transcendentals=0,
         ),
         name="inverse_dft",
-    )(starts, back, angles, wave_row, modes[:, :width], *given)
+    )(starts, back, angles, wave_row, modes, *given)
 
 
 def legendre_kernel(
@@ -195,6 +204,7 @@
     fld_count,
     lats,
     half_cols,
+    pairs,
     arrived,
     low,
     h0,
@@ -217,7 +227,6 @@
     pair = pl.program_id(1)
     blocks = lat_count // 2
     width = 2 * lats
-    pairs = arrived.shape[2] // width
     slot_rows = 2 * fld_count * pairs
     lower = lax.broadcasted_iota(jnp.int32, (GROUP * slot_rows, LANES), 1) < HALF
     flip_tile = mirror[0]
@@ -297,7 +306,12 @@
                 for r in range(2):
                     at = (f * 2 + r) * pairs
                     both = jnp.concatenate(
-                        [value[at : at + pairs], value[slot_rows + at : slot_rows + at + pairs]], 0
+                        [
+                            value[half * slot_rows + at + k : half * slot_rows + at + k + 1]
+                            for k in range(pairs)
+                            for half in range(2)
+                        ],
+                        0,
                     )
                     spectra[f, r, local, :, c * half_cols : c * half_cols + cols] = both
                     if cols < half_cols:
@@ -352,13 +366,14 @@
                         ]
 
 
-def legendre_step(arrived, tables, own_waves, damp_rates, gauss_weight, lat_count, fld_count):
+def legendre_step(
+    arrived, position, pairs, tables, own_waves, damp_rates, gauss_weight, lat_count, fld_count
+):
     slots, half_lats, columns = tables.shape
     half_cols = columns // 2
-    sources, _, wide = arrived.shape
+    sources, travel_rows, _ = arrived.shape
     lats = 2 * half_lats // lat_count
-    width = 2 * lats
-    pairs = wide // width
+    wide = 2 * lats * pairs
     slot_rows = 2 * fld_count * pairs
     rows = 2 * slot_rows
     blocks = lat_count // 2
@@ -370,9 +385,8 @@
     ratio = (degree * (degree + 1)).astype(F32) / float(LMAX * (LMAX + 1))
     degree4 = jnp.where(degree <= LMAX, ratio**4, -1.0)[:, None, :]
 
-    by_field = damp_rates.reshape(fld_count, 2, pairs)
     rates = jnp.broadcast_to(
-        by_field.transpose(1, 0, 2)[:, :, None, :], (2, fld_count, 2, pairs)
+        damp_rates.transpose(2, 0, 1)[:, :, None, :], (2, fld_count, 2, pairs)
     ).reshape(rows, 1)
     w = gauss_weight.reshape(blocks, lats)
     weights = jnp.concatenate([w, w[:, 256:]], 1)
@@ -403,10 +417,10 @@
     scratch = pltpu.VMEM((GROUP, rows, half_lats), BF)
     flops = 2 * 2 * slots * rows * half_lats * columns
     return pl.pallas_call(
-        functools.partial(legendre_kernel, lat_count, fld_count, lats, half_cols),
+        functools.partial(legendre_kernel, lat_count, fld_count, lats, half_cols, pairs),
         grid=(groups, inner),
         in_specs=[
-            pl.BlockSpec((sources, 2 * GROUP, wide), lambda g, p: (0, g, 0)),
+            pl.BlockSpec((sources, 2 * GROUP, wide), lambda g, p: (0, g, position // pairs)),
             pl.BlockSpec((1, half_lats, columns), lambda g, p: (slot_of(g, p), 0, 0)),
             *narrow,
             pl.BlockSpec((2, 1, columns), lambda g, p: (g * inner + p, 0, 0)),
@@ -424,7 +438,7 @@
         ],
         out_shape=[
             jax.ShapeDtypeStruct((fld_count, 2, slots, 2 * pairs, columns), F32),
-            jax.ShapeDtypeStruct(arrived.shape, BF),
+            jax.ShapeDtypeStruct((sources, travel_rows, wide), BF),
         ],
         scratch_shapes=[scratch] * 4,
         compiler_params=pltpu.CompilerParams(vmem_limit_bytes=VMEM_BYTES),
@@ -449,43 +463,58 @@
     flipped = jnp.concatenate([lat_modes[192:], lat_modes[64:192], lat_modes[:64]])
     ordered = jnp.where(southern, flipped, lat_modes)
     modes = jnp.concatenate([ordered[:256], ordered[:256], ordered[256:], ordered[256:]])[None, :]
-    modes = jnp.tile(modes, (1, fields // CHUNKS // 2))
     wave_row = jnp.repeat(wave_slot, 2)[:, None]
     own_waves = lax.dynamic_slice_in_dim(wave_slot, owner * owned, owned)
-    rates = diffusion.reshape(fld_count, CHUNKS, fields // CHUNKS)
+    rates = diffusion.reshape(fld_count, fields // 2, 2)
 
     def exchange(x):
         return lax.all_to_all(x, ("lat", "fld"), 0, 0, tiled=True)
 
     angles = angle_rows(wave_row, lon)
     arrived = [
-        exchange(dft(grid_in, angles, wave_row, modes, starts, owners, c, CHUNKS))
-        for c in range(CHUNKS)
+        exchange(dft(grid_in, angles, wave_row, modes, starts, owners, pairs)) for pairs in OUTWARD
     ]
     parts, back = [], []
-    for c in range(CHUNKS):
+    for i, pairs in enumerate(RETURN):
+        pair, count = pairs[0], len(pairs)
+        source = next(j for j, out in enumerate(OUTWARD) if pair in out)
+        values = arrived[source]
+        if i >= 2:
+            values, back[i - 2] = lax.optimization_barrier((values, back[i - 2]))
         part, leaving = legendre_step(
-            arrived[c], legendre, own_waves, rates[:, c], gauss_weight, lat_count, fld_count
+            values,
+            OUTWARD[source].index(pair),
+            count,
+            legendre,
+            own_waves,
+            rates[:, pair : pair + count],
+            gauss_weight,
+            lat_count,
+            fld_count,
         )
-        if parts:
-            places, blocks = zip(*parts[-1])
+        parts.append(share_spectra(part))
+        for waiting in parts[i - 1 : i + 1] if i == len(RETURN) - 1 else parts[i - 1 : i]:
+            blocks = [block for _, block in waiting]
             leaving, blocks = lax.optimization_barrier((leaving, blocks))
-            parts[-1] = list(zip(places, blocks))
+            waiting[:] = [(at, block) for (at, _), block in zip(waiting, blocks)]
         back.append(exchange(leaving))
-        parts.append(share_spectra(part))
     whole = None
     columns = legendre.shape[2]
     spectra = jnp.zeros((2, fld_count, owned, fields, columns), F32)
-    for c in range(CHUNKS):
-        whole = inverse_dft(back[c], angles, wave_row, modes, starts, lats, whole, c, CHUNKS)
-        if c == 0:
+    for i, pairs in enumerate(RETURN):
+        if i == len(RETURN) - 1:
             whole, spectra = lax.optimization_barrier((whole, spectra))
-    for c in range(CHUNKS):
-        for at, block in parts[c]:
-            spectra = lax.dynamic_update_slice(
-                spectra, block[:, None], (0, at, 0, c * (fields // CHUNKS), 0)
-            )
-    return (whole.reshape(fields, lats, lon), spectra.reshape(2, -1, fields, columns))
+            spectra = assemble(spectra, parts)
+            back[i], spectra = lax.optimization_barrier((back[i], spectra))
+        whole = inverse_dft(back[i], angles, wave_row, modes, starts, grid_in.shape, whole, pairs[0])
+    return (whole, spectra.reshape(2, -1, fields, columns))
+
+
+def assemble(spectra, parts):
+    for pairs, blocks in zip(RETURN, parts):
+        for at, block in blocks:
+            spectra = lax.dynamic_update_slice(spectra, block[:, None], (0, at, 0, 2 * pairs[0], 0))
+    return spectra
 
 
 def share_spectra(part):
@@ -619,10 +648,10 @@
     fits = (
         lats == 2 * LANES + HALF
         and lat_count % 4 == 0
-        and fields % (2 * CHUNKS) == 0
+        and fields == 2 * sum(map(len, OUTWARD))
         and lat_count * lax.axis_size("fld") % 8 == 0
         and slots % GROUP == 0
-        and lon % LANES == 0 and lon % 4 == 0
+        and lon % (3 * LANES) == 0
         and columns == 6 * LANES
     )
     chosen = fast_body if fits else general_body

time: 431 us -> 426 us (0.988)
  waiting for transfers between devices: 227 us -> 171 us
  Pallas kernels: 150 us -> 182 us
  local copies, waits for them, and re-layouts: 20.2 us -> 33.5 us
  starting transfers between devices: 28.4 us -> 32.9 us
    all_to_all x4 -> x5, waiting for transfers between devices: 174 us -> 141 us  [exchange(): return lax.all_to_all(x, ('lat', 'fld'), 0, 0, tiled=True)]
    pallas_call x2 -> x3, Pallas kernels: 62.2 us -> 89.2 us  [legendre_step(): pl.pallas_call(functools.partial(legendre_kernel, lat_count, fld_count, l...]
    ppermute x6 -> x9, waiting for transfers between devices: 53.8 us -> 29.7 us  [share_spectra(): block = lax.ppermute(block, 'fld', ring)]
    pallas_call x2 -> x3, Pallas kernels: 41.4 us -> 47.1 us  [inverse_dft(): pl.pallas_call(inverse_kernel, grid_spec=pltpu.PrefetchScalarGridSpec(num...]
    dynamic_update_slice x8 -> x12, local copies, waits for them, and re-layouts: 8.94 us -> 14.3 us  [assemble(): lax.dynamic_update_slice(spectra, block[:, None], (0, at, 0, 2 * pairs[0]...]
    all_to_all x4 -> x5, starting transfers between devices: 22 us -> 26 us  [exchange(): return lax.all_to_all(x, ('lat', 'fld'), 0, 0, tiled=True)]
  transfers between devices with their start and end apart: 10 -> 14, of which waited for: 10 -> 10; matrix products, arithmetic and copies ran while one was open for 4% -> 7% of each run, Pallas kernels for 24% -> 35%
where the time goes in v4:
time: 426 us; the launch traced here: 425 us
  Pallas kernels  182 us (43%)
  waiting for transfers between devices  171 us (40%)
  local copies, waits for them, and re-layouts  33.5 us (8%)
  starting transfers between devices  32.9 us (8%)
  other arithmetic  4.98 us (1%)
    all_to_all x5, waiting for transfers between devices, exchange(): return lax.all_to_all(x, ('lat', 'fld'), 0, 0, tiled=True)  141 us
    pallas_call x3, Pallas kernels, legendre_step(): pl.pallas_call(functools.partial(legendre_kernel, lat_count, fld_count, l...  89.2 us
    pallas_call x3, Pallas kernels, inverse_dft(): pl.pallas_call(inverse_kernel, grid_spec=pltpu.PrefetchScalarGridSpec(num...  47.1 us
    pallas_call x2, Pallas kernels, dft(): pl.pallas_call(functools.partial(dft_kernel, count), grid_spec=pltpu.Pref...  37.6 us
    ppermute x9, waiting for transfers between devices, share_spectra(): block = lax.ppermute(block, 'fld', ring)  29.7 us
    all_to_all x5, starting transfers between devices, exchange(): return lax.all_to_all(x, ('lat', 'fld'), 0, 0, tiled=True)  26 us
    dynamic_update_slice x12, local copies, waits for them, and re-layouts, assemble(): lax.dynamic_update_slice(spectra, block[:, None], (0, at, 0, 2 * pairs[0]...  14.3 us
  transfers between devices with their start and end apart: 14, of which 10 were waited for; matrix products, arithmetic and copies ran while one was open for 7% of the time, Pallas kernels for 35%

profile of v4, /device:TPU:0, one launch (start us, length us, event | category | flops | bytes accessed | tf_op | source)
XLA Modules:
  0.0 425.2 jit_solution(4201239151363018048)
XLA Ops:
  0.6 0.7 slice.34
  1.3 0.8 fusion.22
  2.1 0.7 add_select_fusion.2
  2.9 0.5 broadcast_select_fusion.starts
  3.4 0.8 broadcast_in_dim.50
  4.3 1.1 broadcast_in_dim_reshape.4.wave_row.refs_7_.refs_3_
  5.4 8.3 %angles.1.refs_6_.refs_2_ = bf16[1536,2688]{1,0:T(8,128)(2,1)} custom-call(s32[1536,1]{1,0:T(8,128)} %broadcast_in_dim_reshape.4.wave_row.refs_7_.refs_3_), custom_call_target="tpu_custom_call" | custom-call | flops 16515072 | bytes 8257536 | tf_op jit(solution)/shard_map/angles/pallas_call | solution.py:77
  13.8 0.6 broadcast_in_dim.51.refs_4_.modes
  14.4 11.8 %dft.3 = bf16[32,48,640]{2,1,0:T(8,128)(2,1)} custom-call(s32[3]{0:T(128)} %broadcast_select_fusion.starts, bf16[8,320,2688]{2,1,0:T(8,128)(2,1)} %refs_1_.3, bf16[8,320,2688]{2,1,0:T(8,128)(2,1)} %refs_1_.3, bf16[1536,2688]{1,0:T(8,128)(2,1)} %angles.1.refs_6_.refs_2_, s32[1536,1]{1,0:T(8,128)} %broadcast_in_dim_reshape.4.wave_row.refs_7_.refs_3_, ...), custom_call_target="tpu_custom_call" | custom-call | flops 5284823040 | bytes 5406720 | tf_op jit(solution)/shard_map/dft/pallas_call | solution.py:118
  26.2 7.3 %all-to-all-start.1 = ((bf16[32,48,640]{2,1,0:T(8,128)(2,1)}), bf16[32,48,640]{2,1,0:T(8,128)(2,1)S(1)}, u32[]{:S(2)}, u32[]{:S(2)}) async-start(bf16[32,48,640]{2,1,0:T(8,128)(2,1)} %dft.3), calls=%async_computation.1 | async-start | bytes 3932160 | tf_op jit(solution)/shard_map/all_to_all | solution.py:471
  33.5 0.6 copy.43
  34.1 25.7 %dft.2 = bf16[32,48,1920]{2,1,0:T(8,128)(2,1)} custom-call(s32[3]{0:T(128)} %broadcast_select_fusion.starts, bf16[8,320,2688]{2,1,0:T(8,128)(2,1)} %refs_1_.3, bf16[8,320,2688]{2,1,0:T(8,128)(2,1)} %refs_1_.3, bf16[8,320,2688]{2,1,0:T(8,128)(2,1)} %refs_1_.3, bf16[8,320,2688]{2,1,0:T(8,128)(2,1)} %refs_1_.3, bf16[8,320,2688]{2,1,0:T(8,128)(2,1)} %refs_1_.3, ...), custom_call_target="tpu_custom_call" | custom-call | flops 15854469120 | bytes 16220160 | tf_op jit(solution)/shard_map/dft/pallas_call | solution.py:118
  59.9 19.5 %all-to-all-done.1.arrived = bf16[32,48,640]{2,1,0:T(8,128)(2,1)S(1)} async-done(((bf16[32,48,640]{2,1,0:T(8,128)(2,1)}), bf16[32,48,640]{2,1,0:T(8,128)(2,1)S(1)}, u32[]{:S(2)}, u32[]{:S(2)}) %all-to-all-start.1) | async-done | bytes 1966112 | tf_op jit(solution)/shard_map/all_to_all | solution.py:471
  79.4 1.3 copy-done.2
  80.7 4.0 all-to-all-start
  84.7 0.8 dynamic_slice.41
  85.8 0.7 broadcast_in_dim.133.rates
  86.6 0.7 pad_maximum_fusion.weights
  87.4 0.6 add_convert_fusion.mirror
  88.0 0.7 fusion.14
  88.7 0.9 compare_select_fusion.degree4
  89.5 29.0 %legendre.3 = (f32[4,2,24,2,768]{4,3,2,1,0:T(2,128)}, bf16[32,48,640]{2,1,0:T(8,128)(2,1)}) custom-call(bf16[32,48,640]{2,1,0:T(8,128)(2,1)} %copy-done.2, bf16[24,1280,768]{2,1,0:T(8,128)(2,1)} %h3.5, bf16[24,1280,768]{2,1,0:T(8,128)(2,1)} %h3.5, bf16[24,1280,768]{2,1,0:T(8,128)(2,1)} %h3.5, bf16[24,1280,768]{2,1,0:T(8,128)(2,1)} %h3.5, ...), custom_call_target="tpu_custom_call" | custom-call | flops 1509949440 | bytes 47185920 | tf_op jit(solution)/shard_map/legendre/pallas_call | solution.py:419
  118.5 97.6 %all-to-all-done.arrived = bf16[32,48,1920]{2,1,0:T(8,128)(2,1)} async-done(((bf16[32,48,1920]{2,1,0:T(8,128)(2,1)}), bf16[32,48,1920]{2,1,0:T(8,128)(2,1)}, u32[]{:S(2)}, u32[]{:S(2)}) %all-to-all-start) | async-done | bytes 5898272 | tf_op jit(solution)/shard_map/all_to_all | solution.py:471
  216.2 5.5 %all-to-all-start.2 = ((bf16[32,48,640]{2,1,0:T(8,128)(2,1)}), bf16[32,48,640]{2,1,0:T(8,128)(2,1)S(1)}, u32[]{:S(2)}, u32[]{:S(2)}) async-start(bf16[32,48,640]{2,1,0:T(8,128)(2,1)} %get-tuple-element.29), calls=%async_computation.2 | async-start | bytes 3932160 | tf_op jit(solution)/shard_map/all_to_all | solution.py:471
  221.7 0.7 fusion.12
  222.4 1.1 dynamic-slice_bitcast_fusion.4
  223.8 1.6 collective-permute-start.7
  225.4 1.4 collective-permute-start.8
  226.9 0.7 reshape.548.rates
  227.6 31.2 %legendre.5 = (f32[4,2,24,4,768]{4,3,2,1,0:T(4,128)}, bf16[32,48,1280]{2,1,0:T(8,128)(2,1)}) custom-call(bf16[32,48,1920]{2,1,0:T(8,128)(2,1)} %all-to-all-done.arrived, bf16[24,1280,768]{2,1,0:T(8,128)(2,1)} %h3.5, bf16[24,1280,768]{2,1,0:T(8,128)(2,1)} %h3.5, bf16[24,1280,768]{2,1,0:T(8,128)(2,1)} %h3.5, bf16[24,1280,768]{2,1,0:T(8,128)(2,1)} %h3.5, ...), custom_call_target="tpu_custom_call" | custom-call | flops 3019898880 | bytes 47185920 | tf_op jit(solution)/shard_map/legendre/pallas_call | solution.py:419
  258.8 8.8 %all-to-all-done.2.back = bf16[32,48,640]{2,1,0:T(8,128)(2,1)S(1)} async-done(((bf16[32,48,640]{2,1,0:T(8,128)(2,1)}), bf16[32,48,640]{2,1,0:T(8,128)(2,1)S(1)}, u32[]{:S(2)}, u32[]{:S(2)}) %all-to-all-start.2) | async-done | bytes 1966112 | tf_op jit(solution)/shard_map/all_to_all | solution.py:471
  267.6 4.0 all-to-all-start.4
  271.6 3.0 dynamic-slice_bitcast_fusion
  275.0 0.7 broadcast_in_dim.134.rates
  275.7 1.6 collective-permute-start.1
  277.3 1.4 collective-permute-start.2
  278.7 29.0 %legendre.4 = (f32[4,2,24,2,768]{4,3,2,1,0:T(2,128)}, bf16[32,48,640]{2,1,0:T(8,128)(2,1)}) custom-call(bf16[32,48,1920]{2,1,0:T(8,128)(2,1)} %all-to-all-done.arrived, bf16[24,1280,768]{2,1,0:T(8,128)(2,1)} %h3.5, bf16[24,1280,768]{2,1,0:T(8,128)(2,1)} %h3.5, bf16[24,1280,768]{2,1,0:T(8,128)(2,1)} %h3.5, bf16[24,1280,768]{2,1,0:T(8,128)(2,1)} %h3.5, ...), custom_call_target="tpu_custom_call" | custom-call | flops 1509949440 | bytes 47185920 | tf_op jit(solution)/shard_map/legendre/pallas_call | solution.py:419
  307.7 1.7 dynamic-slice_bitcast_fusion.8
  309.4 0.4 collective-permute-start.4
  309.8 10.8 %collective-permute-done = f32[2,24,4,768]{3,2,1,0:T(4,128)S(1)} collective-permute-done((f32[2,24,4,768]{3,2,1,0:T(4,128)}, f32[2,24,4,768]{3,2,1,0:T(4,128)S(1)}, u32[]{:S(2)}, u32[]{:S(2)}) %collective-permute-start) | collective-permute-done | bytes 589856 | tf_op jit(solution)/shard_map/ppermute | solution.py:528
  320.6 12.8 %inverse_dft.3.refs_0_ = f32[8,320,2688]{2,1,0:T(8,128)} custom-call(s32[3]{0:T(128)} %broadcast_select_fusion.starts, bf16[32,48,640]{2,1,0:T(8,128)(2,1)} %copy-done, bf16[1536,2688]{1,0:T(8,128)(2,1)} %angles.1.refs_6_.refs_2_, s32[1536,1]{1,0:T(8,128)} %broadcast_in_dim_reshape.4.wave_row.refs_7_.refs_3_, s32[1,640]{1,0:T(1,128)} %broadcast_in_dim.51.refs_4_.modes), custom_call_target="tpu_custom_call" | custom-call | flops 5284823040 | bytes 8847360 | tf_op jit(solution)/shard_map/inverse_dft/pallas_call | solution.py:175
  333.4 1.6 collective-permute-done.2
  335.0 7.3 %collective-permute-done.3 = f32[2,24,2,768]{3,2,1,0:T(2,128)} collective-permute-done((f32[2,24,2,768]{3,2,1,0:T(2,128)S(1)}, f32[2,24,2,768]{3,2,1,0:T(2,128)}, u32[]{:S(2)}, u32[]{:S(2)}) %collective-permute-start.3) | collective-permute-done | bytes 294944 | tf_op jit(solution)/shard_map/ppermute | solution.py:528
  342.3 1.9 collective-permute-done.4
  344.2 8.1 %collective-permute-done.5 = f32[2,24,2,768]{3,2,1,0:T(2,128)} collective-permute-done((f32[2,24,2,768]{3,2,1,0:T(2,128)S(1)}, f32[2,24,2,768]{3,2,1,0:T(2,128)}, u32[]{:S(2)}, u32[]{:S(2)}) %collective-permute-start.5) | collective-permute-done | bytes 294944 | tf_op jit(solution)/shard_map/ppermute | solution.py:528
  352.3 7.9 %all-to-all-done.4.back = bf16[32,48,1280]{2,1,0:T(8,128)(2,1)} async-done(((bf16[32,48,1280]{2,1,0:T(8,128)(2,1)}), bf16[32,48,1280]{2,1,0:T(8,128)(2,1)}, u32[]{:S(2)}, u32[]{:S(2)}) %all-to-all-start.4) | async-done | bytes 3932192 | tf_op jit(solution)/shard_map/all_to_all | solution.py:471
  360.2 5.2 %all-to-all-start.3 = ((bf16[32,48,640]{2,1,0:T(8,128)(2,1)}), bf16[32,48,640]{2,1,0:T(8,128)(2,1)S(1)}, u32[]{:S(2)}, u32[]{:S(2)}) async-start(bf16[32,48,640]{2,1,0:T(8,128)(2,1)} %get-tuple-element.35), calls=%async_computation.3 | async-start | bytes 3932160 | tf_op jit(solution)/shard_map/all_to_all | solution.py:471
  365.4 21.5 %inverse_dft.4.refs_0_ = f32[8,320,2688]{2,1,0:T(8,128)} custom-call(s32[3]{0:T(128)} %broadcast_select_fusion.starts, bf16[32,48,1280]{2,1,0:T(8,128)(2,1)} %all-to-all-done.4.back, bf16[1536,2688]{1,0:T(8,128)(2,1)} %angles.1.refs_6_.refs_2_, s32[1536,1]{1,0:T(8,128)} %broadcast_in_dim_reshape.4.wave_row.refs_7_.refs_3_, ...), custom_call_target="tpu_custom_call", output_to_operand_aliasing={{}: (5, {})} | custom-call | flops 10569646080 | bytes 17694720 | tf_op jit(solution)/shard_map/inverse_dft/pallas_call | solution.py:175
  386.9 2.6 broadcast_in_dim.60
  389.5 0.7 bitcast_dynamic-update-slice_fusion.11
  390.3 0.7 bitcast_dynamic-update-slice_fusion.10
  391.0 0.7 bitcast_dynamic-update-slice_fusion.9
  391.8 0.7 bitcast_dynamic-update-slice_fusion.8
  392.5 0.9 bitcast_dynamic-update-slice_fusion.3
  393.4 0.9 bitcast_dynamic-update-slice_fusion.2
  394.2 1.9 bitcast_dynamic-update-slice_fusion.1
  396.1 1.9 bitcast_dynamic-update-slice_fusion
  398.1 0.7 bitcast_dynamic-update-slice_fusion.7
  398.8 1.7 bitcast_dynamic-update-slice_fusion.6
  400.5 1.7 bitcast_dynamic-update-slice_fusion.5
  402.2 1.7 bitcast_dynamic-update-slice_fusion.4
  403.9 7.2 %all-to-all-done.3.back = bf16[32,48,640]{2,1,0:T(8,128)(2,1)S(1)} async-done(((bf16[32,48,640]{2,1,0:T(8,128)(2,1)}), bf16[32,48,640]{2,1,0:T(8,128)(2,1)S(1)}, u32[]{:S(2)}, u32[]{:S(2)}) %all-to-all-start.3) | async-done | bytes 1966112 | tf_op jit(solution)/shard_map/all_to_all | solution.py:471
  411.1 1.3 copy-done.1
  412.4 12.8 %inverse_dft.5 = f32[8,320,2688]{2,1,0:T(8,128)} custom-call(s32[3]{0:T(128)} %broadcast_select_fusion.starts, bf16[32,48,640]{2,1,0:T(8,128)(2,1)} %copy-done.1, bf16[1536,2688]{1,0:T(8,128)(2,1)} %angles.1.refs_6_.refs_2_, s32[1536,1]{1,0:T(8,128)} %broadcast_in_dim_reshape.4.wave_row.refs_7_.refs_3_, ...), custom_call_target="tpu_custom_call", output_to_operand_aliasing={{}: (5, {})} | custom-call | flops 5284823040 | bytes 8847360 | tf_op jit(solution)/shard_map/inverse_dft/pallas_call | solution.py:175
  (52 shorter events, 1.4 us)
Async XLA Ops:
  26.2 53.2 %all-to-all-start.1 = ((bf16[32,48,640]{2,1,0:T(8,128)(2,1)}), bf16[32,48,640]{2,1,0:T(8,128)(2,1)S(1)}, u32[]{:S(2)}, u32[]{:S(2)}) async-start(bf16[32,48,640]{2,1,0:T(8,128)(2,1)} %dft.3), calls=%async_computation.1 | async-start | bytes 3932160 | tf_op jit(solution)/shard_map/all_to_all | solution.py:471
  59.9 25.6 %copy-start.12 = (f32[32]{0:T(128)S(1)}, f32[32]{0:T(128)}, u32[]{:S(2)}) copy-start(f32[32]{0:T(128)} %param.13) | copy-start | bytes 388
  59.9 26.6 %copy-start.11 = (f32[1280]{0:T(1024)S(1)}, f32[1280]{0:T(1024)}, u32[]{:S(2)}) copy-start(f32[1280]{0:T(1024)} %param.12) | copy-start | bytes 15364
  79.4 1.3 copy-start.2
  80.7 135.5 %all-to-all-start = ((bf16[32,48,1920]{2,1,0:T(8,128)(2,1)}), bf16[32,48,1920]{2,1,0:T(8,128)(2,1)}, u32[]{:S(2)}, u32[]{:S(2)}) async-start(bf16[32,48,1920]{2,1,0:T(8,128)(2,1)} %dft.2), calls=%async_computation | async-start | bytes 11796480 | tf_op jit(solution)/shard_map/all_to_all | solution.py:471
  118.5 103.9 %copy-start.3 = (f32[4,2,24,2,768]{4,3,2,1,0:T(2,128)S(1)}, f32[4,2,24,2,768]{4,3,2,1,0:T(2,128)}, u32[]{:S(2)}) copy-start(f32[4,2,24,2,768]{4,3,2,1,0:T(2,128)} %get-tuple-element.37) | copy-start | bytes 3538948
  216.2 51.4 %all-to-all-start.2 = ((bf16[32,48,640]{2,1,0:T(8,128)(2,1)}), bf16[32,48,640]{2,1,0:T(8,128)(2,1)S(1)}, u32[]{:S(2)}, u32[]{:S(2)}) async-start(bf16[32,48,640]{2,1,0:T(8,128)(2,1)} %get-tuple-element.29), calls=%async_computation.2 | async-start | bytes 3932160 | tf_op jit(solution)/shard_map/all_to_all | solution.py:471
  223.6 35.2 %collective-permute-start.6 = (f32[2,24,2,768]{3,2,1,0:T(2,128)}, f32[2,24,2,768]{3,2,1,0:T(2,128)S(1)}, u32[]{:S(2)}, u32[]{:S(2)}) collective-permute-start(f32[2,24,2,768]{3,2,1,0:T(2,128)} %get-tuple-element.62), channel_id=1, source_target_pairs={{0,1},{1,2},{2,3},{3,0},{4,5},{5,6},{6,7},{7,4},{8,9},{9,10},{10,1... | collective-permute-start | bytes 884744 | tf_op jit(solution)/shard_map/ppermute | solution.py:528
  223.8 35.0 %collective-permute-start.7 = (f32[2,24,2,768]{3,2,1,0:T(2,128)}, f32[2,24,2,768]{3,2,1,0:T(2,128)S(1)}, u32[]{:S(2)}, u32[]{:S(2)}) collective-permute-start(f32[2,24,2,768]{3,2,1,0:T(2,128)} %get-tuple-element.61), channel_id=1, source_target_pairs={{0,2},{1,3},{2,0},{3,1},{4,6},{5,7},{6,4},{7,5},{8,10},{9,11},{10,... | collective-permute-start | bytes 884744 | tf_op jit(solution)/shard_map/ppermute | solution.py:528
  225.4 33.3 %collective-permute-start.8 = (f32[2,24,2,768]{3,2,1,0:T(2,128)S(1)}, f32[2,24,2,768]{3,2,1,0:T(2,128)S(1)}, u32[]{:S(2)}, u32[]{:S(2)}) collective-permute-start(f32[2,24,2,768]{3,2,1,0:T(2,128)S(1)} %get-tuple-element.60), channel_id=1, source_target_pairs={{0,3},{1,0},{2,1},{3,2},{4,7},{5,4},{6,5},{7,6},{8,11},{9,8},{10,9... | collective-permute-start | bytes 884744 | tf_op jit(solution)/shard_map/ppermute | solution.py:528
  258.8 12.9 %copy-start.5 = (f32[2,24,2,768]{3,2,1,0:T(2,128)}, f32[2,24,2,768]{3,2,1,0:T(2,128)S(1)}, u32[]{:S(2)}) copy-start(f32[2,24,2,768]{3,2,1,0:T(2,128)S(1)} %collective-permute-done.6) | copy-start | bytes 884740
  258.8 12.9 %copy-start.7 = (f32[2,24,2,768]{3,2,1,0:T(2,128)}, f32[2,24,2,768]{3,2,1,0:T(2,128)S(1)}, u32[]{:S(2)}) copy-start(f32[2,24,2,768]{3,2,1,0:T(2,128)S(1)} %collective-permute-done.7) | copy-start | bytes 884740
  258.8 15.9 %copy-start.9 = (f32[2,24,2,768]{3,2,1,0:T(2,128)}, f32[2,24,2,768]{3,2,1,0:T(2,128)S(1)}, u32[]{:S(2)}) copy-start(f32[2,24,2,768]{3,2,1,0:T(2,128)S(1)} %collective-permute-done.8) | copy-start | bytes 884740
  267.6 7.1 %copy-start = (bf16[32,48,640]{2,1,0:T(8,128)(2,1)}, bf16[32,48,640]{2,1,0:T(8,128)(2,1)S(1)}, u32[]{:S(2)}) copy-start(bf16[32,48,640]{2,1,0:T(8,128)(2,1)S(1)} %all-to-all-done.2.back) | copy-start | bytes 5898244
  267.6 92.7 %all-to-all-start.4 = ((bf16[32,48,1280]{2,1,0:T(8,128)(2,1)}), bf16[32,48,1280]{2,1,0:T(8,128)(2,1)}, u32[]{:S(2)}, u32[]{:S(2)}) async-start(bf16[32,48,1280]{2,1,0:T(8,128)(2,1)} %get-tuple-element.38), calls=%async_computation.4 | async-start | bytes 7864320 | tf_op jit(solution)/shard_map/all_to_all | solution.py:471
  274.7 45.9 %collective-permute-start = (f32[2,24,4,768]{3,2,1,0:T(4,128)}, f32[2,24,4,768]{3,2,1,0:T(4,128)S(1)}, u32[]{:S(2)}, u32[]{:S(2)}) collective-permute-start(f32[2,24,4,768]{3,2,1,0:T(4,128)} %get-tuple-element.58), channel_id=1, source_target_pairs={{0,1},{1,2},{2,3},{3,0},{4,5},{5,6},{6,7},{7,4},{8,9},{9,10},{10,1... | collective-permute-start | bytes 1769480 | tf_op jit(solution)/shard_map/ppermute | solution.py:528
  275.7 57.7 %collective-permute-start.1 = (f32[2,24,4,768]{3,2,1,0:T(4,128)}, f32[2,24,4,768]{3,2,1,0:T(4,128)}, u32[]{:S(2)}, u32[]{:S(2)}) collective-permute-start(f32[2,24,4,768]{3,2,1,0:T(4,128)} %get-tuple-element.57), channel_id=1, source_target_pairs={{0,2},{1,3},{2,0},{3,1},{4,6},{5,7},{6,4},{7,5},{8,10},{9,11},{10,... | collective-permute-start | bytes 1769480 | tf_op jit(solution)/shard_map/ppermute | solution.py:528
  277.3 57.7 %collective-permute-start.2 = (f32[2,24,4,768]{3,2,1,0:T(4,128)}, f32[2,24,4,768]{3,2,1,0:T(4,128)}, u32[]{:S(2)}, u32[]{:S(2)}) collective-permute-start(f32[2,24,4,768]{3,2,1,0:T(4,128)} %get-tuple-element.56), channel_id=1, source_target_pairs={{0,3},{1,0},{2,1},{3,2},{4,7},{5,4},{6,5},{7,6},{8,11},{9,8},{10,9... | collective-permute-start | bytes 1769480 | tf_op jit(solution)/shard_map/ppermute | solution.py:528
  309.4 32.9 %collective-permute-start.3 = (f32[2,24,2,768]{3,2,1,0:T(2,128)S(1)}, f32[2,24,2,768]{3,2,1,0:T(2,128)}, u32[]{:S(2)}, u32[]{:S(2)}) collective-permute-start(f32[2,24,2,768]{3,2,1,0:T(2,128)S(1)} %get-tuple-element.66), channel_id=1, source_target_pairs={{0,1},{1,2},{2,3},{3,0},{4,5},{5,6},{6,7},{7,4},{8,9},{9,10},{10,1... | collective-permute-start | bytes 884744 | tf_op jit(solution)/shard_map/ppermute | solution.py:528
  309.4 34.8 %collective-permute-start.4 = (f32[2,24,2,768]{3,2,1,0:T(2,128)S(1)}, f32[2,24,2,768]{3,2,1,0:T(2,128)}, u32[]{:S(2)}, u32[]{:S(2)}) collective-permute-start(f32[2,24,2,768]{3,2,1,0:T(2,128)S(1)} %get-tuple-element.65), channel_id=1, source_target_pairs={{0,2},{1,3},{2,0},{3,1},{4,6},{5,7},{6,4},{7,5},{8,10},{9,11},{10,... | collective-permute-start | bytes 884744 | tf_op jit(solution)/shard_map/ppermute | solution.py:528
  320.6 31.7 %collective-permute-start.5 = (f32[2,24,2,768]{3,2,1,0:T(2,128)S(1)}, f32[2,24,2,768]{3,2,1,0:T(2,128)}, u32[]{:S(2)}, u32[]{:S(2)}) collective-permute-start(f32[2,24,2,768]{3,2,1,0:T(2,128)S(1)} %get-tuple-element.64), channel_id=1, source_target_pairs={{0,3},{1,0},{2,1},{3,2},{4,7},{5,4},{6,5},{7,6},{8,11},{9,8},{10,9... | collective-permute-start | bytes 884744 | tf_op jit(solution)/shard_map/ppermute | solution.py:528
  360.2 50.9 %all-to-all-start.3 = ((bf16[32,48,640]{2,1,0:T(8,128)(2,1)}), bf16[32,48,640]{2,1,0:T(8,128)(2,1)S(1)}, u32[]{:S(2)}, u32[]{:S(2)}) async-start(bf16[32,48,640]{2,1,0:T(8,128)(2,1)} %get-tuple-element.35), calls=%async_computation.3 | async-start | bytes 3932160 | tf_op jit(solution)/shard_map/all_to_all | solution.py:471
  386.9 2.6 copy-start.4
  386.9 3.4 copy-start.6
  386.9 4.1 copy-start.8
  386.9 4.8 %copy-start.10 = (f32[2,24,2,768]{3,2,1,0:T(2,128)S(1)}, f32[2,24,2,768]{3,2,1,0:T(2,128)}, u32[]{:S(2)}) copy-start(f32[2,24,2,768]{3,2,1,0:T(2,128)} %copy-done.9) | copy-start | bytes 884740
  411.1 1.3 copy-start.1

commit v5 on v4

--- a/solution.py
+++ b/solution.py
@@ -16,7 +16,7 @@
 RETURN = ((2,), (0, 1), (3,))
 BF = jnp.bfloat16
 F32 = jnp.float32
-VMEM_BYTES = 60 * 1024 * 1024
+VMEM_BYTES = 66_000_000
 
 
 def dot(a, b):
@@ -39,7 +39,7 @@
 
 def angle_kernel(lon, wave_row, out):
     rows = out.shape[0]
-    step = 64
+    step = 128
     scale = 1.0 / math.sqrt(lon)
     tiles = lon // LANES
     middle = tiles // 2
@@ -71,25 +71,13 @@
             put(a, value)
 
 
-def angle_rows(wave_row, lon):
-    rows = wave_row.shape[0]
-    step = 256
-    return pl.pallas_call(
-        functools.partial(angle_kernel, lon),
-        grid=(rows // step,),
-        in_specs=[pl.BlockSpec((step, 1), lambda i: (i, 0))],
-        out_specs=pl.BlockSpec((step, lon), lambda i: (i, 0)),
-        out_shape=jax.ShapeDtypeStruct((rows, lon), BF),
-        cost_estimate=pl.CostEstimate(
-            flops=4 * rows * lon, bytes_accessed=2 * rows * lon, transcendentals=0
-        ),
-        name="angles",
-    )(wave_row)
-
-
-def dft_kernel(count, starts, *refs):
+def dft_kernel(count, makes_angles, starts, *refs):
     fields = refs[:count]
-    angles, wave_row, modes, out, arranged = refs[count:]
+    if makes_angles:
+        wave_row, modes, out, angles, arranged = refs[count:]
+        angle_kernel(arranged.shape[1], wave_row, angles)
+    else:
+        wave_row, modes, angles, out, arranged = refs[count:]
     width = out.shape[2] // (count // 2)
 
     @pl.when(pl.program_id(0) == 0)
@@ -111,12 +99,16 @@
 def dft(grid_in, angles, wave_row, modes, starts, dests, pairs):
     _, lats, lon = grid_in.shape
     count = 2 * len(pairs)
-    rows = angles.shape[0]
+    rows = wave_row.shape[0]
     wide = count * lats
     per = dests // 4
     tile = rows * per // dests
+    makes_angles = angles is None
+    angle_spec = pl.BlockSpec((tile, lon), lambda i, s: (i, 0))
+    out_spec = pl.BlockSpec((per, rows // dests, wide), lambda i, s: (i, 0, 0))
+    out_shape = jax.ShapeDtypeStruct((dests, rows // dests, wide), BF)
     return pl.pallas_call(
-        functools.partial(dft_kernel, count),
+        functools.partial(dft_kernel, count, makes_angles),
         grid_spec=pltpu.PrefetchScalarGridSpec(
             num_scalar_prefetch=1,
             grid=(dests // per,),
@@ -128,20 +120,26 @@
                     for pair in pairs
                     for half in range(2)
                 ],
-                pl.BlockSpec((tile, lon), lambda i, s: (i, 0)),
                 pl.BlockSpec((tile, 1), lambda i, s: (i, 0)),
                 pl.BlockSpec((1, wide), lambda i, s: (0, 0)),
+                *([] if makes_angles else [angle_spec]),
             ],
-            out_specs=pl.BlockSpec((per, rows // dests, wide), lambda i, s: (i, 0, 0)),
+            out_specs=[out_spec, angle_spec] if makes_angles else out_spec,
             scratch_shapes=[pltpu.VMEM((wide, lon), BF)],
         ),
-        out_shape=jax.ShapeDtypeStruct((dests, rows // dests, wide), BF),
+        out_shape=[out_shape, jax.ShapeDtypeStruct((rows, lon), BF)] if makes_angles else out_shape,
         compiler_params=pltpu.CompilerParams(vmem_limit_bytes=VMEM_BYTES),
         cost_estimate=pl.CostEstimate(
             flops=2 * rows * wide * lon, bytes_accessed=2 * wide * (lon + rows), transcendentals=0
         ),
         name="dft",
-    )(starts, *[grid_in] * count, angles, wave_row, jnp.tile(modes, (1, len(pairs))))
+    )(
+        starts,
+        *[grid_in] * count,
+        wave_row,
+        jnp.tile(modes, (1, len(pairs))),
+        *([] if makes_angles else [angles]),
+    )
 
 
 def inverse_kernel(starts, back, angles, wave_row, modes, *refs):
@@ -470,10 +468,10 @@
     def exchange(x):
         return lax.all_to_all(x, ("lat", "fld"), 0, 0, tiled=True)
 
-    angles = angle_rows(wave_row, lon)
-    arrived = [
-        exchange(dft(grid_in, angles, wave_row, modes, starts, owners, pairs)) for pairs in OUTWARD
-    ]
+    sent, angles = dft(grid_in, None, wave_row, modes, starts, owners, OUTWARD[0])
+    arrived = [exchange(sent)]
+    for pairs in OUTWARD[1:]:
+        arrived.append(exchange(dft(grid_in, angles, wave_row, modes, starts, owners, pairs)))
     parts, back = [], []
     for i, pairs in enumerate(RETURN):
         pair, count = pairs[0], len(pairs)

time: 426 us -> 420 us (0.986)
    pallas_call x3 -> x2, Pallas kernels: 45.9 us -> 42.4 us  [dft(): pl.pallas_call(functools.partial(dft_kernel, count, makes_angles), grid_s...]
  transfers between devices with their start and end apart: 14 -> 14, of which waited for: 10 -> 10; matrix products, arithmetic and copies ran while one was open for 7% -> 7% of each run, Pallas kernels for 35% -> 36%
where the time goes in v5:
time: 420 us; the launch traced here: 419 us
  Pallas kernels  179 us (43%)
  waiting for transfers between devices  171 us (41%)
  starting transfers between devices  33.1 us (8%)
  local copies, waits for them, and re-layouts  31.2 us (7%)
  other arithmetic  5.04 us (1%)
    all_to_all x5, waiting for transfers between devices, exchange(): return lax.all_to_all(x, ('lat', 'fld'), 0, 0, tiled=True)  140 us
    pallas_call x3, Pallas kernels, legendre_step(): pl.pallas_call(functools.partial(legendre_kernel, lat_count, fld_count, l...  89.2 us
    pallas_call x3, Pallas kernels, inverse_dft(): pl.pallas_call(inverse_kernel, grid_spec=pltpu.PrefetchScalarGridSpec(num...  47.1 us
    pallas_call x2, Pallas kernels, dft(): pl.pallas_call(functools.partial(dft_kernel, count, makes_angles), grid_s...  42.4 us
    ppermute x9, waiting for transfers between devices, share_spectra(): block = lax.ppermute(block, 'fld', ring)  30.8 us
    all_to_all x5, starting transfers between devices, exchange(): return lax.all_to_all(x, ('lat', 'fld'), 0, 0, tiled=True)  26.4 us
    dynamic_update_slice x12, local copies, waits for them, and re-layouts, assemble(): lax.dynamic_update_slice(spectra, block[:, None], (0, at, 0, 2 * pairs[0]...  15.4 us
  transfers between devices with their start and end apart: 14, of which 10 were waited for; matrix products, arithmetic and copies ran while one was open for 7% of the time, Pallas kernels for 36%

profile of v5, /device:TPU:0, one launch (start us, length us, event | category | flops | bytes accessed | tf_op | source)
XLA Modules:
  0.0 419.4 jit_solution(5154789131000415364)
XLA Ops:
  0.6 0.7 slice.34
  1.3 0.8 fusion.22
  2.1 0.7 add_select_fusion.2
  2.9 0.6 broadcast_select_fusion.starts
  3.5 0.8 broadcast_in_dim.50
  4.3 1.1 broadcast_in_dim_reshape.4.refs_2_.refs_6_.wave_row
  5.5 0.6 broadcast_in_dim.51.refs_3_.modes
  6.1 16.6 %dft.2 = (bf16[32,48,640]{2,1,0:T(8,128)(2,1)}, bf16[1536,2688]{1,0:T(8,128)(2,1)}) custom-call(s32[3]{0:T(128)} %broadcast_select_fusion.starts, bf16[8,320,2688]{2,1,0:T(8,128)(2,1)} %refs_5_.1, bf16[8,320,2688]{2,1,0:T(8,128)(2,1)} %refs_5_.1, s32[1536,1]{1,0:T(8,128)} %broadcast_in_dim_reshape.4.refs_2_.refs_6_.wave_row, ...), custom_call_target="tpu_custom_call" | custom-call | flops 5284823040 | bytes 5406720 | tf_op jit(solution)/shard_map/dft/pallas_call | solution.py:110
  22.6 7.4 %all-to-all-start.1 = ((bf16[32,48,640]{2,1,0:T(8,128)(2,1)}), bf16[32,48,640]{2,1,0:T(8,128)(2,1)}, u32[]{:S(2)}, u32[]{:S(2)}) async-start(bf16[32,48,640]{2,1,0:T(8,128)(2,1)} %get-tuple-element.32), calls=%async_computation.1 | async-start | bytes 3932160 | tf_op jit(solution)/shard_map/all_to_all | solution.py:469
  30.1 0.6 copy.41
  30.7 25.8 %dft.3 = bf16[32,48,1920]{2,1,0:T(8,128)(2,1)} custom-call(s32[3]{0:T(128)} %broadcast_select_fusion.starts, bf16[8,320,2688]{2,1,0:T(8,128)(2,1)} %refs_5_.1, bf16[8,320,2688]{2,1,0:T(8,128)(2,1)} %refs_5_.1, bf16[8,320,2688]{2,1,0:T(8,128)(2,1)} %refs_5_.1, bf16[8,320,2688]{2,1,0:T(8,128)(2,1)} %refs_5_.1, bf16[8,320,2688]{2,1,0:T(8,128)(2,1)} %refs_5_.1, ...), custom_call_target="tpu_custom_call" | custom-call | flops 15854469120 | bytes 16220160 | tf_op jit(solution)/shard_map/dft/pallas_call | solution.py:110
  56.5 19.5 %all-to-all-done.1.arrived = bf16[32,48,640]{2,1,0:T(8,128)(2,1)} async-done(((bf16[32,48,640]{2,1,0:T(8,128)(2,1)}), bf16[32,48,640]{2,1,0:T(8,128)(2,1)}, u32[]{:S(2)}, u32[]{:S(2)}) %all-to-all-start.1) | async-done | bytes 1966112 | tf_op jit(solution)/shard_map/all_to_all | solution.py:469
  76.0 4.0 all-to-all-start
  80.0 0.8 dynamic_slice.41
  81.1 0.7 broadcast_in_dim.133.rates
  81.9 0.7 pad_maximum_fusion.weights
  82.6 0.6 add_convert_fusion.mirror
  83.3 0.7 fusion.14
  84.0 0.9 compare_select_fusion.degree4
  84.8 29.0 %legendre.3 = (f32[4,2,24,2,768]{4,3,2,1,0:T(2,128)}, bf16[32,48,640]{2,1,0:T(8,128)(2,1)}) custom-call(bf16[32,48,640]{2,1,0:T(8,128)(2,1)} %all-to-all-done.1.arrived, bf16[24,1280,768]{2,1,0:T(8,128)(2,1)} %h3.5, bf16[24,1280,768]{2,1,0:T(8,128)(2,1)} %h3.5, bf16[24,1280,768]{2,1,0:T(8,128)(2,1)} %h3.5, bf16[24,1280,768]{2,1,0:T(8,128)(2,1)} %h3.5, ...), custom_call_target="tpu_custom_call" | custom-call | flops 1509949440 | bytes 47185920 | tf_op jit(solution)/shard_map/legendre/pallas_call | solution.py:417
  113.8 97.6 %all-to-all-done.arrived = bf16[32,48,1920]{2,1,0:T(8,128)(2,1)} async-done(((bf16[32,48,1920]{2,1,0:T(8,128)(2,1)}), bf16[32,48,1920]{2,1,0:T(8,128)(2,1)}, u32[]{:S(2)}, u32[]{:S(2)}) %all-to-all-start) | async-done | bytes 5898272 | tf_op jit(solution)/shard_map/all_to_all | solution.py:469
  211.4 5.6 %all-to-all-start.2 = ((bf16[32,48,640]{2,1,0:T(8,128)(2,1)}), bf16[32,48,640]{2,1,0:T(8,128)(2,1)}, u32[]{:S(2)}, u32[]{:S(2)}) async-start(bf16[32,48,640]{2,1,0:T(8,128)(2,1)} %get-tuple-element.33), calls=%async_computation.2 | async-start | bytes 3932160 | tf_op jit(solution)/shard_map/all_to_all | solution.py:469
  217.1 0.7 fusion.12
  217.8 1.3 dynamic-slice_bitcast_fusion.4
  219.1 0.2 collective-permute-start.6
  219.2 1.6 collective-permute-start.7
  220.9 1.4 collective-permute-start.8
  222.2 0.1 copy.36
  222.4 0.7 reshape.548.rates
  223.0 31.2 %legendre.5 = (f32[4,2,24,4,768]{4,3,2,1,0:T(4,128)}, bf16[32,48,1280]{2,1,0:T(8,128)(2,1)}) custom-call(bf16[32,48,1920]{2,1,0:T(8,128)(2,1)} %all-to-all-done.arrived, bf16[24,1280,768]{2,1,0:T(8,128)(2,1)} %h3.5, bf16[24,1280,768]{2,1,0:T(8,128)(2,1)} %h3.5, bf16[24,1280,768]{2,1,0:T(8,128)(2,1)} %h3.5, bf16[24,1280,768]{2,1,0:T(8,128)(2,1)} %h3.5, ...), custom_call_target="tpu_custom_call" | custom-call | flops 3019898880 | bytes 47185920 | tf_op jit(solution)/shard_map/legendre/pallas_call | solution.py:417
  254.3 8.7 %all-to-all-done.2.back = bf16[32,48,640]{2,1,0:T(8,128)(2,1)} async-done(((bf16[32,48,640]{2,1,0:T(8,128)(2,1)}), bf16[32,48,640]{2,1,0:T(8,128)(2,1)}, u32[]{:S(2)}, u32[]{:S(2)}) %all-to-all-start.2) | async-done | bytes 1966112 | tf_op jit(solution)/shard_map/all_to_all | solution.py:469
  263.0 4.0 all-to-all-start.4
  267.0 1.4 dynamic-slice_bitcast_fusion
  268.5 0.2 collective-permute-start
  268.8 0.7 broadcast_in_dim.134.rates
  269.5 1.6 collective-permute-start.1
  271.1 1.4 collective-permute-start.2
  272.5 29.0 %legendre.4 = (f32[4,2,24,2,768]{4,3,2,1,0:T(2,128)}, bf16[32,48,640]{2,1,0:T(8,128)(2,1)}) custom-call(bf16[32,48,1920]{2,1,0:T(8,128)(2,1)} %all-to-all-done.arrived, bf16[24,1280,768]{2,1,0:T(8,128)(2,1)} %h3.5, bf16[24,1280,768]{2,1,0:T(8,128)(2,1)} %h3.5, bf16[24,1280,768]{2,1,0:T(8,128)(2,1)} %h3.5, bf16[24,1280,768]{2,1,0:T(8,128)(2,1)} %h3.5, ...), custom_call_target="tpu_custom_call" | custom-call | flops 1509949440 | bytes 47185920 | tf_op jit(solution)/shard_map/legendre/pallas_call | solution.py:417
  301.5 2.4 dynamic-slice_bitcast_fusion.8
  303.9 0.4 collective-permute-start.4
  304.2 11.9 %collective-permute-done = f32[2,24,4,768]{3,2,1,0:T(4,128)} collective-permute-done((f32[2,24,4,768]{3,2,1,0:T(4,128)}, f32[2,24,4,768]{3,2,1,0:T(4,128)}, u32[]{:S(2)}, u32[]{:S(2)}) %collective-permute-start) | collective-permute-done | bytes 589856 | tf_op jit(solution)/shard_map/ppermute | solution.py:526
  316.1 12.8 %inverse_dft.3.refs_0_ = f32[8,320,2688]{2,1,0:T(8,128)} custom-call(s32[3]{0:T(128)} %broadcast_select_fusion.starts, bf16[32,48,640]{2,1,0:T(8,128)(2,1)} %all-to-all-done.2.back, bf16[1536,2688]{1,0:T(8,128)(2,1)} %get-tuple-element.31.refs_8_.angles, s32[1536,1]{1,0:T(8,128)} %broadcast_in_dim_reshape.4.refs_2_.refs_6_.wave_row, ...), custom_call_target="tpu_custom_call" | custom-call | flops 5284823040 | bytes 8847360 | tf_op jit(solution)/shard_map/inverse_dft/pallas_call | solution.py:173
  328.9 1.5 collective-permute-done.2
  330.4 7.3 %collective-permute-done.3 = f32[2,24,2,768]{3,2,1,0:T(2,128)} collective-permute-done((f32[2,24,2,768]{3,2,1,0:T(2,128)}, f32[2,24,2,768]{3,2,1,0:T(2,128)}, u32[]{:S(2)}, u32[]{:S(2)}) %collective-permute-start.3) | collective-permute-done | bytes 294944 | tf_op jit(solution)/shard_map/ppermute | solution.py:526
  337.7 1.9 collective-permute-done.4
  339.6 8.2 %collective-permute-done.5 = f32[2,24,2,768]{3,2,1,0:T(2,128)} collective-permute-done((f32[2,24,2,768]{3,2,1,0:T(2,128)}, f32[2,24,2,768]{3,2,1,0:T(2,128)}, u32[]{:S(2)}, u32[]{:S(2)}) %collective-permute-start.5) | collective-permute-done | bytes 294944 | tf_op jit(solution)/shard_map/ppermute | solution.py:526
  347.8 7.8 %all-to-all-done.4.back = bf16[32,48,1280]{2,1,0:T(8,128)(2,1)} async-done(((bf16[32,48,1280]{2,1,0:T(8,128)(2,1)}), bf16[32,48,1280]{2,1,0:T(8,128)(2,1)}, u32[]{:S(2)}, u32[]{:S(2)}) %all-to-all-start.4) | async-done | bytes 3932192 | tf_op jit(solution)/shard_map/all_to_all | solution.py:469
  355.6 5.3 %all-to-all-start.3 = ((bf16[32,48,640]{2,1,0:T(8,128)(2,1)}), bf16[32,48,640]{2,1,0:T(8,128)(2,1)}, u32[]{:S(2)}, u32[]{:S(2)}) async-start(bf16[32,48,640]{2,1,0:T(8,128)(2,1)} %get-tuple-element.39), calls=%async_computation.3 | async-start | bytes 3932160 | tf_op jit(solution)/shard_map/all_to_all | solution.py:469
  360.9 21.5 %inverse_dft.4.refs_0_ = f32[8,320,2688]{2,1,0:T(8,128)} custom-call(s32[3]{0:T(128)} %broadcast_select_fusion.starts, bf16[32,48,1280]{2,1,0:T(8,128)(2,1)} %all-to-all-done.4.back, bf16[1536,2688]{1,0:T(8,128)(2,1)} %get-tuple-element.31.refs_8_.angles, s32[1536,1]{1,0:T(8,128)} %broadcast_in_dim_reshape.4.refs_2_.refs_6_.wave_row, ...), custom_call_target="tpu_custom_call", output_to_operand_aliasing={{}: (5, {})} | custom-call | flops 10569646080 | bytes 17694720 | tf_op jit(solution)/shard_map/inverse_dft/pallas_call | solution.py:173
  382.5 2.6 broadcast_in_dim.60
  385.1 0.7 bitcast_dynamic-update-slice_fusion.11
  385.8 0.7 bitcast_dynamic-update-slice_fusion.10
  386.5 0.7 bitcast_dynamic-update-slice_fusion.9
  387.3 0.7 bitcast_dynamic-update-slice_fusion.8
  388.0 0.9 bitcast_dynamic-update-slice_fusion.3
  388.9 1.9 bitcast_dynamic-update-slice_fusion.2
  390.8 1.9 bitcast_dynamic-update-slice_fusion.1
  392.7 1.9 bitcast_dynamic-update-slice_fusion
  394.6 0.7 bitcast_dynamic-update-slice_fusion.7
  395.4 1.7 bitcast_dynamic-update-slice_fusion.6
  397.1 1.7 bitcast_dynamic-update-slice_fusion.5
  398.8 1.7 bitcast_dynamic-update-slice_fusion.4
  400.5 6.1 %all-to-all-done.3.back = bf16[32,48,640]{2,1,0:T(8,128)(2,1)} async-done(((bf16[32,48,640]{2,1,0:T(8,128)(2,1)}), bf16[32,48,640]{2,1,0:T(8,128)(2,1)}, u32[]{:S(2)}, u32[]{:S(2)}) %all-to-all-start.3) | async-done | bytes 1966112 | tf_op jit(solution)/shard_map/all_to_all | solution.py:469
  406.6 12.8 %inverse_dft.5 = f32[8,320,2688]{2,1,0:T(8,128)} custom-call(s32[3]{0:T(128)} %broadcast_select_fusion.starts, bf16[32,48,640]{2,1,0:T(8,128)(2,1)} %all-to-all-done.3.back, bf16[1536,2688]{1,0:T(8,128)(2,1)} %get-tuple-element.31.refs_8_.angles, s32[1536,1]{1,0:T(8,128)} %broadcast_in_dim_reshape.4.refs_2_.refs_6_.wave_row, ...), custom_call_target="tpu_custom_call", output_to_operand_aliasing={{}: (5, {})} | custom-call | flops 5284823040 | bytes 8847360 | tf_op jit(solution)/shard_map/inverse_dft/pallas_call | solution.py:173
  (47 shorter events, 0.8 us)
Async XLA Ops:
  22.6 53.3 %all-to-all-start.1 = ((bf16[32,48,640]{2,1,0:T(8,128)(2,1)}), bf16[32,48,640]{2,1,0:T(8,128)(2,1)}, u32[]{:S(2)}, u32[]{:S(2)}) async-start(bf16[32,48,640]{2,1,0:T(8,128)(2,1)} %get-tuple-element.32), calls=%async_computation.1 | async-start | bytes 3932160 | tf_op jit(solution)/shard_map/all_to_all | solution.py:469
  56.5 24.3 %copy-start.10 = (f32[32]{0:T(128)S(1)}, f32[32]{0:T(128)}, u32[]{:S(2)}) copy-start(f32[32]{0:T(128)} %param.13) | copy-start | bytes 388
  56.5 25.3 %copy-start.9 = (f32[1280]{0:T(1024)S(1)}, f32[1280]{0:T(1024)}, u32[]{:S(2)}) copy-start(f32[1280]{0:T(1024)} %param.12) | copy-start | bytes 15364
  76.0 135.5 %all-to-all-start = ((bf16[32,48,1920]{2,1,0:T(8,128)(2,1)}), bf16[32,48,1920]{2,1,0:T(8,128)(2,1)}, u32[]{:S(2)}, u32[]{:S(2)}) async-start(bf16[32,48,1920]{2,1,0:T(8,128)(2,1)} %dft.3), calls=%async_computation | async-start | bytes 11796480 | tf_op jit(solution)/shard_map/all_to_all | solution.py:469
  113.8 104.0 %copy-start.1 = (f32[4,2,24,2,768]{4,3,2,1,0:T(2,128)S(1)}, f32[4,2,24,2,768]{4,3,2,1,0:T(2,128)}, u32[]{:S(2)}) copy-start(f32[4,2,24,2,768]{4,3,2,1,0:T(2,128)} %get-tuple-element.41) | copy-start | bytes 3538948
  211.4 51.5 %all-to-all-start.2 = ((bf16[32,48,640]{2,1,0:T(8,128)(2,1)}), bf16[32,48,640]{2,1,0:T(8,128)(2,1)}, u32[]{:S(2)}, u32[]{:S(2)}) async-start(bf16[32,48,640]{2,1,0:T(8,128)(2,1)} %get-tuple-element.33), calls=%async_computation.2 | async-start | bytes 3932160 | tf_op jit(solution)/shard_map/all_to_all | solution.py:469
  219.1 35.1 %collective-permute-start.6 = (f32[2,24,2,768]{3,2,1,0:T(2,128)}, f32[2,24,2,768]{3,2,1,0:T(2,128)S(1)}, u32[]{:S(2)}, u32[]{:S(2)}) collective-permute-start(f32[2,24,2,768]{3,2,1,0:T(2,128)} %get-tuple-element.66), channel_id=1, source_target_pairs={{0,1},{1,2},{2,3},{3,0},{4,5},{5,6},{6,7},{7,4},{8,9},{9,10},{10,1... | collective-permute-start | bytes 884744 | tf_op jit(solution)/shard_map/ppermute | solution.py:526
  219.2 35.0 %collective-permute-start.7 = (f32[2,24,2,768]{3,2,1,0:T(2,128)}, f32[2,24,2,768]{3,2,1,0:T(2,128)S(1)}, u32[]{:S(2)}, u32[]{:S(2)}) collective-permute-start(f32[2,24,2,768]{3,2,1,0:T(2,128)} %get-tuple-element.65), channel_id=1, source_target_pairs={{0,2},{1,3},{2,0},{3,1},{4,6},{5,7},{6,4},{7,5},{8,10},{9,11},{10,... | collective-permute-start | bytes 884744 | tf_op jit(solution)/shard_map/ppermute | solution.py:526
  220.9 33.4 %collective-permute-start.8 = (f32[2,24,2,768]{3,2,1,0:T(2,128)}, f32[2,24,2,768]{3,2,1,0:T(2,128)S(1)}, u32[]{:S(2)}, u32[]{:S(2)}) collective-permute-start(f32[2,24,2,768]{3,2,1,0:T(2,128)} %get-tuple-element.64), channel_id=1, source_target_pairs={{0,3},{1,0},{2,1},{3,2},{4,7},{5,4},{6,5},{7,6},{8,11},{9,8},{10,9... | collective-permute-start | bytes 884744 | tf_op jit(solution)/shard_map/ppermute | solution.py:526
  254.2 12.8 %copy-start = (f32[4,2,24,4,768]{4,3,2,1,0:T(4,128)S(1)}, f32[4,2,24,4,768]{4,3,2,1,0:T(4,128)}, u32[]{:S(2)}) copy-start(f32[4,2,24,4,768]{4,3,2,1,0:T(4,128)} %get-tuple-element.36) | copy-start | bytes 7077892
  254.2 12.8 %copy-start.3 = (f32[2,24,2,768]{3,2,1,0:T(2,128)}, f32[2,24,2,768]{3,2,1,0:T(2,128)S(1)}, u32[]{:S(2)}) copy-start(f32[2,24,2,768]{3,2,1,0:T(2,128)S(1)} %collective-permute-done.6) | copy-start | bytes 884740
  254.2 12.8 %copy-start.5 = (f32[2,24,2,768]{3,2,1,0:T(2,128)}, f32[2,24,2,768]{3,2,1,0:T(2,128)S(1)}, u32[]{:S(2)}) copy-start(f32[2,24,2,768]{3,2,1,0:T(2,128)S(1)} %collective-permute-done.7) | copy-start | bytes 884740
  254.3 14.2 %copy-start.7 = (f32[2,24,2,768]{3,2,1,0:T(2,128)}, f32[2,24,2,768]{3,2,1,0:T(2,128)S(1)}, u32[]{:S(2)}) copy-start(f32[2,24,2,768]{3,2,1,0:T(2,128)S(1)} %collective-permute-done.8) | copy-start | bytes 884740
  263.0 92.7 %all-to-all-start.4 = ((bf16[32,48,1280]{2,1,0:T(8,128)(2,1)}), bf16[32,48,1280]{2,1,0:T(8,128)(2,1)}, u32[]{:S(2)}, u32[]{:S(2)}) async-start(bf16[32,48,1280]{2,1,0:T(8,128)(2,1)} %get-tuple-element.42), calls=%async_computation.4 | async-start | bytes 7864320 | tf_op jit(solution)/shard_map/all_to_all | solution.py:469
  268.5 47.7 %collective-permute-start = (f32[2,24,4,768]{3,2,1,0:T(4,128)}, f32[2,24,4,768]{3,2,1,0:T(4,128)}, u32[]{:S(2)}, u32[]{:S(2)}) collective-permute-start(f32[2,24,4,768]{3,2,1,0:T(4,128)} %get-tuple-element.62), channel_id=1, source_target_pairs={{0,1},{1,2},{2,3},{3,0},{4,5},{5,6},{6,7},{7,4},{8,9},{9,10},{10,1... | collective-permute-start | bytes 1769480 | tf_op jit(solution)/shard_map/ppermute | solution.py:526
  269.5 59.4 %collective-permute-start.1 = (f32[2,24,4,768]{3,2,1,0:T(4,128)}, f32[2,24,4,768]{3,2,1,0:T(4,128)}, u32[]{:S(2)}, u32[]{:S(2)}) collective-permute-start(f32[2,24,4,768]{3,2,1,0:T(4,128)} %get-tuple-element.61), channel_id=1, source_target_pairs={{0,2},{1,3},{2,0},{3,1},{4,6},{5,7},{6,4},{7,5},{8,10},{9,11},{10,... | collective-permute-start | bytes 1769480 | tf_op jit(solution)/shard_map/ppermute | solution.py:526
  271.1 59.3 %collective-permute-start.2 = (f32[2,24,4,768]{3,2,1,0:T(4,128)}, f32[2,24,4,768]{3,2,1,0:T(4,128)}, u32[]{:S(2)}, u32[]{:S(2)}) collective-permute-start(f32[2,24,4,768]{3,2,1,0:T(4,128)} %get-tuple-element.60), channel_id=1, source_target_pairs={{0,3},{1,0},{2,1},{3,2},{4,7},{5,4},{6,5},{7,6},{8,11},{9,8},{10,9... | collective-permute-start | bytes 1769480 | tf_op jit(solution)/shard_map/ppermute | solution.py:526
  303.9 33.8 %collective-permute-start.3 = (f32[2,24,2,768]{3,2,1,0:T(2,128)}, f32[2,24,2,768]{3,2,1,0:T(2,128)}, u32[]{:S(2)}, u32[]{:S(2)}) collective-permute-start(f32[2,24,2,768]{3,2,1,0:T(2,128)} %get-tuple-element.70), channel_id=1, source_target_pairs={{0,1},{1,2},{2,3},{3,0},{4,5},{5,6},{6,7},{7,4},{8,9},{9,10},{10,1... | collective-permute-start | bytes 884744 | tf_op jit(solution)/shard_map/ppermute | solution.py:526
  303.9 35.8 %collective-permute-start.4 = (f32[2,24,2,768]{3,2,1,0:T(2,128)}, f32[2,24,2,768]{3,2,1,0:T(2,128)}, u32[]{:S(2)}, u32[]{:S(2)}) collective-permute-start(f32[2,24,2,768]{3,2,1,0:T(2,128)} %get-tuple-element.69), channel_id=1, source_target_pairs={{0,2},{1,3},{2,0},{3,1},{4,6},{5,7},{6,4},{7,5},{8,10},{9,11},{10,... | collective-permute-start | bytes 884744 | tf_op jit(solution)/shard_map/ppermute | solution.py:526
  316.1 31.7 %collective-permute-start.5 = (f32[2,24,2,768]{3,2,1,0:T(2,128)}, f32[2,24,2,768]{3,2,1,0:T(2,128)}, u32[]{:S(2)}, u32[]{:S(2)}) collective-permute-start(f32[2,24,2,768]{3,2,1,0:T(2,128)} %get-tuple-element.68), channel_id=1, source_target_pairs={{0,3},{1,0},{2,1},{3,2},{4,7},{5,4},{6,5},{7,6},{8,11},{9,8},{10,9... | collective-permute-start | bytes 884744 | tf_op jit(solution)/shard_map/ppermute | solution.py:526
  355.6 51.0 %all-to-all-start.3 = ((bf16[32,48,640]{2,1,0:T(8,128)(2,1)}), bf16[32,48,640]{2,1,0:T(8,128)(2,1)}, u32[]{:S(2)}, u32[]{:S(2)}) async-start(bf16[32,48,640]{2,1,0:T(8,128)(2,1)} %get-tuple-element.39), calls=%async_computation.3 | async-start | bytes 3932160 | tf_op jit(solution)/shard_map/all_to_all | solution.py:469
  382.4 2.6 copy-start.2
  382.4 3.4 copy-start.4
  382.4 4.1 copy-start.6
  382.4 4.8 %copy-start.8 = (f32[2,24,2,768]{3,2,1,0:T(2,128)S(1)}, f32[2,24,2,768]{3,2,1,0:T(2,128)}, u32[]{:S(2)}) copy-start(f32[2,24,2,768]{3,2,1,0:T(2,128)} %copy-done.7) | copy-start | bytes 884740

commit v6 on v5

--- a/solution.py
+++ b/solution.py
@@ -101,7 +101,7 @@
     count = 2 * len(pairs)
     rows = wave_row.shape[0]
     wide = count * lats
-    per = dests // 4
+    per = dests // (2 if angles is None else 4)
     tile = rows * per // dests
     makes_angles = angles is None
     angle_spec = pl.BlockSpec((tile, lon), lambda i, s: (i, 0))

time: 420 us -> 420 us (level)
  no operation moved by 1% of the time
where the time goes in v6:
time: 420 us; the launch traced here: 419 us
  Pallas kernels  178 us (42%)
  waiting for transfers between devices  171 us (41%)
  starting transfers between devices  33.1 us (8%)
  local copies, waits for them, and re-layouts  31.2 us (7%)
  other arithmetic  5.04 us (1%)
    all_to_all x5, waiting for transfers between devices, exchange(): return lax.all_to_all(x, ('lat', 'fld'), 0, 0, tiled=True)  140 us
    pallas_call x3, Pallas kernels, legendre_step(): pl.pallas_call(functools.partial(legendre_kernel, lat_count, fld_count, l...  89.1 us
    pallas_call x3, Pallas kernels, inverse_dft(): pl.pallas_call(inverse_kernel, grid_spec=pltpu.PrefetchScalarGridSpec(num...  47.1 us
    pallas_call x2, Pallas kernels, dft(): pl.pallas_call(functools.partial(dft_kernel, count, makes_angles), grid_s...  42.1 us
    ppermute x9, waiting for transfers between devices, share_spectra(): block = lax.ppermute(block, 'fld', ring)  30.7 us
    all_to_all x5, starting transfers between devices, exchange(): return lax.all_to_all(x, ('lat', 'fld'), 0, 0, tiled=True)  26.4 us
    dynamic_update_slice x12, local copies, waits for them, and re-layouts, assemble(): lax.dynamic_update_slice(spectra, block[:, None], (0, at, 0, 2 * pairs[0]...  15.4 us
  transfers between devices with their start and end apart: 14, of which 10 were waited for; matrix products, arithmetic and copies ran while one was open for 7% of the time, Pallas kernels for 36%

profile of v6, /device:TPU:0, one launch (start us, length us, event | category | flops | bytes accessed | tf_op | source)
XLA Modules:
  0.0 419.1 jit_solution(15765369364229605660)
XLA Ops:
  0.6 0.7 slice.34
  1.3 0.8 fusion.22
  2.1 0.7 add_select_fusion.2
  2.9 0.6 broadcast_select_fusion.starts
  3.5 0.8 broadcast_in_dim.50
  4.3 1.1 broadcast_in_dim_reshape.4.refs_2_.refs_6_.wave_row
  5.5 0.6 broadcast_in_dim.51.refs_3_.modes
  6.1 16.3 %dft.2 = (bf16[32,48,640]{2,1,0:T(8,128)(2,1)}, bf16[1536,2688]{1,0:T(8,128)(2,1)}) custom-call(s32[3]{0:T(128)} %broadcast_select_fusion.starts, bf16[8,320,2688]{2,1,0:T(8,128)(2,1)} %refs_5_.1, bf16[8,320,2688]{2,1,0:T(8,128)(2,1)} %refs_5_.1, s32[1536,1]{1,0:T(8,128)} %broadcast_in_dim_reshape.4.refs_2_.refs_6_.wave_row, ...), custom_call_target="tpu_custom_call" | custom-call | flops 5284823040 | bytes 5406720 | tf_op jit(solution)/shard_map/dft/pallas_call | solution.py:110
  22.4 7.4 %all-to-all-start.1 = ((bf16[32,48,640]{2,1,0:T(8,128)(2,1)}), bf16[32,48,640]{2,1,0:T(8,128)(2,1)}, u32[]{:S(2)}, u32[]{:S(2)}) async-start(bf16[32,48,640]{2,1,0:T(8,128)(2,1)} %get-tuple-element.32), calls=%async_computation.1 | async-start | bytes 3932160 | tf_op jit(solution)/shard_map/all_to_all | solution.py:469
  29.8 0.6 copy.41
  30.4 25.8 %dft.3 = bf16[32,48,1920]{2,1,0:T(8,128)(2,1)} custom-call(s32[3]{0:T(128)} %broadcast_select_fusion.starts, bf16[8,320,2688]{2,1,0:T(8,128)(2,1)} %refs_5_.1, bf16[8,320,2688]{2,1,0:T(8,128)(2,1)} %refs_5_.1, bf16[8,320,2688]{2,1,0:T(8,128)(2,1)} %refs_5_.1, bf16[8,320,2688]{2,1,0:T(8,128)(2,1)} %refs_5_.1, bf16[8,320,2688]{2,1,0:T(8,128)(2,1)} %refs_5_.1, ...), custom_call_target="tpu_custom_call" | custom-call | flops 15854469120 | bytes 16220160 | tf_op jit(solution)/shard_map/dft/pallas_call | solution.py:110
  56.2 19.5 %all-to-all-done.1.arrived = bf16[32,48,640]{2,1,0:T(8,128)(2,1)} async-done(((bf16[32,48,640]{2,1,0:T(8,128)(2,1)}), bf16[32,48,640]{2,1,0:T(8,128)(2,1)}, u32[]{:S(2)}, u32[]{:S(2)}) %all-to-all-start.1) | async-done | bytes 1966112 | tf_op jit(solution)/shard_map/all_to_all | solution.py:469
  75.7 4.0 all-to-all-start
  79.7 0.8 dynamic_slice.41
  80.8 0.7 broadcast_in_dim.133.rates
  81.6 0.7 pad_maximum_fusion.weights
  82.4 0.6 add_convert_fusion.mirror
  83.0 0.7 fusion.14
  83.7 0.9 compare_select_fusion.degree4
  84.5 29.0 %legendre.3 = (f32[4,2,24,2,768]{4,3,2,1,0:T(2,128)}, bf16[32,48,640]{2,1,0:T(8,128)(2,1)}) custom-call(bf16[32,48,640]{2,1,0:T(8,128)(2,1)} %all-to-all-done.1.arrived, bf16[24,1280,768]{2,1,0:T(8,128)(2,1)} %h3.5, bf16[24,1280,768]{2,1,0:T(8,128)(2,1)} %h3.5, bf16[24,1280,768]{2,1,0:T(8,128)(2,1)} %h3.5, bf16[24,1280,768]{2,1,0:T(8,128)(2,1)} %h3.5, ...), custom_call_target="tpu_custom_call" | custom-call | flops 1509949440 | bytes 47185920 | tf_op jit(solution)/shard_map/legendre/pallas_call | solution.py:417
  113.5 97.7 %all-to-all-done.arrived = bf16[32,48,1920]{2,1,0:T(8,128)(2,1)} async-done(((bf16[32,48,1920]{2,1,0:T(8,128)(2,1)}), bf16[32,48,1920]{2,1,0:T(8,128)(2,1)}, u32[]{:S(2)}, u32[]{:S(2)}) %all-to-all-start) | async-done | bytes 5898272 | tf_op jit(solution)/shard_map/all_to_all | solution.py:469
  211.2 5.6 %all-to-all-start.2 = ((bf16[32,48,640]{2,1,0:T(8,128)(2,1)}), bf16[32,48,640]{2,1,0:T(8,128)(2,1)}, u32[]{:S(2)}, u32[]{:S(2)}) async-start(bf16[32,48,640]{2,1,0:T(8,128)(2,1)} %get-tuple-element.33), calls=%async_computation.2 | async-start | bytes 3932160 | tf_op jit(solution)/shard_map/all_to_all | solution.py:469
  216.8 0.7 fusion.12
  217.5 1.3 dynamic-slice_bitcast_fusion.4
  218.8 0.2 collective-permute-start.6
  219.0 1.6 collective-permute-start.7
  220.6 1.4 collective-permute-start.8
  222.0 0.1 copy.36
  222.1 0.7 reshape.548.rates
  222.8 31.2 %legendre.5 = (f32[4,2,24,4,768]{4,3,2,1,0:T(4,128)}, bf16[32,48,1280]{2,1,0:T(8,128)(2,1)}) custom-call(bf16[32,48,1920]{2,1,0:T(8,128)(2,1)} %all-to-all-done.arrived, bf16[24,1280,768]{2,1,0:T(8,128)(2,1)} %h3.5, bf16[24,1280,768]{2,1,0:T(8,128)(2,1)} %h3.5, bf16[24,1280,768]{2,1,0:T(8,128)(2,1)} %h3.5, bf16[24,1280,768]{2,1,0:T(8,128)(2,1)} %h3.5, ...), custom_call_target="tpu_custom_call" | custom-call | flops 3019898880 | bytes 47185920 | tf_op jit(solution)/shard_map/legendre/pallas_call | solution.py:417
  254.0 8.7 %all-to-all-done.2.back = bf16[32,48,640]{2,1,0:T(8,128)(2,1)} async-done(((bf16[32,48,640]{2,1,0:T(8,128)(2,1)}), bf16[32,48,640]{2,1,0:T(8,128)(2,1)}, u32[]{:S(2)}, u32[]{:S(2)}) %all-to-all-start.2) | async-done | bytes 1966112 | tf_op jit(solution)/shard_map/all_to_all | solution.py:469
  262.7 4.0 all-to-all-start.4
  266.8 1.4 dynamic-slice_bitcast_fusion
  268.2 0.2 collective-permute-start
  268.5 0.7 broadcast_in_dim.134.rates
  269.2 1.6 collective-permute-start.1
  270.8 1.4 collective-permute-start.2
  272.2 29.0 %legendre.4 = (f32[4,2,24,2,768]{4,3,2,1,0:T(2,128)}, bf16[32,48,640]{2,1,0:T(8,128)(2,1)}) custom-call(bf16[32,48,1920]{2,1,0:T(8,128)(2,1)} %all-to-all-done.arrived, bf16[24,1280,768]{2,1,0:T(8,128)(2,1)} %h3.5, bf16[24,1280,768]{2,1,0:T(8,128)(2,1)} %h3.5, bf16[24,1280,768]{2,1,0:T(8,128)(2,1)} %h3.5, bf16[24,1280,768]{2,1,0:T(8,128)(2,1)} %h3.5, ...), custom_call_target="tpu_custom_call" | custom-call | flops 1509949440 | bytes 47185920 | tf_op jit(solution)/shard_map/legendre/pallas_call | solution.py:417
  301.2 2.4 dynamic-slice_bitcast_fusion.8
  303.6 0.4 collective-permute-start.4
  304.0 11.9 %collective-permute-done = f32[2,24,4,768]{3,2,1,0:T(4,128)} collective-permute-done((f32[2,24,4,768]{3,2,1,0:T(4,128)}, f32[2,24,4,768]{3,2,1,0:T(4,128)}, u32[]{:S(2)}, u32[]{:S(2)}) %collective-permute-start) | collective-permute-done | bytes 589856 | tf_op jit(solution)/shard_map/ppermute | solution.py:526
  315.8 12.8 %inverse_dft.3.refs_0_ = f32[8,320,2688]{2,1,0:T(8,128)} custom-call(s32[3]{0:T(128)} %broadcast_select_fusion.starts, bf16[32,48,640]{2,1,0:T(8,128)(2,1)} %all-to-all-done.2.back, bf16[1536,2688]{1,0:T(8,128)(2,1)} %get-tuple-element.31.refs_8_.angles, s32[1536,1]{1,0:T(8,128)} %broadcast_in_dim_reshape.4.refs_2_.refs_6_.wave_row, ...), custom_call_target="tpu_custom_call" | custom-call | flops 5284823040 | bytes 8847360 | tf_op jit(solution)/shard_map/inverse_dft/pallas_call | solution.py:173
  328.6 1.5 collective-permute-done.2
  330.1 7.3 %collective-permute-done.3 = f32[2,24,2,768]{3,2,1,0:T(2,128)} collective-permute-done((f32[2,24,2,768]{3,2,1,0:T(2,128)}, f32[2,24,2,768]{3,2,1,0:T(2,128)}, u32[]{:S(2)}, u32[]{:S(2)}) %collective-permute-start.3) | collective-permute-done | bytes 294944 | tf_op jit(solution)/shard_map/ppermute | solution.py:526
  337.4 1.9 collective-permute-done.4
  339.3 8.2 %collective-permute-done.5 = f32[2,24,2,768]{3,2,1,0:T(2,128)} collective-permute-done((f32[2,24,2,768]{3,2,1,0:T(2,128)}, f32[2,24,2,768]{3,2,1,0:T(2,128)}, u32[]{:S(2)}, u32[]{:S(2)}) %collective-permute-start.5) | collective-permute-done | bytes 294944 | tf_op jit(solution)/shard_map/ppermute | solution.py:526
  347.5 7.8 %all-to-all-done.4.back = bf16[32,48,1280]{2,1,0:T(8,128)(2,1)} async-done(((bf16[32,48,1280]{2,1,0:T(8,128)(2,1)}), bf16[32,48,1280]{2,1,0:T(8,128)(2,1)}, u32[]{:S(2)}, u32[]{:S(2)}) %all-to-all-start.4) | async-done | bytes 3932192 | tf_op jit(solution)/shard_map/all_to_all | solution.py:469
  355.4 5.3 %all-to-all-start.3 = ((bf16[32,48,640]{2,1,0:T(8,128)(2,1)}), bf16[32,48,640]{2,1,0:T(8,128)(2,1)}, u32[]{:S(2)}, u32[]{:S(2)}) async-start(bf16[32,48,640]{2,1,0:T(8,128)(2,1)} %get-tuple-element.39), calls=%async_computation.3 | async-start | bytes 3932160 | tf_op jit(solution)/shard_map/all_to_all | solution.py:469
  360.6 21.5 %inverse_dft.4.refs_0_ = f32[8,320,2688]{2,1,0:T(8,128)} custom-call(s32[3]{0:T(128)} %broadcast_select_fusion.starts, bf16[32,48,1280]{2,1,0:T(8,128)(2,1)} %all-to-all-done.4.back, bf16[1536,2688]{1,0:T(8,128)(2,1)} %get-tuple-element.31.refs_8_.angles, s32[1536,1]{1,0:T(8,128)} %broadcast_in_dim_reshape.4.refs_2_.refs_6_.wave_row, ...), custom_call_target="tpu_custom_call", output_to_operand_aliasing={{}: (5, {})} | custom-call | flops 10569646080 | bytes 17694720 | tf_op jit(solution)/shard_map/inverse_dft/pallas_call | solution.py:173
  382.2 2.6 broadcast_in_dim.60
  384.8 0.7 bitcast_dynamic-update-slice_fusion.11
  385.5 0.7 bitcast_dynamic-update-slice_fusion.10
  386.3 0.7 bitcast_dynamic-update-slice_fusion.9
  387.0 0.7 bitcast_dynamic-update-slice_fusion.8
  387.7 0.9 bitcast_dynamic-update-slice_fusion.3
  388.6 1.9 bitcast_dynamic-update-slice_fusion.2
  390.5 1.9 bitcast_dynamic-update-slice_fusion.1
  392.4 1.9 bitcast_dynamic-update-slice_fusion
  394.3 0.7 bitcast_dynamic-update-slice_fusion.7
  395.1 1.7 bitcast_dynamic-update-slice_fusion.6
  396.8 1.7 bitcast_dynamic-update-slice_fusion.5
  398.5 1.7 bitcast_dynamic-update-slice_fusion.4
  400.2 6.1 %all-to-all-done.3.back = bf16[32,48,640]{2,1,0:T(8,128)(2,1)} async-done(((bf16[32,48,640]{2,1,0:T(8,128)(2,1)}), bf16[32,48,640]{2,1,0:T(8,128)(2,1)}, u32[]{:S(2)}, u32[]{:S(2)}) %all-to-all-start.3) | async-done | bytes 1966112 | tf_op jit(solution)/shard_map/all_to_all | solution.py:469
  406.3 12.8 %inverse_dft.5 = f32[8,320,2688]{2,1,0:T(8,128)} custom-call(s32[3]{0:T(128)} %broadcast_select_fusion.starts, bf16[32,48,640]{2,1,0:T(8,128)(2,1)} %all-to-all-done.3.back, bf16[1536,2688]{1,0:T(8,128)(2,1)} %get-tuple-element.31.refs_8_.angles, s32[1536,1]{1,0:T(8,128)} %broadcast_in_dim_reshape.4.refs_2_.refs_6_.wave_row, ...), custom_call_target="tpu_custom_call", output_to_operand_aliasing={{}: (5, {})} | custom-call | flops 5284823040 | bytes 8847360 | tf_op jit(solution)/shard_map/inverse_dft/pallas_call | solution.py:173
  (47 shorter events, 0.8 us)
Async XLA Ops:
  22.4 53.3 %all-to-all-start.1 = ((bf16[32,48,640]{2,1,0:T(8,128)(2,1)}), bf16[32,48,640]{2,1,0:T(8,128)(2,1)}, u32[]{:S(2)}, u32[]{:S(2)}) async-start(bf16[32,48,640]{2,1,0:T(8,128)(2,1)} %get-tuple-element.32), calls=%async_computation.1 | async-start | bytes 3932160 | tf_op jit(solution)/shard_map/all_to_all | solution.py:469
  56.2 24.3 %copy-start.10 = (f32[32]{0:T(128)S(1)}, f32[32]{0:T(128)}, u32[]{:S(2)}) copy-start(f32[32]{0:T(128)} %param.13) | copy-start | bytes 388
  56.2 25.3 %copy-start.9 = (f32[1280]{0:T(1024)S(1)}, f32[1280]{0:T(1024)}, u32[]{:S(2)}) copy-start(f32[1280]{0:T(1024)} %param.12) | copy-start | bytes 15364
  75.7 135.5 %all-to-all-start = ((bf16[32,48,1920]{2,1,0:T(8,128)(2,1)}), bf16[32,48,1920]{2,1,0:T(8,128)(2,1)}, u32[]{:S(2)}, u32[]{:S(2)}) async-start(bf16[32,48,1920]{2,1,0:T(8,128)(2,1)} %dft.3), calls=%async_computation | async-start | bytes 11796480 | tf_op jit(solution)/shard_map/all_to_all | solution.py:469
  113.5 104.0 %copy-start.1 = (f32[4,2,24,2,768]{4,3,2,1,0:T(2,128)S(1)}, f32[4,2,24,2,768]{4,3,2,1,0:T(2,128)}, u32[]{:S(2)}) copy-start(f32[4,2,24,2,768]{4,3,2,1,0:T(2,128)} %get-tuple-element.41) | copy-start | bytes 3538948
  211.2 51.5 %all-to-all-start.2 = ((bf16[32,48,640]{2,1,0:T(8,128)(2,1)}), bf16[32,48,640]{2,1,0:T(8,128)(2,1)}, u32[]{:S(2)}, u32[]{:S(2)}) async-start(bf16[32,48,640]{2,1,0:T(8,128)(2,1)} %get-tuple-element.33), calls=%async_computation.2 | async-start | bytes 3932160 | tf_op jit(solution)/shard_map/all_to_all | solution.py:469
  218.8 35.1 %collective-permute-start.6 = (f32[2,24,2,768]{3,2,1,0:T(2,128)}, f32[2,24,2,768]{3,2,1,0:T(2,128)S(1)}, u32[]{:S(2)}, u32[]{:S(2)}) collective-permute-start(f32[2,24,2,768]{3,2,1,0:T(2,128)} %get-tuple-element.66), channel_id=1, source_target_pairs={{0,1},{1,2},{2,3},{3,0},{4,5},{5,6},{6,7},{7,4},{8,9},{9,10},{10,1... | collective-permute-start | bytes 884744 | tf_op jit(solution)/shard_map/ppermute | solution.py:526
  219.0 35.0 %collective-permute-start.7 = (f32[2,24,2,768]{3,2,1,0:T(2,128)}, f32[2,24,2,768]{3,2,1,0:T(2,128)S(1)}, u32[]{:S(2)}, u32[]{:S(2)}) collective-permute-start(f32[2,24,2,768]{3,2,1,0:T(2,128)} %get-tuple-element.65), channel_id=1, source_target_pairs={{0,2},{1,3},{2,0},{3,1},{4,6},{5,7},{6,4},{7,5},{8,10},{9,11},{10,... | collective-permute-start | bytes 884744 | tf_op jit(solution)/shard_map/ppermute | solution.py:526
  220.6 33.4 %collective-permute-start.8 = (f32[2,24,2,768]{3,2,1,0:T(2,128)}, f32[2,24,2,768]{3,2,1,0:T(2,128)S(1)}, u32[]{:S(2)}, u32[]{:S(2)}) collective-permute-start(f32[2,24,2,768]{3,2,1,0:T(2,128)} %get-tuple-element.64), channel_id=1, source_target_pairs={{0,3},{1,0},{2,1},{3,2},{4,7},{5,4},{6,5},{7,6},{8,11},{9,8},{10,9... | collective-permute-start | bytes 884744 | tf_op jit(solution)/shard_map/ppermute | solution.py:526
  253.9 12.8 %copy-start = (f32[4,2,24,4,768]{4,3,2,1,0:T(4,128)S(1)}, f32[4,2,24,4,768]{4,3,2,1,0:T(4,128)}, u32[]{:S(2)}) copy-start(f32[4,2,24,4,768]{4,3,2,1,0:T(4,128)} %get-tuple-element.36) | copy-start | bytes 7077892
  253.9 12.8 %copy-start.3 = (f32[2,24,2,768]{3,2,1,0:T(2,128)}, f32[2,24,2,768]{3,2,1,0:T(2,128)S(1)}, u32[]{:S(2)}) copy-start(f32[2,24,2,768]{3,2,1,0:T(2,128)S(1)} %collective-permute-done.6) | copy-start | bytes 884740
  253.9 12.8 %copy-start.5 = (f32[2,24,2,768]{3,2,1,0:T(2,128)}, f32[2,24,2,768]{3,2,1,0:T(2,128)S(1)}, u32[]{:S(2)}) copy-start(f32[2,24,2,768]{3,2,1,0:T(2,128)S(1)} %collective-permute-done.7) | copy-start | bytes 884740
  254.0 14.2 %copy-start.7 = (f32[2,24,2,768]{3,2,1,0:T(2,128)}, f32[2,24,2,768]{3,2,1,0:T(2,128)S(1)}, u32[]{:S(2)}) copy-start(f32[2,24,2,768]{3,2,1,0:T(2,128)S(1)} %collective-permute-done.8) | copy-start | bytes 884740
  262.7 92.7 %all-to-all-start.4 = ((bf16[32,48,1280]{2,1,0:T(8,128)(2,1)}), bf16[32,48,1280]{2,1,0:T(8,128)(2,1)}, u32[]{:S(2)}, u32[]{:S(2)}) async-start(bf16[32,48,1280]{2,1,0:T(8,128)(2,1)} %get-tuple-element.42), calls=%async_computation.4 | async-start | bytes 7864320 | tf_op jit(solution)/shard_map/all_to_all | solution.py:469
  268.2 47.7 %collective-permute-start = (f32[2,24,4,768]{3,2,1,0:T(4,128)}, f32[2,24,4,768]{3,2,1,0:T(4,128)}, u32[]{:S(2)}, u32[]{:S(2)}) collective-permute-start(f32[2,24,4,768]{3,2,1,0:T(4,128)} %get-tuple-element.62), channel_id=1, source_target_pairs={{0,1},{1,2},{2,3},{3,0},{4,5},{5,6},{6,7},{7,4},{8,9},{9,10},{10,1... | collective-permute-start | bytes 1769480 | tf_op jit(solution)/shard_map/ppermute | solution.py:526
  269.2 59.4 %collective-permute-start.1 = (f32[2,24,4,768]{3,2,1,0:T(4,128)}, f32[2,24,4,768]{3,2,1,0:T(4,128)}, u32[]{:S(2)}, u32[]{:S(2)}) collective-permute-start(f32[2,24,4,768]{3,2,1,0:T(4,128)} %get-tuple-element.61), channel_id=1, source_target_pairs={{0,2},{1,3},{2,0},{3,1},{4,6},{5,7},{6,4},{7,5},{8,10},{9,11},{10,... | collective-permute-start | bytes 1769480 | tf_op jit(solution)/shard_map/ppermute | solution.py:526
  270.8 59.3 %collective-permute-start.2 = (f32[2,24,4,768]{3,2,1,0:T(4,128)}, f32[2,24,4,768]{3,2,1,0:T(4,128)}, u32[]{:S(2)}, u32[]{:S(2)}) collective-permute-start(f32[2,24,4,768]{3,2,1,0:T(4,128)} %get-tuple-element.60), channel_id=1, source_target_pairs={{0,3},{1,0},{2,1},{3,2},{4,7},{5,4},{6,5},{7,6},{8,11},{9,8},{10,9... | collective-permute-start | bytes 1769480 | tf_op jit(solution)/shard_map/ppermute | solution.py:526
  303.6 33.8 %collective-permute-start.3 = (f32[2,24,2,768]{3,2,1,0:T(2,128)}, f32[2,24,2,768]{3,2,1,0:T(2,128)}, u32[]{:S(2)}, u32[]{:S(2)}) collective-permute-start(f32[2,24,2,768]{3,2,1,0:T(2,128)} %get-tuple-element.70), channel_id=1, source_target_pairs={{0,1},{1,2},{2,3},{3,0},{4,5},{5,6},{6,7},{7,4},{8,9},{9,10},{10,1... | collective-permute-start | bytes 884744 | tf_op jit(solution)/shard_map/ppermute | solution.py:526
  303.6 35.8 %collective-permute-start.4 = (f32[2,24,2,768]{3,2,1,0:T(2,128)}, f32[2,24,2,768]{3,2,1,0:T(2,128)}, u32[]{:S(2)}, u32[]{:S(2)}) collective-permute-start(f32[2,24,2,768]{3,2,1,0:T(2,128)} %get-tuple-element.69), channel_id=1, source_target_pairs={{0,2},{1,3},{2,0},{3,1},{4,6},{5,7},{6,4},{7,5},{8,10},{9,11},{10,... | collective-permute-start | bytes 884744 | tf_op jit(solution)/shard_map/ppermute | solution.py:526
  315.8 31.7 %collective-permute-start.5 = (f32[2,24,2,768]{3,2,1,0:T(2,128)}, f32[2,24,2,768]{3,2,1,0:T(2,128)}, u32[]{:S(2)}, u32[]{:S(2)}) collective-permute-start(f32[2,24,2,768]{3,2,1,0:T(2,128)} %get-tuple-element.68), channel_id=1, source_target_pairs={{0,3},{1,0},{2,1},{3,2},{4,7},{5,4},{6,5},{7,6},{8,11},{9,8},{10,9... | collective-permute-start | bytes 884744 | tf_op jit(solution)/shard_map/ppermute | solution.py:526
  355.4 51.0 %all-to-all-start.3 = ((bf16[32,48,640]{2,1,0:T(8,128)(2,1)}), bf16[32,48,640]{2,1,0:T(8,128)(2,1)}, u32[]{:S(2)}, u32[]{:S(2)}) async-start(bf16[32,48,640]{2,1,0:T(8,128)(2,1)} %get-tuple-element.39), calls=%async_computation.3 | async-start | bytes 3932160 | tf_op jit(solution)/shard_map/all_to_all | solution.py:469
  382.2 2.6 copy-start.2
  382.2 3.4 copy-start.4
  382.2 4.1 copy-start.6
  382.2 4.8 %copy-start.8 = (f32[2,24,2,768]{3,2,1,0:T(2,128)S(1)}, f32[2,24,2,768]{3,2,1,0:T(2,128)}, u32[]{:S(2)}) copy-start(f32[2,24,2,768]{3,2,1,0:T(2,128)} %copy-done.7) | copy-start | bytes 884740
